TPU v7x, 128 devices: a whole 4x4x4 slice. The times are simulated.
128 devices in a mesh: tm: 8 (over x, y_hi), tile: 16 (over z, y_lo, core).
Axes of the slice: x: 4, y: 4 (y_hi: 2, y_lo: 2; y = y_hi * 2 + y_lo), z: 4, core: 2. Of those that a mesh axis runs over, the one named last changes fastest.
Arguments:
- first_input: bfloat16 [16, 32, 64, 384], P('tm', None, 'tile'), may hold values from -6 to 6
- second_input: bfloat16 [16, 32, 64, 384], P('tm', None, 'tile'), may hold values from -6 to 6
- output_grad: bfloat16 [16, 32, 64, 384], P('tm', None, 'tile'), may hold values from -6 to 6
- first_gain: float32 [384], replicated, may hold values from 0.1 to 1.9
- first_shift: float32 [384], replicated, may hold values from -1 to 1
- first_kernel: bfloat16 [27, 384, 384], replicated, may hold values from -1 to 1
- second_gain: float32 [384], replicated, may hold values from 0.1 to 1.9
- second_shift: float32 [384], replicated, may hold values from -1 to 1
- second_kernel: bfloat16 [27, 384, 384], replicated, may hold values from -1 to 1
- latent_kernel: bfloat16 [27, 16, 384], replicated, may hold values from -0.0625 to 0.0625
Outputs:
- latent_grad: float32 [64, 8192], P(None, ('tm', 'tile'))
All inputs are finite; a program needn't handle non-finite values.
Results may differ from a plain program's by a relative error of at most 0.0044.
Values may be sent and summed in bfloat16 or wider, within the bound.
No kernel may reach another device: no remote copies, remote signals or barrier semaphores. Data moves between devices by JAX's collectives and lax.ppermute only.
A program may use at most 64 MiB of HBM per device.

v0:
```python
import functools

import jax
import jax.numpy as jnp
import numpy as np
from jax import lax
from jax.experimental import pallas as pl
from jax.experimental.pallas import tpu as pltpu
from jax.experimental.layout import Layout, with_layout_constraint
from jax.sharding import Mesh
from jax.sharding import PartitionSpec as P

GROUPS = 32
TILE = ("tile_0", "tile_1", "tile_2")
TM_TILE = ("tm",) + TILE
EPSILON = 1e-05
MIB = 1 << 20


def vmem(count):
    return [pl.BlockSpec(memory_space=pltpu.VMEM)] * count


WEIGHTS_COVER = pl.CostEstimate(flops=1 << 33, bytes_accessed=1 << 23, transcendentals=0)
HBM = [pl.BlockSpec(memory_space=pltpu.HBM)]


def matmul_cost(count, kernel):
    return pl.CostEstimate(
        flops=2 * count * kernel.size, bytes_accessed=2 * kernel.size, transcendentals=0
    )


def in_hbm(value):
    return pltpu.with_memory_space_constraint(value, pltpu.HBM)


def nt_dot(left, right, **kw):
    return lax.dot_general(
        left, right, (((1,), (1,)), ((), ())), preferred_element_type=jnp.float32, **kw
    )


def thirds(value):
    high = value.astype(jnp.bfloat16)
    rest = value - high.astype(jnp.float32)
    middle = rest.astype(jnp.bfloat16)
    return high, middle, (rest - middle.astype(jnp.float32)).astype(jnp.bfloat16)


def group_sum(rows):
    count, channels = rows.shape
    per = channels // GROUPS
    row = lax.broadcasted_iota(jnp.int32, (channels, channels), 0) // per
    col = lax.broadcasted_iota(jnp.int32, (channels, channels), 1) // per
    same = jnp.where(row == col, 1.0, 0.0).astype(jnp.bfloat16)
    if count < 8:
        rows = jnp.concatenate([rows, jnp.zeros((8 - count, channels), jnp.float32)], axis=0)
    split = jnp.concatenate([part.astype(jnp.float32) for part in thirds(rows)], axis=0)
    sums = jnp.dot(split.astype(jnp.bfloat16), same, preferred_element_type=jnp.float32)
    return sums[0:count] + sums[8 : 8 + count] + sums[16 : 16 + count]


def spread(ref, rows):
    ref[...] = jnp.broadcast_to(rows[None], ref.shape)


def moments_kernel(second_hbm, first_hbm, out_ref, second_ref, first_ref, sems):
    pairs = ((second_hbm, second_ref), (first_hbm, first_ref))
    copies = [pltpu.make_async_copy(*pair, sems.at[k]) for k, pair in enumerate(pairs)]
    for copy in copies:
        copy.start()
    rows = []
    for copy, (_, ref) in zip(copies, pairs):
        copy.wait()
        frames = ref.shape[0]
        values = [ref[f].astype(jnp.float32) for f in range(frames)]
        rows += [jnp.sum(v, axis=(0, 1)).reshape(1, -1) for v in values]
        rows += [jnp.sum(v * v, axis=(0, 1)).reshape(1, -1) for v in values]
    spread(out_ref, jnp.concatenate(rows, axis=0))


def moments(second, first, peers):
    frames, _, _, channels = second.shape
    return pl.pallas_call(
        moments_kernel,
        out_shape=jax.ShapeDtypeStruct((peers, 4 * frames, channels), jnp.float32),
        in_specs=[pl.BlockSpec(memory_space=pltpu.HBM)] * 2,
        out_specs=pl.BlockSpec(memory_space=pltpu.VMEM),
        scratch_shapes=[
            pltpu.VMEM(second.shape, jnp.bfloat16),
            pltpu.VMEM(first.shape, jnp.bfloat16),
            pltpu.SemaphoreType.DMA((2,)),
        ],
        compiler_params=pltpu.CompilerParams(vmem_limit_bytes=16 * MIB),
        name="moments",
    )(in_hbm(second), in_hbm(first))


def fill(ext, at, block, a, b, even):
    frames, cols = block.shape[:2]
    ext[at : at + frames, 1 : cols + 1] = block
    ext[at : at + frames, 0] = jnp.where(even, b, a)
    ext[at : at + frames, cols + 1] = jnp.where(even, a, b)


def time_taps(ext, w_ref, taps, frames, cols):
    _, channels = ext.shape[2:]
    pairs = [(a, c) for a in taps for c in range(3)]
    left = jnp.concatenate(
        [
            ext[2 - a : 2 - a + frames, 2 - c : 2 - c + cols].reshape(-1, channels)
            for a, c in pairs
        ],
        axis=1,
    )
    right = jnp.concatenate(
        [
            jnp.concatenate([w_ref[9 * a + 3 * b + c] for a, c in pairs], axis=1)
            for b in range(3)
        ],
        axis=0,
    )
    return nt_dot(left, right)


def row_taps(wide, rows):
    count, channels = wide.shape[0], wide.shape[1] // 3
    row = lax.broadcasted_iota(jnp.int32, (count, 1), 0) % rows
    up = jnp.where(row < rows - 1, pltpu.roll(wide[:, :channels], count - 1, 0), 0.0)
    down = jnp.where(row > 0, pltpu.roll(wide[:, 2 * channels :], 1, 0), 0.0)
    return wide[:, channels : 2 * channels] + up + down


def window(par_ref, own_ref, next_ref, ra_ref, rb_ref, ran_ref, rbn_ref, ext):
    frames = own_ref.shape[0]
    even, side, later = par_ref[0] == 0, par_ref[1] == 1, par_ref[2] == 1
    zero = jnp.bfloat16(0)
    own = lambda v: jnp.where(side, v, zero)
    nxt = lambda v: jnp.where(later, v, zero)
    fill(ext, 0, own_ref[...], ra_ref[...], own(rb_ref[...]), even)
    fill(ext, frames, nxt(next_ref[...]), nxt(ran_ref[...]), nxt(own(rbn_ref[...])), even)


def conv_kernel(
    par_ref,
    own_ref,
    next_ref,
    ra_ref,
    rb_ref,
    ran_ref,
    rbn_ref,
    w_hbm,
    u_ref,
    ext,
    acc,
    w_ref,
    sems,
):
    frames, cols, rows, _ = own_ref.shape
    copies = {
        a: pltpu.make_async_copy(
            w_hbm.at[pl.ds(9 * a, 9)], w_ref.at[pl.ds(9 * a, 9)], sems.at[a]
        )
        for a in (2, 1, 0)
    }
    for copy in copies.values():
        copy.start()
    window(par_ref, own_ref, next_ref, ra_ref, rb_ref, ran_ref, rbn_ref, ext)
    for a, copy in copies.items():
        copy.wait()
        part = time_taps(ext, w_ref, (a,), frames, cols)
        acc[...] = part if a == 2 else acc[...] + part
    u_ref[...] = row_taps(acc, rows)


def conv_section(par, grad, halo, kernel):
    frames, cols, rows, channels = grad.shape
    count = frames * cols * rows
    return pl.pallas_call(
        conv_kernel,
        out_shape=jax.ShapeDtypeStruct((count, channels), jnp.float32),
        in_specs=[pl.BlockSpec(memory_space=pltpu.SMEM)] + vmem(6) + HBM,
        out_specs=vmem(1)[0],
        scratch_shapes=[
            pltpu.VMEM((2 * frames, cols + 2, rows, channels), jnp.bfloat16),
            pltpu.VMEM((count, 3 * channels), jnp.float32),
            pltpu.VMEM(kernel.shape, jnp.bfloat16),
            pltpu.SemaphoreType.DMA((3,)),
        ],
        compiler_params=pltpu.CompilerParams(vmem_limit_bytes=16 * MIB),
        cost_estimate=matmul_cost(count, kernel),
        name="conv",
    )(par, grad, *halo, in_hbm(kernel))


def norm_stats(cells, base, frames, mom_ref):
    totals = group_sum(jnp.sum(mom_ref[...], axis=0)) * (1.0 / cells)
    means, scales = [], []
    for f in range(frames):
        mean = totals[base + f : base + f + 1]
        var = totals[base + frames + f : base + frames + f + 1] - mean * mean
        means.append(mean)
        scales.append(lax.rsqrt(var + EPSILON))
    return means, scales


def through(upstream, normed, gain, shift):
    pre = normed * gain + shift
    sig = jax.nn.sigmoid(pre)
    return upstream * sig * (1.0 + pre * (1.0 - sig)) * gain


def finish(cells, base, upstream, x_ref, mom_ref, affine_ref, at, q_ref, sums_ref, stats_ref):
    frames, cols, rows, channels = x_ref.shape
    means, scales = norm_stats(cells, base, frames, mom_ref)
    gain, shift = affine_ref[at : at + 1], affine_ref[at + 1 : at + 2]
    half = cols * rows
    sums, crosses = [], []
    for f in range(frames):
        normed = (x_ref[f].astype(jnp.float32).reshape(half, channels) - means[f]) * scales[f]
        q = through(upstream[f * half : (f + 1) * half], normed, gain, shift)
        q_ref[f] = q.reshape(cols, rows, channels)
        sums.append(jnp.sum(q, axis=0, keepdims=True))
        crosses.append(jnp.sum(q * normed, axis=0, keepdims=True))
    spread(sums_ref, jnp.concatenate(sums + crosses, axis=0))
    stats_ref[...] = jnp.concatenate(means + scales, axis=0)


def finish_shapes(stored, peers):
    frames, _, _, channels = stored.shape
    return (
        jax.ShapeDtypeStruct(stored.shape, jnp.float32),
        jax.ShapeDtypeStruct((peers, 2 * frames, channels), jnp.float32),
        jax.ShapeDtypeStruct((2 * frames, channels), jnp.float32),
    )


def norm_kernel(cells, u_ref, x_ref, mom_ref, affine_ref, q_ref, sums_ref, stats_ref):
    finish(cells, 0, u_ref, x_ref, mom_ref, affine_ref, 0, q_ref, sums_ref, stats_ref)


def norm_section(upstream, stored, mom, affine, cells, peers):
    return pl.pallas_call(
        functools.partial(norm_kernel, cells),
        out_shape=finish_shapes(stored, peers),
        in_specs=vmem(4),
        out_specs=tuple(vmem(3)),
        compiler_params=pltpu.CompilerParams(vmem_limit_bytes=16 * MIB),
        name="norm",
    )(upstream, stored, mom, affine)


def block_grad(cells, grad_ref, q_ref, x_ref, stats_ref, sums_ref):
    frames, cols, rows, channels = grad_ref.shape
    totals = group_sum(jnp.sum(sums_ref[...], axis=0)) * (1.0 / cells)
    result = []
    for f in range(frames):
        mean = stats_ref[f : f + 1]
        scale = stats_ref[frames + f : frames + f + 1]
        flat = (cols * rows, channels)
        normed = (x_ref[f].astype(jnp.float32).reshape(flat) - mean) * scale
        value = grad_ref[f].astype(jnp.float32).reshape(flat) + scale * (
            q_ref[f].reshape(flat)
            - totals[f : f + 1]
            - normed * totals[frames + f : frames + f + 1]
        )
        result.append(value.astype(jnp.bfloat16))
    return result


def dx_kernel(cells, par_ref, grad_ref, q_ref, x_ref, stats_ref, sums_ref, dx_ref, sa_ref, sb_ref):
    _, cols, rows, channels = grad_ref.shape
    even = par_ref[0] == 0
    for f, value in enumerate(block_grad(cells, grad_ref, q_ref, x_ref, stats_ref, sums_ref)):
        value = value.reshape(cols, rows, channels)
        dx_ref[f] = value
        sa_ref[f] = jnp.where(even, value[cols - 1], value[0])
        sb_ref[f] = jnp.where(even, value[0], value[cols - 1])


def dx_section(par, grad, q, stored, stats, sums, cells):
    frames, _, rows, channels = grad.shape
    edge = jax.ShapeDtypeStruct((frames, rows, channels), jnp.bfloat16)
    return pl.pallas_call(
        functools.partial(dx_kernel, cells),
        out_shape=(jax.ShapeDtypeStruct(grad.shape, jnp.bfloat16), edge, edge),
        in_specs=[pl.BlockSpec(memory_space=pltpu.SMEM)] + vmem(5),
        out_specs=tuple(vmem(3)),
        compiler_params=pltpu.CompilerParams(vmem_limit_bytes=16 * MIB),
        cost_estimate=WEIGHTS_COVER,
        name="dx",
    )(par, grad, q, stored, stats, sums)


def conv_norm_kernel(
    cells,
    base,
    par_ref,
    own_ref,
    next_ref,
    ra_ref,
    rb_ref,
    ran_ref,
    rbn_ref,
    w_ref,
    x_ref,
    mom_ref,
    affine_ref,
    q_ref,
    sums_ref,
    stats_ref,
    ext,
    acc,
):
    rows = own_ref.shape[2]
    window(par_ref, own_ref, next_ref, ra_ref, rb_ref, ran_ref, rbn_ref, ext)
    acc[...] = time_taps(ext, w_ref, (2, 1, 0), *own_ref.shape[:2])
    upstream = row_taps(acc, rows)
    finish(cells, base, upstream, x_ref, mom_ref, affine_ref, 2, q_ref, sums_ref, stats_ref)


def conv_norm_section(par, grad, halo, kernel, stored, mom, affine, cells, base, peers):
    frames, cols, rows, channels = grad.shape
    count = frames * cols * rows
    return pl.pallas_call(
        functools.partial(conv_norm_kernel, cells, base),
        out_shape=finish_shapes(stored, peers),
        in_specs=[pl.BlockSpec(memory_space=pltpu.SMEM)] + vmem(10),
        out_specs=tuple(vmem(3)),
        scratch_shapes=[
            pltpu.VMEM((2 * frames, cols + 2, rows, channels), jnp.bfloat16),
            pltpu.VMEM((count, 3 * channels), jnp.float32),
        ],
        compiler_params=pltpu.CompilerParams(vmem_limit_bytes=16 * MIB),
        cost_estimate=matmul_cost(count, kernel),
        name="convnorm",
    )(par, grad, *halo, kernel, stored, mom, affine)


def edge_kernel(par_ref, block_ref, sa_ref, sb_ref):
    cols = block_ref.shape[1]
    even = par_ref[0] == 0
    first, last = block_ref[:, 0], block_ref[:, cols - 1]
    sa_ref[...] = jnp.where(even, last, first)
    sb_ref[...] = jnp.where(even, first, last)


def edge_section(par, block):
    frames, _, rows, channels = block.shape
    edge = jax.ShapeDtypeStruct((frames, rows, channels), block.dtype)
    return pl.pallas_call(
        edge_kernel,
        out_shape=(edge, edge),
        in_specs=[pl.BlockSpec(memory_space=pltpu.SMEM)] + vmem(1),
        out_specs=tuple(vmem(2)),
        compiler_params=pltpu.CompilerParams(vmem_limit_bytes=4 * MIB),
        name="edge",
    )(par, block)


def latent_kernel_body(cells, grad_ref, q_ref, x_ref, stats_ref, sums_ref, k_ref, own_ref, prev_ref, wide):
    frames, cols, rows, channels = grad_ref.shape
    lat = k_ref.shape[1]
    lanes = wide.shape[1]
    values = block_grad(cells, grad_ref, q_ref, x_ref, stats_ref, sums_ref)
    grad = jnp.concatenate(values, axis=0)
    count = frames * cols * rows
    wide[...] = jnp.zeros_like(wide)
    for k in range(9):
        wide[k, 0 : 3 * lat] = k_ref[3 * k : 3 * k + 3].reshape(3 * lat, channels)
    row = lax.broadcasted_iota(jnp.int32, (count, 1), 0) % rows
    placed = {}
    for a in range(3):
        z = [nt_dot(grad, wide[3 * a + b]) for b in range(3)]
        up = jnp.where(row < rows - 1, pltpu.roll(z[0], count - 1, 0), 0.0)
        down = jnp.where(row > 0, pltpu.roll(z[2], 1, 0), 0.0)
        total = (z[1] + up + down).reshape(frames, cols, rows, lanes)
        for f in range(frames):
            out = total[f, 0]
            for w in range(1, cols):
                out = out + pltpu.roll(total[f, w], lat * w, 1)
            at = f + a - 2
            placed[at] = placed[at] + out if at in placed else out
    for f in range(frames):
        own_ref[f] = placed[f]
        prev_ref[f] = placed[f - 2]


def latent_section(grad, q, stored, stats, sums, kernel, cells):
    frames, _, rows, channels = grad.shape
    lanes = 128
    out = jax.ShapeDtypeStruct((frames, rows, lanes), jnp.float32)
    return pl.pallas_call(
        functools.partial(latent_kernel_body, cells),
        out_shape=(out, out),
        in_specs=vmem(6),
        out_specs=tuple(vmem(2)),
        scratch_shapes=[pltpu.VMEM((9, lanes, channels), jnp.bfloat16)],
        compiler_params=pltpu.CompilerParams(vmem_limit_bytes=16 * MIB),
        name="latent",
    )(grad, q, stored, stats, sums, kernel)


def assemble_kernel(lat, cols, got_ref, e_ref, perm_ref, out_ref):
    parts = {}
    for p in range(2):
        rows = jnp.concatenate([got_ref[:, p, :], got_ref[:, 2 + p, :]], axis=0)
        spots = lax.dot_general(
            jnp.concatenate(thirds(rows), axis=0),
            e_ref[...],
            (((0,), (0,)), ((), ())),
            preferred_element_type=jnp.float32,
        )
        for col in range(cols + 2):
            q = (col + 1) % 2
            piece = spots[lat * col : lat * (col + 1), 128 * col : 128 * (col + 1)]
            parts[p, q] = parts[p, q] + piece if (p, q) in parts else piece
    stacked = jnp.concatenate([parts[p, q] for p in range(2) for q in range(2)], axis=0)
    final = jnp.dot(
        perm_ref[...],
        jnp.concatenate(thirds(stacked), axis=0),
        preferred_element_type=jnp.float32,
    )
    out_ref[...] = final[:, : out_ref.shape[1]]


def assemble(got, lat, cols):
    peers, quad, _ = got.shape
    width = peers * cols // 2
    tokens = quad // 2 * width
    place = np.zeros((quad // 2, peers, (cols + 2) * 128), np.float32)
    for hh in range(quad // 2):
        for s in range(peers):
            for col in range(cols + 2):
                x = s * cols + col - 1
                if 0 <= x < peers * cols:
                    place[hh, s, 128 * col + hh * width + x // 2] = 1.0
    place = np.tile(place.reshape(-1, place.shape[-1]), (3, 1))
    perm = np.zeros((4 * lat, 4 * lat), np.float32)
    for pq in range(4):
        for one in range(lat):
            perm[one * 4 + pq, pq * lat + one] = 1.0
    perm = np.tile(perm, (1, 3))
    return pl.pallas_call(
        functools.partial(assemble_kernel, lat, cols),
        out_shape=jax.ShapeDtypeStruct((4 * lat, tokens), jnp.float32),
        in_specs=vmem(3),
        out_specs=pl.BlockSpec(memory_space=pltpu.VMEM),
        compiler_params=pltpu.CompilerParams(vmem_limit_bytes=16 * MIB),
        name="assemble",
    )(got, jnp.asarray(place, jnp.bfloat16), jnp.asarray(perm, jnp.bfloat16))


def exchange(par, value, send_a, send_b):
    tms = lax.axis_size("tm")
    tiles = lax.axis_size(TILE)
    back = ring(tms)
    swap = [(0, 1), (1, 0)]
    hops = []
    for k in range(1, tiles, 2):
        hops += [(k, (k + 1) % tiles), ((k + 1) % tiles, k)]
    diagonal = [(t * tiles + s, u * tiles + d) for t, u in back for s, d in hops]
    nxt = lax.ppermute(value, "tm", back)
    rb = lax.ppermute(send_b, TILE, hops)
    rbn = lax.ppermute(send_b, TM_TILE, diagonal)
    ra = lax.ppermute(send_a, "tile_2", swap)
    corner = edge_section(par, nxt)[0]
    ran = lax.ppermute(corner, "tile_2", swap)
    return nxt, ra, rb, ran, rbn


def ring(count):
    return [(t, (t - 1) % count) for t in range(count)]


def everyone(rows):
    return lax.all_to_all(rows, TILE, 0, 0)


def shards(
    first_input,
    second_input,
    output_grad,
    first_gain,
    first_shift,
    first_kernel,
    second_gain,
    second_shift,
    second_kernel,
    latent_kernel,
):
    frames, rows, cols, channels = first_input.shape
    peers = lax.axis_size(TILE)
    cells = rows * cols * peers * (channels // GROUPS)
    core = lax.axis_index("tile_2")
    even = core == 0
    tile, when = lax.axis_index(TILE), lax.axis_index("tm")
    later = when < lax.axis_size("tm") - 1
    side = jnp.where(even, tile > 0, tile < peers - 1)
    par = jnp.stack([core.astype(jnp.int32), side.astype(jnp.int32), later.astype(jnp.int32)])
    affine = jnp.stack([second_gain, second_shift, first_gain, first_shift])
    par, later, affine, output_grad, second_input, first_input = lax.optimization_barrier(
        (par, later, affine, output_grad, second_input, first_input)
    )
    turn = lambda x: with_layout_constraint(
        jnp.transpose(x, (0, 2, 1, 3)), Layout(major_to_minor=(0, 1, 2, 3))
    )

    grad = turn(output_grad)
    mine = moments(second_input, first_input, peers)
    mom = everyone(mine)
    halo = exchange(par, grad, *edge_section(par, grad))
    second, first = turn(second_input), turn(first_input)
    upstream = conv_section(par, grad, halo, second_kernel)
    q, sums, stats = norm_section(upstream, second, mom, affine, cells, peers)
    grad, send_a, send_b = dx_section(par, grad, q, second, stats, everyone(sums), cells)
    nxt, ra, rb, ran, rbn = exchange(par, grad, send_a, send_b)
    q, sums, stats = conv_norm_section(
        par, grad, (nxt, ra, rb, ran, rbn), first_kernel, first, mom, affine, cells,
        2 * frames, peers,
    )
    own, prev = latent_section(grad, q, first, stats, everyone(sums), latent_kernel, cells)
    tms = lax.axis_size("tm")
    own = own + jnp.where(later, lax.ppermute(prev, "tm", ring(tms)), 0.0)
    got = everyone(own.reshape(peers, frames * rows // peers, own.shape[-1]))
    return assemble(got, latent_kernel.shape[1], cols)


def solution(mesh):
    torus = Mesh(
        mesh.devices.reshape(mesh.shape["tm"], 4, 2, 2), ("tm", "tile_0", "tile_1", "tile_2")
    )
    block = P("tm", None, TILE, None)
    placed = (block, block, block) + (P(),) * 7
    return jax.shard_map(
        shards, mesh=torus, in_specs=placed, out_specs=P(None, TM_TILE), check_vma=False
    )
```

profile of v0, /device:TPU:1, one launch (start us, length us, event | category | flops | bytes accessed | tf_op | source)
XLA Modules:
  0.0 89.4 jit_solution(10272961575101016217)
XLA Ops:
  0.0 0.7 stack.39
  2.8 1.0 %copy.21 = bf16[2,32,4,384]{3,1,2,0:T(8,128)(2,1)S(1)} copy(bf16[2,32,4,384]{3,2,1,0:T(4,128)(2,1)} %param.14) | data formatting | bytes 393216 | tf_op jit(solution)/shard_map/optimization_barrier | solution.py:503
  3.8 6.0 %collective-permute-start = (bf16[2,4,32,384]{3,2,1,0:T(8,128)(2,1)S(1)}, bf16[2,4,32,384]{3,2,1,0:T(8,128)(2,1)S(1)}, u32[]{:S(2)}, u32[]{:S(2)}) collective-permute-start(bf16[2,4,32,384]{3,2,1,0:T(8,128)(2,1)S(1)} %bitcast.15), channel_id=1, source_target_pairs={{0,112},{16,0},{32,16},{48,32},{64,48},{80,64},{96,80},{112,96},{1... | collective-permute-start | bytes 589832 | tf_op jit(solution)/shard_map/ppermute | solution.py:464
  10.3 1.3 %collective-permute-start.2 = (bf16[2,32,384]{2,1,0:T(8,128)(2,1)S(1)}, bf16[2,32,384]{2,1,0:T(8,128)(2,1)S(1)}, u32[]{:S(2)}, u32[]{:S(2)}) collective-permute-start(bf16[2,32,384]{2,1,0:T(8,128)(2,1)S(1)} %get-tuple-element.29), channel_id=1, source_target_pairs={{1,2},{2,1},{3,4},{4,3},{5,6},{6,5},{7,8},{8,7},{9,10},{10,9},{11,... | collective-permute-start | bytes 147464 | tf_op jit(solution)/shard_map/ppermute | solution.py:465
  12.1 3.0 %collective-permute-start.1 = (bf16[2,32,384]{2,1,0:T(8,128)(2,1)S(1)}, bf16[2,32,384]{2,1,0:T(8,128)(2,1)S(1)}, u32[]{:S(2)}, u32[]{:S(2)}) collective-permute-start(bf16[2,32,384]{2,1,0:T(8,128)(2,1)S(1)} %get-tuple-element.28), channel_id=1, source_target_pairs={{0,1},{1,0},{2,3},{3,2},{4,5},{5,4},{6,7},{7,6},{8,9},{9,8},{10,11... | collective-permute-start | bytes 147464 | tf_op jit(solution)/shard_map/ppermute | solution.py:467
  15.1 1.2 %edge.4 = (bf16[2,32,384]{2,1,0:T(8,128)(2,1)S(1)}, bf16[2,32,384]{2,1,0:T(8,128)(2,1)}) custom-call(s32[3]{0:T(128)S(1)} %pad_add_fusion.par_ref, bf16[2,4,32,384]{3,2,1,0:T(8,128)(2,1)S(1)} %collective-permute-done.block_ref.next_ref), custom_call_target="tpu_custom_call" | custom-call | tf_op jit(solution)/shard_map/edge/pallas_call | solution.py:352
  16.6 2.0 %moments.1 = f32[16,8,384]{2,1,0:T(8,128)} custom-call(bf16[2,32,4,384]{3,2,1,0:T(4,128)(2,1)} %second_hbm, bf16[2,32,4,384]{3,2,1,0:T(4,128)(2,1)} %first_hbm), custom_call_target="tpu_custom_call" | custom-call | tf_op jit(solution)/shard_map/moments/pallas_call | solution.py:85
  18.6 5.5 %all-to-all-start = ((f32[16,8,384]{2,1,0:T(8,128)}), f32[16,8,384]{2,1,0:T(8,128)S(1)}, u32[]{:S(2)}, u32[]{:S(2)}) async-start(f32[16,8,384]{2,1,0:T(8,128)} %moments.1), calls=%async_computation | async-start | bytes 393216 | tf_op jit(solution)/shard_map/all_to_all | solution.py:478
  24.1 0.9 %copy.20 = bf16[2,32,4,384]{3,1,2,0:T(8,128)(2,1)S(1)} copy(bf16[2,32,4,384]{3,2,1,0:T(4,128)(2,1)} %second_hbm) | data formatting | bytes 393216 | tf_op jit(solution)/shard_map/optimization_barrier | solution.py:503
  25.1 5.7 %conv.1.u_ref = f32[256,384]{1,0:T(8,128)S(1)} custom-call(s32[3]{0:T(128)S(1)} %pad_add_fusion.par_ref, bf16[2,4,32,384]{3,2,1,0:T(8,128)(2,1)S(1)} %bitcast.17, bf16[2,4,32,384]{3,2,1,0:T(8,128)(2,1)S(1)} %collective-permute-done.block_ref.next_ref, bf16[2,32,384]{2,1,0:T(8,128)(2,1)S(1)} %collective-permute-done.1.ra_ref, ...), custom_call_target="tpu_custom_call" | custom-call | flops 2038431744 | bytes 7962624 | tf_op jit(solution)/shard_map/conv/pallas_call | solution.py:180
  31.3 11.6 %all_to_all.20.sums_ref = f32[16,4,384]{2,1,0:T(4,128)S(1)} all-to-all(f32[16,4,384]{2,1,0:T(4,128)S(1)} %get-tuple-element.36), channel_id=1, replica_groups=mesh['tm'=8,'tile_0'=4,'tile_1'=2,'tile_2'=2] {'tile_0','tile_1','tile_2'}, dimensions={0} | all-to-all | bytes 196608 | tf_op jit(solution)/shard_map/all_to_all | solution.py:478
  42.9 0.9 dx.1
  43.8 6.7 %collective-permute-start.5 = (bf16[2,4,32,384]{3,2,1,0:T(8,128)(2,1)S(1)}, bf16[2,4,32,384]{3,2,1,0:T(8,128)(2,1)S(1)}, u32[]{:S(2)}, u32[]{:S(2)}) collective-permute-start(bf16[2,4,32,384]{3,2,1,0:T(8,128)(2,1)S(1)} %get-tuple-element.37.own_ref.grad_ref), channel_id=1, source_target_pairs={{0,112},{16,0},{32,16},{48,32},{64,48},{80,64},{96,80},{112,96},{1... | collective-permute-start | bytes 589832 | tf_op jit(solution)/shard_map/ppermute | solution.py:464
  51.1 2.7 %collective-permute-start.6 = (bf16[2,32,384]{2,1,0:T(8,128)(2,1)S(1)}, bf16[2,32,384]{2,1,0:T(8,128)(2,1)S(1)}, u32[]{:S(2)}, u32[]{:S(2)}) collective-permute-start(bf16[2,32,384]{2,1,0:T(8,128)(2,1)S(1)} %get-tuple-element.38), channel_id=1, source_target_pairs={{0,1},{1,0},{2,3},{3,2},{4,5},{5,4},{6,7},{7,6},{8,9},{9,8},{10,11... | collective-permute-start | bytes 147464 | tf_op jit(solution)/shard_map/ppermute | solution.py:467
  54.2 1.2 %edge.5 = (bf16[2,32,384]{2,1,0:T(8,128)(2,1)S(1)}, bf16[2,32,384]{2,1,0:T(8,128)(2,1)}) custom-call(s32[3]{0:T(128)S(1)} %pad_add_fusion.par_ref, bf16[2,4,32,384]{3,2,1,0:T(8,128)(2,1)S(1)} %collective-permute-done.5.block_ref.next_ref), custom_call_target="tpu_custom_call" | custom-call | tf_op jit(solution)/shard_map/edge/pallas_call | solution.py:352
  55.3 1.9 %collective-permute-start.8 = (bf16[2,32,384]{2,1,0:T(8,128)(2,1)S(1)}, bf16[2,32,384]{2,1,0:T(8,128)(2,1)S(1)}, u32[]{:S(2)}, u32[]{:S(2)}) collective-permute-start(bf16[2,32,384]{2,1,0:T(8,128)(2,1)S(1)} %get-tuple-element.40), channel_id=1, source_target_pairs={{0,1},{1,0},{2,3},{3,2},{4,5},{5,4},{6,7},{7,6},{8,9},{9,8},{10,11... | collective-permute-start | bytes 147464 | tf_op jit(solution)/shard_map/ppermute | solution.py:469
  57.3 0.8 collective-permute-done.8.ran_ref
  58.2 3.4 %convnorm.1 = (f32[2,4,32,384]{3,2,1,0:T(8,128)S(1)}, f32[16,4,384]{2,1,0:T(4,128)S(1)}, f32[4,384]{1,0:T(4,128)S(1)}) custom-call(s32[3]{0:T(128)S(1)} %pad_add_fusion.par_ref, bf16[2,4,32,384]{3,2,1,0:T(8,128)(2,1)S(1)} %get-tuple-element.37.own_ref.grad_ref, bf16[2,4,32,384]{3,2,1,0:T(8,128)(2,1)S(1)} %collective-permute-done.5.block_ref.next_ref, ...), custom_call_target="tpu_custom_call" | custom-call | flops 2038431744 | bytes 7962624 | tf_op jit(solution)/shard_map/convnorm/pallas_call | solution.py:326
  61.6 9.6 %all_to_all.21.sums_ref = f32[16,4,384]{2,1,0:T(4,128)S(1)} all-to-all(f32[16,4,384]{2,1,0:T(4,128)S(1)} %get-tuple-element.43), channel_id=1, replica_groups=mesh['tm'=8,'tile_0'=4,'tile_1'=2,'tile_2'=2] {'tile_0','tile_1','tile_2'}, dimensions={0} | all-to-all | bytes 196608 | tf_op jit(solution)/shard_map/all_to_all | solution.py:478
  71.2 1.0 %latent.1 = (f32[2,32,128]{2,1,0:T(8,128)S(1)}, f32[2,32,128]{2,1,0:T(8,128)S(1)}) custom-call(bf16[2,4,32,384]{3,2,1,0:T(8,128)(2,1)S(1)} %get-tuple-element.37.own_ref.grad_ref, f32[2,4,32,384]{3,2,1,0:T(8,128)S(1)} %get-tuple-element.41.q_ref, bf16[2,4,32,384]{3,2,1,0:T(8,128)(2,1)S(1)} %bitcast.20, f32[4,384]{1,0:T(4,128)S(1)} %get-tuple-element.42.stats_ref, ...), custom_call_target="tpu_custom_call" | custom-call | tf_op jit(solution)/shard_map/latent/pallas_call | solution.py:394
  72.1 5.5 %collective-permute-start.10 = (f32[2,32,128]{2,1,0:T(8,128)S(1)}, f32[2,32,128]{2,1,0:T(8,128)S(1)}, u32[]{:S(2)}, u32[]{:S(2)}) collective-permute-start(f32[2,32,128]{2,1,0:T(8,128)S(1)} %get-tuple-element.46), channel_id=1, source_target_pairs={{0,112},{16,0},{32,16},{48,32},{64,48},{80,64},{96,80},{112,96},{1... | collective-permute-start | bytes 98312 | tf_op jit(solution)/shard_map/ppermute | solution.py:525
  77.6 1.0 %collective-permute-done.10 = f32[2,32,128]{2,1,0:T(8,128)S(1)} collective-permute-done((f32[2,32,128]{2,1,0:T(8,128)S(1)}, f32[2,32,128]{2,1,0:T(8,128)S(1)}, u32[]{:S(2)}, u32[]{:S(2)}) %collective-permute-start.10) | collective-permute-done | bytes 32800 | tf_op jit(solution)/shard_map/ppermute | solution.py:525
  78.6 9.7 %all_to_all.22.got_ref = f32[16,4,128]{2,1,0:T(4,128)S(1)} all-to-all(f32[16,4,128]{2,1,0:T(4,128)S(1)} %bitcast.23), channel_id=1, replica_groups=mesh['tm'=8,'tile_0'=4,'tile_1'=2,'tile_2'=2] {'tile_0','tile_1','tile_2'}, dimensions={0} | all-to-all | bytes 65536 | tf_op jit(solution)/shard_map/all_to_all | solution.py:478
  88.3 1.1 %assemble.1 = f32[64,64]{1,0:T(8,128)} custom-call(f32[16,4,128]{2,1,0:T(4,128)S(1)} %all_to_all.22.got_ref, bf16[96,768]{1,0:T(8,128)(2,1)S(1)} %copy-done.1, bf16[64,192]{1,0:T(8,128)(2,1)S(1)} %copy-done.2), custom_call_target="tpu_custom_call" | custom-call | tf_op jit(solution)/shard_map/assemble/pallas_call | solution.py:445
  (36 shorter events, 5.0 us)
Async XLA Ops:
  3.8 11.4 %collective-permute-start = (bf16[2,4,32,384]{3,2,1,0:T(8,128)(2,1)S(1)}, bf16[2,4,32,384]{3,2,1,0:T(8,128)(2,1)S(1)}, u32[]{:S(2)}, u32[]{:S(2)}) collective-permute-start(bf16[2,4,32,384]{3,2,1,0:T(8,128)(2,1)S(1)} %bitcast.15), channel_id=1, source_target_pairs={{0,112},{16,0},{32,16},{48,32},{64,48},{80,64},{96,80},{112,96},{1... | collective-permute-start | bytes 589832 | tf_op jit(solution)/shard_map/ppermute | solution.py:464
  10.3 14.7 %collective-permute-start.2 = (bf16[2,32,384]{2,1,0:T(8,128)(2,1)S(1)}, bf16[2,32,384]{2,1,0:T(8,128)(2,1)S(1)}, u32[]{:S(2)}, u32[]{:S(2)}) collective-permute-start(bf16[2,32,384]{2,1,0:T(8,128)(2,1)S(1)} %get-tuple-element.29), channel_id=1, source_target_pairs={{1,2},{2,1},{3,4},{4,3},{5,6},{6,5},{7,8},{8,7},{9,10},{10,9},{11,... | collective-permute-start | bytes 147464 | tf_op jit(solution)/shard_map/ppermute | solution.py:465
  11.7 13.4 %collective-permute-start.4 = (bf16[2,32,384]{2,1,0:T(8,128)(2,1)S(1)}, bf16[2,32,384]{2,1,0:T(8,128)(2,1)S(1)}, u32[]{:S(2)}, u32[]{:S(2)}) collective-permute-start(bf16[2,32,384]{2,1,0:T(8,128)(2,1)S(1)} %get-tuple-element.29), channel_id=1, source_target_pairs={{1,114},{2,113},{3,116},{4,115},{5,118},{6,117},{7,120},{8,119},{9... | collective-permute-start | bytes 147464 | tf_op jit(solution)/shard_map/ppermute | solution.py:466
  12.1 12.9 %collective-permute-start.1 = (bf16[2,32,384]{2,1,0:T(8,128)(2,1)S(1)}, bf16[2,32,384]{2,1,0:T(8,128)(2,1)S(1)}, u32[]{:S(2)}, u32[]{:S(2)}) collective-permute-start(bf16[2,32,384]{2,1,0:T(8,128)(2,1)S(1)} %get-tuple-element.28), channel_id=1, source_target_pairs={{0,1},{1,0},{2,3},{3,2},{4,5},{5,4},{6,7},{7,6},{8,9},{9,8},{10,11... | collective-permute-start | bytes 147464 | tf_op jit(solution)/shard_map/ppermute | solution.py:467
  16.3 8.7 %collective-permute-start.3 = (bf16[2,32,384]{2,1,0:T(8,128)(2,1)S(1)}, bf16[2,32,384]{2,1,0:T(8,128)(2,1)S(1)}, u32[]{:S(2)}, u32[]{:S(2)}) collective-permute-start(bf16[2,32,384]{2,1,0:T(8,128)(2,1)S(1)} %get-tuple-element.30), channel_id=1, source_target_pairs={{0,1},{1,0},{2,3},{3,2},{4,5},{5,4},{6,7},{7,6},{8,9},{9,8},{10,11... | collective-permute-start | bytes 147464 | tf_op jit(solution)/shard_map/ppermute | solution.py:469
  18.6 12.2 %all-to-all-start = ((f32[16,8,384]{2,1,0:T(8,128)}), f32[16,8,384]{2,1,0:T(8,128)S(1)}, u32[]{:S(2)}, u32[]{:S(2)}) async-start(f32[16,8,384]{2,1,0:T(8,128)} %moments.1), calls=%async_computation | async-start | bytes 393216 | tf_op jit(solution)/shard_map/all_to_all | solution.py:478
  30.8 27.3 %slice-start = ((s8[7962624]{0:T(1024)(128)(4,1)}), s8[4194304]{0:T(1024)(128)(4,1)S(1)}, s32[]{:S(2)}) async-start(s8[7962624]{0:T(1024)(128)(4,1)} %bitcast.13), calls=%async_computation.4 | async-start | bytes 8388608
  42.9 14.4 %copy-start.3 = (bf16[2,32,4,384]{3,2,1,0:T(4,128)(2,1)S(1)}, bf16[2,32,4,384]{3,2,1,0:T(4,128)(2,1)}, u32[]{:S(2)}) copy-start(bf16[2,32,4,384]{3,2,1,0:T(4,128)(2,1)} %first_hbm) | copy-start | bytes 589828
  42.9 15.3 %slice-start.1 = ((s8[7962624]{0:T(1024)(128)(4,1)}), s8[3768320]{0:T(1024)(128)(4,1)S(1)}, s32[]{:S(2)}) async-start(s8[7962624]{0:T(1024)(128)(4,1)} %bitcast.13), calls=%async_computation.5 | async-start | bytes 7536640
  43.8 27.4 %copy-start = (bf16[27,16,384]{2,1,0:T(8,128)(2,1)S(1)}, bf16[27,16,384]{2,1,0:T(8,128)(2,1)}, u32[]{:S(2)}) copy-start(bf16[27,16,384]{2,1,0:T(8,128)(2,1)} %k_ref.1) | copy-start | bytes 995332
  43.8 44.5 %copy-start.1 = (bf16[96,768]{1,0:T(8,128)(2,1)S(1)}, bf16[96,768]{1,0:T(8,128)(2,1)}, u32[]{:S(2)}) copy-start(bf16[96,768]{1,0:T(8,128)(2,1)} %constant.33.clone.e_ref) | copy-start | bytes 442372
  43.8 44.5 %copy-start.2 = (bf16[64,192]{1,0:T(8,128)(2,1)S(1)}, bf16[64,192]{1,0:T(8,128)(2,1)}, u32[]{:S(2)}) copy-start(bf16[64,192]{1,0:T(8,128)(2,1)} %constant.34.clone.perm_ref) | copy-start | bytes 73732
  43.8 10.4 %collective-permute-start.5 = (bf16[2,4,32,384]{3,2,1,0:T(8,128)(2,1)S(1)}, bf16[2,4,32,384]{3,2,1,0:T(8,128)(2,1)S(1)}, u32[]{:S(2)}, u32[]{:S(2)}) collective-permute-start(bf16[2,4,32,384]{3,2,1,0:T(8,128)(2,1)S(1)} %get-tuple-element.37.own_ref.grad_ref), channel_id=1, source_target_pairs={{0,112},{16,0},{32,16},{48,32},{64,48},{80,64},{96,80},{112,96},{1... | collective-permute-start | bytes 589832 | tf_op jit(solution)/shard_map/ppermute | solution.py:464
  50.5 6.8 %collective-permute-start.7 = (bf16[2,32,384]{2,1,0:T(8,128)(2,1)S(1)}, bf16[2,32,384]{2,1,0:T(8,128)(2,1)S(1)}, u32[]{:S(2)}, u32[]{:S(2)}) collective-permute-start(bf16[2,32,384]{2,1,0:T(8,128)(2,1)S(1)} %get-tuple-element.39), channel_id=1, source_target_pairs={{1,2},{2,1},{3,4},{4,3},{5,6},{6,5},{7,8},{8,7},{9,10},{10,9},{11,... | collective-permute-start | bytes 147464 | tf_op jit(solution)/shard_map/ppermute | solution.py:465
  50.9 6.4 %collective-permute-start.9 = (bf16[2,32,384]{2,1,0:T(8,128)(2,1)S(1)}, bf16[2,32,384]{2,1,0:T(8,128)(2,1)S(1)}, u32[]{:S(2)}, u32[]{:S(2)}) collective-permute-start(bf16[2,32,384]{2,1,0:T(8,128)(2,1)S(1)} %get-tuple-element.39), channel_id=1, source_target_pairs={{1,114},{2,113},{3,116},{4,115},{5,118},{6,117},{7,120},{8,119},{9... | collective-permute-start | bytes 147464 | tf_op jit(solution)/shard_map/ppermute | solution.py:466
  51.1 6.2 %collective-permute-start.6 = (bf16[2,32,384]{2,1,0:T(8,128)(2,1)S(1)}, bf16[2,32,384]{2,1,0:T(8,128)(2,1)S(1)}, u32[]{:S(2)}, u32[]{:S(2)}) collective-permute-start(bf16[2,32,384]{2,1,0:T(8,128)(2,1)S(1)} %get-tuple-element.38), channel_id=1, source_target_pairs={{0,1},{1,0},{2,3},{3,2},{4,5},{5,4},{6,7},{7,6},{8,9},{9,8},{10,11... | collective-permute-start | bytes 147464 | tf_op jit(solution)/shard_map/ppermute | solution.py:467
  55.3 2.8 %collective-permute-start.8 = (bf16[2,32,384]{2,1,0:T(8,128)(2,1)S(1)}, bf16[2,32,384]{2,1,0:T(8,128)(2,1)S(1)}, u32[]{:S(2)}, u32[]{:S(2)}) collective-permute-start(bf16[2,32,384]{2,1,0:T(8,128)(2,1)S(1)} %get-tuple-element.40), channel_id=1, source_target_pairs={{0,1},{1,0},{2,3},{3,2},{4,5},{5,4},{6,7},{7,6},{8,9},{9,8},{10,11... | collective-permute-start | bytes 147464 | tf_op jit(solution)/shard_map/ppermute | solution.py:469
  72.1 6.5 %collective-permute-start.10 = (f32[2,32,128]{2,1,0:T(8,128)S(1)}, f32[2,32,128]{2,1,0:T(8,128)S(1)}, u32[]{:S(2)}, u32[]{:S(2)}) collective-permute-start(f32[2,32,128]{2,1,0:T(8,128)S(1)} %get-tuple-element.46), channel_id=1, source_target_pairs={{0,112},{16,0},{32,16},{48,32},{64,48},{80,64},{96,80},{112,96},{1... | collective-permute-start | bytes 98312 | tf_op jit(solution)/shard_map/ppermute | solution.py:525
where the time goes:
time: 89.8 us; the launch traced here: 89.4 us
  starting transfers between devices  34 us (38%)
  blocking collectives  30.9 us (34%)
  Pallas kernels  17.3 us (19%)
  local copies, waits for them, and re-layouts  4.69 us (5%)
  waiting for transfers between devices  2.23 us (2%)
    all_to_all x3, blocking collectives, everyone(): return lax.all_to_all(rows, TILE, 0, 0)  30.9 us
    ppermute x2, starting transfers between devices, exchange(): nxt = lax.ppermute(value, 'tm', back)  12.7 us
    pallas_call x1, Pallas kernels, conv_section(): pl.pallas_call(conv_kernel, out_shape=jax.ShapeDtypeStruct((count, channe...  5.73 us
    ppermute x2, starting transfers between devices, exchange(): ra = lax.ppermute(send_a, 'tile_2', swap)  5.7 us
    ppermute x1, starting transfers between devices, shards(): own = own + jnp.where(later, lax.ppermute(prev, 'tm', ring(tms)), 0.0)  5.47 us
    all_to_all x1, starting transfers between devices, everyone(): return lax.all_to_all(rows, TILE, 0, 0)  5.46 us
    pallas_call x1, Pallas kernels, conv_norm_section(): pl.pallas_call(functools.partial(conv_norm_kernel, cells, base), out_shap...  3.41 us
    pallas_call x3, Pallas kernels, edge_section(): pl.pallas_call(edge_kernel, out_shape=(edge, edge), in_specs=[pl.BlockSpe...  2.88 us
  transfers between devices with their start and end apart: 12, of which 3 were waited for; matrix products, arithmetic and copies ran while one was open for 1% of the time, Pallas kernels for 12%

commit v1 on v0

--- a/solution.py
+++ b/solution.py
@@ -65,9 +65,14 @@
     ref[...] = jnp.broadcast_to(rows[None], ref.shape)
 
 
-def moments_kernel(second_hbm, first_hbm, out_ref, second_ref, first_ref, sems):
+def moments_kernel(second_hbm, first_hbm, *refs):
+    vectors, (out_ref, affine_ref), scratch = refs[:4], refs[4:6], refs[6:]
+    second_ref, first_ref, lines, sems = *scratch[:2], scratch[2:6], scratch[6]
     pairs = ((second_hbm, second_ref), (first_hbm, first_ref))
-    copies = [pltpu.make_async_copy(*pair, sems.at[k]) for k, pair in enumerate(pairs)]
+    copies = [
+        pltpu.make_async_copy(*pair, sems.at[k])
+        for k, pair in enumerate(pairs + tuple(zip(vectors, lines)))
+    ]
     for copy in copies:
         copy.start()
     rows = []
@@ -78,30 +83,38 @@
         rows += [jnp.sum(v, axis=(0, 1)).reshape(1, -1) for v in values]
         rows += [jnp.sum(v * v, axis=(0, 1)).reshape(1, -1) for v in values]
     spread(out_ref, jnp.concatenate(rows, axis=0))
-
-
-def moments(second, first, peers):
+    for k, (copy, line) in enumerate(zip(copies[2:], lines)):
+        copy.wait()
+        affine_ref[k : k + 1] = line[...].reshape(1, -1)
+
+
+def moments(second, first, vectors, peers):
     frames, _, _, channels = second.shape
     return pl.pallas_call(
         moments_kernel,
-        out_shape=jax.ShapeDtypeStruct((peers, 4 * frames, channels), jnp.float32),
-        in_specs=[pl.BlockSpec(memory_space=pltpu.HBM)] * 2,
-        out_specs=pl.BlockSpec(memory_space=pltpu.VMEM),
+        out_shape=(
+            jax.ShapeDtypeStruct((peers, 4 * frames, channels), jnp.float32),
+            jax.ShapeDtypeStruct((len(vectors), channels), jnp.float32),
+        ),
+        in_specs=HBM * (2 + len(vectors)),
+        out_specs=tuple(vmem(2)),
         scratch_shapes=[
             pltpu.VMEM(second.shape, jnp.bfloat16),
             pltpu.VMEM(first.shape, jnp.bfloat16),
-            pltpu.SemaphoreType.DMA((2,)),
+            *[pltpu.VMEM(v.shape, jnp.float32) for v in vectors],
+            pltpu.SemaphoreType.DMA((2 + len(vectors),)),
         ],
         compiler_params=pltpu.CompilerParams(vmem_limit_bytes=16 * MIB),
         name="moments",
-    )(in_hbm(second), in_hbm(first))
+    )(*map(in_hbm, (second, first, *vectors)))
 
 
 def fill(ext, at, block, a, b, even):
     frames, cols = block.shape[:2]
     ext[at : at + frames, 1 : cols + 1] = block
-    ext[at : at + frames, 0] = jnp.where(even, b, a)
-    ext[at : at + frames, cols + 1] = jnp.where(even, a, b)
+    right, left = swapped(even, a, b)
+    ext[at : at + frames, 0] = left
+    ext[at : at + frames, cols + 1] = right
 
 
 def time_taps(ext, w_ref, taps, frames, cols):
@@ -132,14 +145,27 @@
     return wide[:, channels : 2 * channels] + up + down
 
 
+def flags(par_ref):
+    return [par_ref[k : k + 1] for k in range(3)]
+
+
+def swapped(even, a, b):
+    odd = 1 - even
+    return a * even + b * odd, b * even + a * odd
+
+
 def window(par_ref, own_ref, next_ref, ra_ref, rb_ref, ran_ref, rbn_ref, ext):
     frames = own_ref.shape[0]
-    even, side, later = par_ref[0] == 0, par_ref[1] == 1, par_ref[2] == 1
-    zero = jnp.bfloat16(0)
-    own = lambda v: jnp.where(side, v, zero)
-    nxt = lambda v: jnp.where(later, v, zero)
-    fill(ext, 0, own_ref[...], ra_ref[...], own(rb_ref[...]), even)
-    fill(ext, frames, nxt(next_ref[...]), nxt(ran_ref[...]), nxt(own(rbn_ref[...])), even)
+    even, side, later = flags(par_ref)
+    fill(ext, 0, own_ref[...], ra_ref[...], rb_ref[...] * side, even)
+    fill(
+        ext,
+        frames,
+        next_ref[...] * later,
+        ran_ref[...] * later,
+        rbn_ref[...] * (later * side),
+        even,
+    )
 
 
 def conv_kernel(
@@ -180,7 +206,7 @@
     return pl.pallas_call(
         conv_kernel,
         out_shape=jax.ShapeDtypeStruct((count, channels), jnp.float32),
-        in_specs=[pl.BlockSpec(memory_space=pltpu.SMEM)] + vmem(6) + HBM,
+        in_specs=vmem(7) + HBM,
         out_specs=vmem(1)[0],
         scratch_shapes=[
             pltpu.VMEM((2 * frames, cols + 2, rows, channels), jnp.bfloat16),
@@ -271,12 +297,11 @@
 
 def dx_kernel(cells, par_ref, grad_ref, q_ref, x_ref, stats_ref, sums_ref, dx_ref, sa_ref, sb_ref):
     _, cols, rows, channels = grad_ref.shape
-    even = par_ref[0] == 0
+    even, _, _ = flags(par_ref)
     for f, value in enumerate(block_grad(cells, grad_ref, q_ref, x_ref, stats_ref, sums_ref)):
         value = value.reshape(cols, rows, channels)
         dx_ref[f] = value
-        sa_ref[f] = jnp.where(even, value[cols - 1], value[0])
-        sb_ref[f] = jnp.where(even, value[0], value[cols - 1])
+        sa_ref[f], sb_ref[f] = swapped(even, value[cols - 1], value[0])
 
 
 def dx_section(par, grad, q, stored, stats, sums, cells):
@@ -285,7 +310,7 @@
     return pl.pallas_call(
         functools.partial(dx_kernel, cells),
         out_shape=(jax.ShapeDtypeStruct(grad.shape, jnp.bfloat16), edge, edge),
-        in_specs=[pl.BlockSpec(memory_space=pltpu.SMEM)] + vmem(5),
+        in_specs=vmem(6),
         out_specs=tuple(vmem(3)),
         compiler_params=pltpu.CompilerParams(vmem_limit_bytes=16 * MIB),
         cost_estimate=WEIGHTS_COVER,
@@ -326,7 +351,7 @@
     return pl.pallas_call(
         functools.partial(conv_norm_kernel, cells, base),
         out_shape=finish_shapes(stored, peers),
-        in_specs=[pl.BlockSpec(memory_space=pltpu.SMEM)] + vmem(10),
+        in_specs=vmem(11),
         out_specs=tuple(vmem(3)),
         scratch_shapes=[
             pltpu.VMEM((2 * frames, cols + 2, rows, channels), jnp.bfloat16),
@@ -340,10 +365,8 @@
 
 def edge_kernel(par_ref, block_ref, sa_ref, sb_ref):
     cols = block_ref.shape[1]
-    even = par_ref[0] == 0
-    first, last = block_ref[:, 0], block_ref[:, cols - 1]
-    sa_ref[...] = jnp.where(even, last, first)
-    sb_ref[...] = jnp.where(even, first, last)
+    even, _, _ = flags(par_ref)
+    sa_ref[...], sb_ref[...] = swapped(even, block_ref[:, cols - 1], block_ref[:, 0])
 
 
 def edge_section(par, block):
@@ -352,7 +375,7 @@
     return pl.pallas_call(
         edge_kernel,
         out_shape=(edge, edge),
-        in_specs=[pl.BlockSpec(memory_space=pltpu.SMEM)] + vmem(1),
+        in_specs=vmem(2),
         out_specs=tuple(vmem(2)),
         compiler_params=pltpu.CompilerParams(vmem_limit_bytes=4 * MIB),
         name="edge",
@@ -362,24 +385,39 @@
 def latent_kernel_body(cells, grad_ref, q_ref, x_ref, stats_ref, sums_ref, k_ref, own_ref, prev_ref, wide):
     frames, cols, rows, channels = grad_ref.shape
     lat = k_ref.shape[1]
-    lanes = wide.shape[1]
+    lanes = own_ref.shape[-1]
     values = block_grad(cells, grad_ref, q_ref, x_ref, stats_ref, sums_ref)
     grad = jnp.concatenate(values, axis=0)
     count = frames * cols * rows
     wide[...] = jnp.zeros_like(wide)
-    for k in range(9):
-        wide[k, 0 : 3 * lat] = k_ref[3 * k : 3 * k + 3].reshape(3 * lat, channels)
+    width = 3 * lat
+    spots = (0, width, lanes)
+    for b in range(3):
+        for a in range(3):
+            k = 9 * a + 3 * b
+            wide[b, spots[a] : spots[a] + width] = k_ref[k : k + 3].reshape(width, channels)
     row = lax.broadcasted_iota(jnp.int32, (count, 1), 0) % rows
+    z = [nt_dot(grad, wide[b]) for b in range(3)]
+    up = jnp.where(row < rows - 1, pltpu.roll(z[0], count - 1, 0), 0.0)
+    down = jnp.where(row > 0, pltpu.roll(z[2], 1, 0), 0.0)
+    total = z[1] + up + down
+    lane = lax.broadcasted_iota(jnp.int32, (1, lanes), 1)
+    both, third = total[:, :lanes], total[:, lanes:]
+    parts = (
+        jnp.where(lane < width, both, 0.0),
+        jnp.where(lane < width, 0.0, both),
+        third,
+    )
     placed = {}
     for a in range(3):
-        z = [nt_dot(grad, wide[3 * a + b]) for b in range(3)]
-        up = jnp.where(row < rows - 1, pltpu.roll(z[0], count - 1, 0), 0.0)
-        down = jnp.where(row > 0, pltpu.roll(z[2], 1, 0), 0.0)
-        total = (z[1] + up + down).reshape(frames, cols, rows, lanes)
+        part = parts[a].reshape(frames, cols, rows, lanes)
+        base = width if a == 1 else 0
         for f in range(frames):
-            out = total[f, 0]
-            for w in range(1, cols):
-                out = out + pltpu.roll(total[f, w], lat * w, 1)
+            out = None
+            for w in range(cols):
+                shift = (lat * w - base) % lanes
+                one = pltpu.roll(part[f, w], shift, 1) if shift else part[f, w]
+                out = one if out is None else out + one
             at = f + a - 2
             placed[at] = placed[at] + out if at in placed else out
     for f in range(frames):
@@ -396,7 +434,7 @@
         out_shape=(out, out),
         in_specs=vmem(6),
         out_specs=tuple(vmem(2)),
-        scratch_shapes=[pltpu.VMEM((9, lanes, channels), jnp.bfloat16)],
+        scratch_shapes=[pltpu.VMEM((3, 2 * lanes, channels), jnp.bfloat16)],
         compiler_params=pltpu.CompilerParams(vmem_limit_bytes=16 * MIB),
         name="latent",
     )(grad, q, stored, stats, sums, kernel)
@@ -452,7 +490,7 @@
     )(got, jnp.asarray(place, jnp.bfloat16), jnp.asarray(perm, jnp.bfloat16))
 
 
-def exchange(par, value, send_a, send_b):
+def exchange(value, send_a, send_b):
     tms = lax.axis_size("tm")
     tiles = lax.axis_size(TILE)
     back = ring(tms)
@@ -461,12 +499,14 @@
     for k in range(1, tiles, 2):
         hops += [(k, (k + 1) % tiles), ((k + 1) % tiles, k)]
     diagonal = [(t * tiles + s, u * tiles + d) for t, u in back for s, d in hops]
+    partner = [
+        (t * tiles + s, u * tiles + (s ^ 1)) for t, u in back for s in range(tiles)
+    ]
     nxt = lax.ppermute(value, "tm", back)
     rb = lax.ppermute(send_b, TILE, hops)
     rbn = lax.ppermute(send_b, TM_TILE, diagonal)
+    ran = lax.ppermute(send_a, TM_TILE, partner)
     ra = lax.ppermute(send_a, "tile_2", swap)
-    corner = edge_section(par, nxt)[0]
-    ran = lax.ppermute(corner, "tile_2", swap)
     return nxt, ra, rb, ran, rbn
 
 
@@ -498,24 +538,25 @@
     tile, when = lax.axis_index(TILE), lax.axis_index("tm")
     later = when < lax.axis_size("tm") - 1
     side = jnp.where(even, tile > 0, tile < peers - 1)
-    par = jnp.stack([core.astype(jnp.int32), side.astype(jnp.int32), later.astype(jnp.int32)])
-    affine = jnp.stack([second_gain, second_shift, first_gain, first_shift])
-    par, later, affine, output_grad, second_input, first_input = lax.optimization_barrier(
-        (par, later, affine, output_grad, second_input, first_input)
+    ones = jnp.stack([even, side, later]).astype(jnp.bfloat16)
+    par = jnp.broadcast_to(ones[:, None], (3, channels))
+    par, later, output_grad, second_input, first_input = lax.optimization_barrier(
+        (par, later, output_grad, second_input, first_input)
     )
     turn = lambda x: with_layout_constraint(
         jnp.transpose(x, (0, 2, 1, 3)), Layout(major_to_minor=(0, 1, 2, 3))
     )
 
     grad = turn(output_grad)
-    mine = moments(second_input, first_input, peers)
+    vectors = (second_gain, second_shift, first_gain, first_shift)
+    mine, affine = moments(second_input, first_input, vectors, peers)
     mom = everyone(mine)
-    halo = exchange(par, grad, *edge_section(par, grad))
+    halo = exchange(grad, *edge_section(par, grad))
     second, first = turn(second_input), turn(first_input)
     upstream = conv_section(par, grad, halo, second_kernel)
     q, sums, stats = norm_section(upstream, second, mom, affine, cells, peers)
     grad, send_a, send_b = dx_section(par, grad, q, second, stats, everyone(sums), cells)
-    nxt, ra, rb, ran, rbn = exchange(par, grad, send_a, send_b)
+    nxt, ra, rb, ran, rbn = exchange(grad, send_a, send_b)
     q, sums, stats = conv_norm_section(
         par, grad, (nxt, ra, rb, ran, rbn), first_kernel, first, mom, affine, cells,
         2 * frames, peers,

time: 89.8 us -> 80.4 us (0.90)
  starting transfers between devices: 34 us -> 27.4 us
  waiting for transfers between devices: 2.23 us -> 7.17 us
  Pallas kernels: 17.3 us -> 12.7 us
  local copies, waits for them, and re-layouts: 4.69 us -> 2.03 us
    ppermute x2, starting transfers between devices: 2.25 us -> 9.19 us  [exchange(): ran = lax.ppermute(send_a, TM_TILE, partner)]
    ppermute x2, starting transfers between devices: 12.7 us -> 6.82 us  [exchange(): nxt = lax.ppermute(value, 'tm', back)]
    ppermute x2, starting transfers between devices: 5.7 us -> 1.88 us  [exchange(): ra = lax.ppermute(send_a, 'tile_2', swap)]
    ppermute x2, waiting for transfers between devices: 0.01 us -> 3.33 us  [exchange(): rb = lax.ppermute(send_b, TILE, hops)]
    pallas_call x4 -> x2, Pallas kernels: 4.86 us -> 2.06 us  [the longest x1 2.03 us: moments(): pl.pallas_call(moments_kernel, out_shape=(jax.ShapeDtypeStruct((peers, 4...]
    another operation x4 -> x0, local copies, waits for them, and re-layouts: 2.73 us -> none  [shards(): affine = jnp.stack([second_gain, second_shift, first_gain, first_shift])]
    ppermute x1, starting transfers between devices: 5.47 us -> 3.22 us  [shards(): own = own + jnp.where(later, lax.ppermute(prev, 'tm', ring(tms)), 0.0)]
    ppermute x2, starting transfers between devices: 1.75 us -> 0.38 us  [exchange(): rb = lax.ppermute(send_b, TILE, hops)]
  transfers between devices with their start and end apart: 12 -> 12, of which waited for: 3 -> 5; matrix products, arithmetic and copies ran while one was open for 1% -> 1% of each run, Pallas kernels for 12% -> 9%
where the time goes in v1:
time: 80.4 us; the launch traced here: 80.1 us
  blocking collectives  30.6 us (38%)
  starting transfers between devices  27.4 us (34%)
  Pallas kernels  12.7 us (16%)
  waiting for transfers between devices  7.17 us (9%)
  local copies, waits for them, and re-layouts  2.03 us (3%)
    all_to_all x3, blocking collectives, everyone(): return lax.all_to_all(rows, TILE, 0, 0)  30.6 us
    ppermute x2, starting transfers between devices, exchange(): ran = lax.ppermute(send_a, TM_TILE, partner)  9.19 us
    ppermute x2, starting transfers between devices, exchange(): nxt = lax.ppermute(value, 'tm', back)  6.82 us
    all_to_all x1, starting transfers between devices, everyone(): return lax.all_to_all(rows, TILE, 0, 0)  5.86 us
    pallas_call x1, Pallas kernels, conv_section(): pl.pallas_call(conv_kernel, out_shape=jax.ShapeDtypeStruct((count, channe...  5.19 us
    ppermute x2, waiting for transfers between devices, exchange(): rb = lax.ppermute(send_b, TILE, hops)  3.33 us
    ppermute x1, starting transfers between devices, shards(): own = own + jnp.where(later, lax.ppermute(prev, 'tm', ring(tms)), 0.0)  3.22 us
    pallas_call x1, Pallas kernels, conv_norm_section(): pl.pallas_call(functools.partial(conv_norm_kernel, cells, base), out_shap...  2.89 us
  transfers between devices with their start and end apart: 12, of which 5 were waited for; matrix products, arithmetic and copies ran while one was open for 1% of the time, Pallas kernels for 9%

profile of v1, /device:TPU:1, one launch (start us, length us, event | category | flops | bytes accessed | tf_op | source)
XLA Modules:
  0.0 80.1 jit_solution(7282705886822748176)
XLA Ops:
  0.2 1.0 %copy.21 = bf16[2,32,4,384]{3,1,2,0:T(8,128)(2,1)S(1)} copy(bf16[2,32,4,384]{3,2,1,0:T(4,128)(2,1)} %param.14) | data formatting | bytes 393216 | tf_op jit(solution)/shard_map/optimization_barrier | solution.py:543
  1.1 6.0 %collective-permute-start = (bf16[2,4,32,384]{3,2,1,0:T(8,128)(2,1)S(1)}, bf16[2,4,32,384]{3,2,1,0:T(8,128)(2,1)S(1)}, u32[]{:S(2)}, u32[]{:S(2)}) collective-permute-start(bf16[2,4,32,384]{3,2,1,0:T(8,128)(2,1)S(1)} %bitcast.17), channel_id=1, source_target_pairs={{0,112},{16,0},{32,16},{48,32},{64,48},{80,64},{96,80},{112,96},{1... | collective-permute-start | bytes 589832 | tf_op jit(solution)/shard_map/ppermute | solution.py:505
  7.1 1.0 %collective-permute-start.1 = (bf16[2,32,384]{2,1,0:T(8,128)(2,1)S(1)}, bf16[2,32,384]{2,1,0:T(8,128)(2,1)S(1)}, u32[]{:S(2)}, u32[]{:S(2)}) collective-permute-start(bf16[2,32,384]{2,1,0:T(8,128)(2,1)S(1)} %get-tuple-element.27), channel_id=1, source_target_pairs={{0,1},{1,0},{2,3},{3,2},{4,5},{5,4},{6,7},{7,6},{8,9},{9,8},{10,11... | collective-permute-start | bytes 147464 | tf_op jit(solution)/shard_map/ppermute | solution.py:509
  8.5 5.3 %collective-permute-start.3 = (bf16[2,32,384]{2,1,0:T(8,128)(2,1)S(1)}, bf16[2,32,384]{2,1,0:T(8,128)(2,1)S(1)}, u32[]{:S(2)}, u32[]{:S(2)}) collective-permute-start(bf16[2,32,384]{2,1,0:T(8,128)(2,1)S(1)} %get-tuple-element.27), channel_id=1, source_target_pairs={{0,113},{1,112},{2,115},{3,114},{4,117},{5,116},{6,119},{7,118},{8... | collective-permute-start | bytes 147464 | tf_op jit(solution)/shard_map/ppermute | solution.py:508
  13.9 2.0 %moments.1 = (f32[16,8,384]{2,1,0:T(8,128)}, f32[4,384]{1,0:T(4,128)S(1)}) custom-call(bf16[2,32,4,384]{3,2,1,0:T(4,128)(2,1)} %second_hbm, bf16[2,32,4,384]{3,2,1,0:T(4,128)(2,1)} %first_hbm, f32[384]{0:T(512)} %refs_0_.1, f32[384]{0:T(512)} %refs_1_.1, f32[384]{0:T(512)} %refs_2_.1, f32[384]{0:T(512)} %refs_3_.1), custom_call_target="tpu_custom_call" | custom-call | tf_op jit(solution)/shard_map/moments/pallas_call | solution.py:93
  15.9 5.9 %all-to-all-start = ((f32[16,8,384]{2,1,0:T(8,128)}), f32[16,8,384]{2,1,0:T(8,128)S(1)}, u32[]{:S(2)}, u32[]{:S(2)}) async-start(f32[16,8,384]{2,1,0:T(8,128)} %get-tuple-element.31), calls=%async_computation | async-start | bytes 393216 | tf_op jit(solution)/shard_map/all_to_all | solution.py:518
  21.8 0.9 %copy.20 = bf16[2,32,4,384]{3,1,2,0:T(8,128)(2,1)S(1)} copy(bf16[2,32,4,384]{3,2,1,0:T(4,128)(2,1)} %second_hbm) | data formatting | bytes 393216 | tf_op jit(solution)/shard_map/optimization_barrier | solution.py:543
  22.8 5.2 %conv.1.u_ref = f32[256,384]{1,0:T(8,128)S(1)} custom-call(bf16[3,384]{1,0:T(4,128)(2,1)S(1)} %broadcast_in_dim.10.par_ref, bf16[2,4,32,384]{3,2,1,0:T(8,128)(2,1)S(1)} %bitcast.19, bf16[2,4,32,384]{3,2,1,0:T(8,128)(2,1)S(1)} %collective-permute-done.next_ref, bf16[2,32,384]{2,1,0:T(8,128)(2,1)S(1)} %collective-permute-done.1.ra_ref, ...), custom_call_target="tpu_custom_call" | custom-call | flops 2038431744 | bytes 7962624 | tf_op jit(solution)/shard_map/conv/pallas_call | solution.py:206
  28.0 0.5 all-to-all-done.mom_ref
  28.5 0.4 norm.1
  28.9 11.2 %all_to_all.20.sums_ref = f32[16,4,384]{2,1,0:T(4,128)S(1)} all-to-all(f32[16,4,384]{2,1,0:T(4,128)S(1)} %get-tuple-element.35), channel_id=1, replica_groups=mesh['tm'=8,'tile_0'=4,'tile_1'=2,'tile_2'=2] {'tile_0','tile_1','tile_2'}, dimensions={0} | all-to-all | bytes 196608 | tf_op jit(solution)/shard_map/all_to_all | solution.py:518
  40.5 0.8 %collective-permute-start.5 = (bf16[2,4,32,384]{3,2,1,0:T(8,128)(2,1)S(1)}, bf16[2,4,32,384]{3,2,1,0:T(8,128)(2,1)S(1)}, u32[]{:S(2)}, u32[]{:S(2)}) collective-permute-start(bf16[2,4,32,384]{3,2,1,0:T(8,128)(2,1)S(1)} %get-tuple-element.36.own_ref.grad_ref), channel_id=1, source_target_pairs={{0,112},{16,0},{32,16},{48,32},{64,48},{80,64},{96,80},{112,96},{1... | collective-permute-start | bytes 589832 | tf_op jit(solution)/shard_map/ppermute | solution.py:505
  41.4 0.8 %collective-permute-start.6 = (bf16[2,32,384]{2,1,0:T(8,128)(2,1)S(1)}, bf16[2,32,384]{2,1,0:T(8,128)(2,1)S(1)}, u32[]{:S(2)}, u32[]{:S(2)}) collective-permute-start(bf16[2,32,384]{2,1,0:T(8,128)(2,1)S(1)} %get-tuple-element.37), channel_id=1, source_target_pairs={{0,1},{1,0},{2,3},{3,2},{4,5},{5,4},{6,7},{7,6},{8,9},{9,8},{10,11... | collective-permute-start | bytes 147464 | tf_op jit(solution)/shard_map/ppermute | solution.py:509
  42.2 3.9 %collective-permute-start.8 = (bf16[2,32,384]{2,1,0:T(8,128)(2,1)S(1)}, bf16[2,32,384]{2,1,0:T(8,128)(2,1)S(1)}, u32[]{:S(2)}, u32[]{:S(2)}) collective-permute-start(bf16[2,32,384]{2,1,0:T(8,128)(2,1)S(1)} %get-tuple-element.37), channel_id=1, source_target_pairs={{0,113},{1,112},{2,115},{3,114},{4,117},{5,116},{6,119},{7,118},{8... | collective-permute-start | bytes 147464 | tf_op jit(solution)/shard_map/ppermute | solution.py:508
  46.1 3.3 %collective-permute-done.7.rb_ref = bf16[2,32,384]{2,1,0:T(8,128)(2,1)S(1)} collective-permute-done((bf16[2,32,384]{2,1,0:T(8,128)(2,1)S(1)}, bf16[2,32,384]{2,1,0:T(8,128)(2,1)S(1)}, u32[]{:S(2)}, u32[]{:S(2)}) %collective-permute-start.7) | collective-permute-done | bytes 49184 | tf_op jit(solution)/shard_map/ppermute | solution.py:506
  49.4 1.4 %collective-permute-done.8.ran_ref = bf16[2,32,384]{2,1,0:T(8,128)(2,1)S(1)} collective-permute-done((bf16[2,32,384]{2,1,0:T(8,128)(2,1)S(1)}, bf16[2,32,384]{2,1,0:T(8,128)(2,1)S(1)}, u32[]{:S(2)}, u32[]{:S(2)}) %collective-permute-start.8) | collective-permute-done | bytes 49184 | tf_op jit(solution)/shard_map/ppermute | solution.py:508
  50.8 0.8 %collective-permute-done.9.rbn_ref = bf16[2,32,384]{2,1,0:T(8,128)(2,1)S(1)} collective-permute-done((bf16[2,32,384]{2,1,0:T(8,128)(2,1)S(1)}, bf16[2,32,384]{2,1,0:T(8,128)(2,1)S(1)}, u32[]{:S(2)}, u32[]{:S(2)}) %collective-permute-start.9) | collective-permute-done | bytes 49184 | tf_op jit(solution)/shard_map/ppermute | solution.py:507
  51.7 2.9 %convnorm.1 = (f32[2,4,32,384]{3,2,1,0:T(8,128)S(1)}, f32[16,4,384]{2,1,0:T(4,128)S(1)}, f32[4,384]{1,0:T(4,128)S(1)}) custom-call(bf16[3,384]{1,0:T(4,128)(2,1)S(1)} %broadcast_in_dim.10.par_ref, bf16[2,4,32,384]{3,2,1,0:T(8,128)(2,1)S(1)} %get-tuple-element.36.own_ref.grad_ref, bf16[2,4,32,384]{3,2,1,0:T(8,128)(2,1)S(1)} %collective-permute-done.5.next_ref, ...), custom_call_target="tpu_custom_call" | custom-call | flops 2038431744 | bytes 7962624 | tf_op jit(solution)/shard_map/convnorm/pallas_call | solution.py:351
  54.6 9.4 %all_to_all.21.sums_ref = f32[16,4,384]{2,1,0:T(4,128)S(1)} all-to-all(f32[16,4,384]{2,1,0:T(4,128)S(1)} %get-tuple-element.41), channel_id=1, replica_groups=mesh['tm'=8,'tile_0'=4,'tile_1'=2,'tile_2'=2] {'tile_0','tile_1','tile_2'}, dimensions={0} | all-to-all | bytes 196608 | tf_op jit(solution)/shard_map/all_to_all | solution.py:518
  64.0 0.7 latent.1
  64.7 3.2 %collective-permute-start.10 = (f32[2,32,128]{2,1,0:T(8,128)S(1)}, f32[2,32,128]{2,1,0:T(8,128)S(1)}, u32[]{:S(2)}, u32[]{:S(2)}) collective-permute-start(f32[2,32,128]{2,1,0:T(8,128)S(1)} %get-tuple-element.44), channel_id=1, source_target_pairs={{0,112},{16,0},{32,16},{48,32},{64,48},{80,64},{96,80},{112,96},{1... | collective-permute-start | bytes 98312 | tf_op jit(solution)/shard_map/ppermute | solution.py:566
  67.9 1.1 %collective-permute-done.10 = f32[2,32,128]{2,1,0:T(8,128)S(1)} collective-permute-done((f32[2,32,128]{2,1,0:T(8,128)S(1)}, f32[2,32,128]{2,1,0:T(8,128)S(1)}, u32[]{:S(2)}, u32[]{:S(2)}) %collective-permute-start.10) | collective-permute-done | bytes 32800 | tf_op jit(solution)/shard_map/ppermute | solution.py:566
  69.0 10.0 %all_to_all.22.got_ref = f32[16,4,128]{2,1,0:T(4,128)S(1)} all-to-all(f32[16,4,128]{2,1,0:T(4,128)S(1)} %bitcast.23), channel_id=1, replica_groups=mesh['tm'=8,'tile_0'=4,'tile_1'=2,'tile_2'=2] {'tile_0','tile_1','tile_2'}, dimensions={0} | all-to-all | bytes 65536 | tf_op jit(solution)/shard_map/all_to_all | solution.py:518
  79.0 1.1 %assemble.1 = f32[64,64]{1,0:T(8,128)} custom-call(f32[16,4,128]{2,1,0:T(4,128)S(1)} %all_to_all.22.got_ref, bf16[96,768]{1,0:T(8,128)(2,1)S(1)} %copy-done.1, bf16[64,192]{1,0:T(8,128)(2,1)S(1)} %copy-done.2), custom_call_target="tpu_custom_call" | custom-call | tf_op jit(solution)/shard_map/assemble/pallas_call | solution.py:483
  (30 shorter events, 1.0 us)
Async XLA Ops:
  1.1 21.7 %collective-permute-start = (bf16[2,4,32,384]{3,2,1,0:T(8,128)(2,1)S(1)}, bf16[2,4,32,384]{3,2,1,0:T(8,128)(2,1)S(1)}, u32[]{:S(2)}, u32[]{:S(2)}) collective-permute-start(bf16[2,4,32,384]{3,2,1,0:T(8,128)(2,1)S(1)} %bitcast.17), channel_id=1, source_target_pairs={{0,112},{16,0},{32,16},{48,32},{64,48},{80,64},{96,80},{112,96},{1... | collective-permute-start | bytes 589832 | tf_op jit(solution)/shard_map/ppermute | solution.py:505
  7.1 15.6 %collective-permute-start.1 = (bf16[2,32,384]{2,1,0:T(8,128)(2,1)S(1)}, bf16[2,32,384]{2,1,0:T(8,128)(2,1)S(1)}, u32[]{:S(2)}, u32[]{:S(2)}) collective-permute-start(bf16[2,32,384]{2,1,0:T(8,128)(2,1)S(1)} %get-tuple-element.27), channel_id=1, source_target_pairs={{0,1},{1,0},{2,3},{3,2},{4,5},{5,4},{6,7},{7,6},{8,9},{9,8},{10,11... | collective-permute-start | bytes 147464 | tf_op jit(solution)/shard_map/ppermute | solution.py:509
  8.2 14.6 %collective-permute-start.2 = (bf16[2,32,384]{2,1,0:T(8,128)(2,1)S(1)}, bf16[2,32,384]{2,1,0:T(8,128)(2,1)S(1)}, u32[]{:S(2)}, u32[]{:S(2)}) collective-permute-start(bf16[2,32,384]{2,1,0:T(8,128)(2,1)S(1)} %get-tuple-element.28), channel_id=1, source_target_pairs={{1,2},{2,1},{3,4},{4,3},{5,6},{6,5},{7,8},{8,7},{9,10},{10,9},{11,... | collective-permute-start | bytes 147464 | tf_op jit(solution)/shard_map/ppermute | solution.py:506
  8.5 14.2 %collective-permute-start.3 = (bf16[2,32,384]{2,1,0:T(8,128)(2,1)S(1)}, bf16[2,32,384]{2,1,0:T(8,128)(2,1)S(1)}, u32[]{:S(2)}, u32[]{:S(2)}) collective-permute-start(bf16[2,32,384]{2,1,0:T(8,128)(2,1)S(1)} %get-tuple-element.27), channel_id=1, source_target_pairs={{0,113},{1,112},{2,115},{3,114},{4,117},{5,116},{6,119},{7,118},{8... | collective-permute-start | bytes 147464 | tf_op jit(solution)/shard_map/ppermute | solution.py:508
  13.9 8.9 %collective-permute-start.4 = (bf16[2,32,384]{2,1,0:T(8,128)(2,1)S(1)}, bf16[2,32,384]{2,1,0:T(8,128)(2,1)S(1)}, u32[]{:S(2)}, u32[]{:S(2)}) collective-permute-start(bf16[2,32,384]{2,1,0:T(8,128)(2,1)S(1)} %get-tuple-element.28), channel_id=1, source_target_pairs={{1,114},{2,113},{3,116},{4,115},{5,118},{6,117},{7,120},{8,119},{9... | collective-permute-start | bytes 147464 | tf_op jit(solution)/shard_map/ppermute | solution.py:507
  15.9 12.5 %all-to-all-start = ((f32[16,8,384]{2,1,0:T(8,128)}), f32[16,8,384]{2,1,0:T(8,128)S(1)}, u32[]{:S(2)}, u32[]{:S(2)}) async-start(f32[16,8,384]{2,1,0:T(8,128)} %get-tuple-element.31), calls=%async_computation | async-start | bytes 393216 | tf_op jit(solution)/shard_map/all_to_all | solution.py:518
  28.5 23.2 %slice-start = ((s8[7962624]{0:T(1024)(128)(4,1)}), s8[4194304]{0:T(1024)(128)(4,1)S(1)}, s32[]{:S(2)}) async-start(s8[7962624]{0:T(1024)(128)(4,1)} %bitcast.13), calls=%async_computation.4 | async-start | bytes 8388608
  40.2 5.9 %copy-start.3 = (bf16[2,32,4,384]{3,2,1,0:T(4,128)(2,1)S(1)}, bf16[2,32,4,384]{3,2,1,0:T(4,128)(2,1)}, u32[]{:S(2)}) copy-start(bf16[2,32,4,384]{3,2,1,0:T(4,128)(2,1)} %first_hbm) | copy-start | bytes 589828
  40.2 11.5 %slice-start.1 = ((s8[7962624]{0:T(1024)(128)(4,1)}), s8[3768320]{0:T(1024)(128)(4,1)S(1)}, s32[]{:S(2)}) async-start(s8[7962624]{0:T(1024)(128)(4,1)} %bitcast.13), calls=%async_computation.5 | async-start | bytes 7536640
  40.5 23.5 %copy-start = (bf16[27,16,384]{2,1,0:T(8,128)(2,1)S(1)}, bf16[27,16,384]{2,1,0:T(8,128)(2,1)}, u32[]{:S(2)}) copy-start(bf16[27,16,384]{2,1,0:T(8,128)(2,1)} %k_ref.1) | copy-start | bytes 995332
  40.5 38.5 %copy-start.1 = (bf16[96,768]{1,0:T(8,128)(2,1)S(1)}, bf16[96,768]{1,0:T(8,128)(2,1)}, u32[]{:S(2)}) copy-start(bf16[96,768]{1,0:T(8,128)(2,1)} %constant.33.clone.e_ref) | copy-start | bytes 442372
  40.5 38.5 %copy-start.2 = (bf16[64,192]{1,0:T(8,128)(2,1)S(1)}, bf16[64,192]{1,0:T(8,128)(2,1)}, u32[]{:S(2)}) copy-start(bf16[64,192]{1,0:T(8,128)(2,1)} %constant.34.clone.perm_ref) | copy-start | bytes 73732
  40.5 11.1 %collective-permute-start.5 = (bf16[2,4,32,384]{3,2,1,0:T(8,128)(2,1)S(1)}, bf16[2,4,32,384]{3,2,1,0:T(8,128)(2,1)S(1)}, u32[]{:S(2)}, u32[]{:S(2)}) collective-permute-start(bf16[2,4,32,384]{3,2,1,0:T(8,128)(2,1)S(1)} %get-tuple-element.36.own_ref.grad_ref), channel_id=1, source_target_pairs={{0,112},{16,0},{32,16},{48,32},{64,48},{80,64},{96,80},{112,96},{1... | collective-permute-start | bytes 589832 | tf_op jit(solution)/shard_map/ppermute | solution.py:505
  41.4 4.7 %collective-permute-start.6 = (bf16[2,32,384]{2,1,0:T(8,128)(2,1)S(1)}, bf16[2,32,384]{2,1,0:T(8,128)(2,1)S(1)}, u32[]{:S(2)}, u32[]{:S(2)}) collective-permute-start(bf16[2,32,384]{2,1,0:T(8,128)(2,1)S(1)} %get-tuple-element.37), channel_id=1, source_target_pairs={{0,1},{1,0},{2,3},{3,2},{4,5},{5,4},{6,7},{7,6},{8,9},{9,8},{10,11... | collective-permute-start | bytes 147464 | tf_op jit(solution)/shard_map/ppermute | solution.py:509
  42.2 7.2 %collective-permute-start.7 = (bf16[2,32,384]{2,1,0:T(8,128)(2,1)S(1)}, bf16[2,32,384]{2,1,0:T(8,128)(2,1)S(1)}, u32[]{:S(2)}, u32[]{:S(2)}) collective-permute-start(bf16[2,32,384]{2,1,0:T(8,128)(2,1)S(1)} %get-tuple-element.38), channel_id=1, source_target_pairs={{1,2},{2,1},{3,4},{4,3},{5,6},{6,5},{7,8},{8,7},{9,10},{10,9},{11,... | collective-permute-start | bytes 147464 | tf_op jit(solution)/shard_map/ppermute | solution.py:506
  42.2 8.6 %collective-permute-start.8 = (bf16[2,32,384]{2,1,0:T(8,128)(2,1)S(1)}, bf16[2,32,384]{2,1,0:T(8,128)(2,1)S(1)}, u32[]{:S(2)}, u32[]{:S(2)}) collective-permute-start(bf16[2,32,384]{2,1,0:T(8,128)(2,1)S(1)} %get-tuple-element.37), channel_id=1, source_target_pairs={{0,113},{1,112},{2,115},{3,114},{4,117},{5,116},{6,119},{7,118},{8... | collective-permute-start | bytes 147464 | tf_op jit(solution)/shard_map/ppermute | solution.py:508
  46.1 5.6 %collective-permute-start.9 = (bf16[2,32,384]{2,1,0:T(8,128)(2,1)S(1)}, bf16[2,32,384]{2,1,0:T(8,128)(2,1)S(1)}, u32[]{:S(2)}, u32[]{:S(2)}) collective-permute-start(bf16[2,32,384]{2,1,0:T(8,128)(2,1)S(1)} %get-tuple-element.38), channel_id=1, source_target_pairs={{1,114},{2,113},{3,116},{4,115},{5,118},{6,117},{7,120},{8,119},{9... | collective-permute-start | bytes 147464 | tf_op jit(solution)/shard_map/ppermute | solution.py:507
  64.7 4.3 %collective-permute-start.10 = (f32[2,32,128]{2,1,0:T(8,128)S(1)}, f32[2,32,128]{2,1,0:T(8,128)S(1)}, u32[]{:S(2)}, u32[]{:S(2)}) collective-permute-start(f32[2,32,128]{2,1,0:T(8,128)S(1)} %get-tuple-element.44), channel_id=1, source_target_pairs={{0,112},{16,0},{32,16},{48,32},{64,48},{80,64},{96,80},{112,96},{1... | collective-permute-start | bytes 98312 | tf_op jit(solution)/shard_map/ppermute | solution.py:566

commit v2 on v1

--- a/solution.py
+++ b/solution.py
@@ -22,6 +22,7 @@
 
 
 WEIGHTS_COVER = pl.CostEstimate(flops=1 << 33, bytes_accessed=1 << 23, transcendentals=0)
+INPUTS_COVER = pl.CostEstimate(flops=1 << 31, bytes_accessed=1 << 20, transcendentals=0)
 HBM = [pl.BlockSpec(memory_space=pltpu.HBM)]
 
 
@@ -65,25 +66,21 @@
     ref[...] = jnp.broadcast_to(rows[None], ref.shape)
 
 
-def moments_kernel(second_hbm, first_hbm, *refs):
-    vectors, (out_ref, affine_ref), scratch = refs[:4], refs[4:6], refs[6:]
-    second_ref, first_ref, lines, sems = *scratch[:2], scratch[2:6], scratch[6]
-    pairs = ((second_hbm, second_ref), (first_hbm, first_ref))
+def moments_kernel(second_ref, first_ref, *refs):
+    vectors, (out_ref, affine_ref), (*lines, sems) = refs[:4], refs[4:6], refs[6:]
     copies = [
-        pltpu.make_async_copy(*pair, sems.at[k])
-        for k, pair in enumerate(pairs + tuple(zip(vectors, lines)))
+        pltpu.make_async_copy(*pair, sems.at[k]) for k, pair in enumerate(zip(vectors, lines))
     ]
     for copy in copies:
         copy.start()
     rows = []
-    for copy, (_, ref) in zip(copies, pairs):
-        copy.wait()
+    for ref in (second_ref, first_ref):
         frames = ref.shape[0]
         values = [ref[f].astype(jnp.float32) for f in range(frames)]
         rows += [jnp.sum(v, axis=(0, 1)).reshape(1, -1) for v in values]
         rows += [jnp.sum(v * v, axis=(0, 1)).reshape(1, -1) for v in values]
     spread(out_ref, jnp.concatenate(rows, axis=0))
-    for k, (copy, line) in enumerate(zip(copies[2:], lines)):
+    for k, (copy, line) in enumerate(zip(copies, lines)):
         copy.wait()
         affine_ref[k : k + 1] = line[...].reshape(1, -1)
 
@@ -96,17 +93,15 @@
             jax.ShapeDtypeStruct((peers, 4 * frames, channels), jnp.float32),
             jax.ShapeDtypeStruct((len(vectors), channels), jnp.float32),
         ),
-        in_specs=HBM * (2 + len(vectors)),
+        in_specs=vmem(2) + HBM * len(vectors),
         out_specs=tuple(vmem(2)),
         scratch_shapes=[
-            pltpu.VMEM(second.shape, jnp.bfloat16),
-            pltpu.VMEM(first.shape, jnp.bfloat16),
             *[pltpu.VMEM(v.shape, jnp.float32) for v in vectors],
-            pltpu.SemaphoreType.DMA((2 + len(vectors),)),
+            pltpu.SemaphoreType.DMA((len(vectors),)),
         ],
         compiler_params=pltpu.CompilerParams(vmem_limit_bytes=16 * MIB),
         name="moments",
-    )(*map(in_hbm, (second, first, *vectors)))
+    )(second, first, *map(in_hbm, vectors))
 
 
 def fill(ext, at, block, a, b, even):
@@ -363,21 +358,23 @@
     )(par, grad, *halo, kernel, stored, mom, affine)
 
 
-def edge_kernel(par_ref, block_ref, sa_ref, sb_ref):
+def edge_kernel(par_ref, block_ref, *out_refs):
     cols = block_ref.shape[1]
     even, _, _ = flags(par_ref)
-    sa_ref[...], sb_ref[...] = swapped(even, block_ref[:, cols - 1], block_ref[:, 0])
-
-
-def edge_section(par, block):
+    for ref, value in zip(out_refs, swapped(even, block_ref[:, cols - 1], block_ref[:, 0])):
+        ref[...] = value
+
+
+def edge_section(par, block, count, cost):
     frames, _, rows, channels = block.shape
     edge = jax.ShapeDtypeStruct((frames, rows, channels), block.dtype)
     return pl.pallas_call(
         edge_kernel,
-        out_shape=(edge, edge),
+        out_shape=(edge,) * count,
         in_specs=vmem(2),
-        out_specs=tuple(vmem(2)),
+        out_specs=tuple(vmem(count)),
         compiler_params=pltpu.CompilerParams(vmem_limit_bytes=4 * MIB),
+        cost_estimate=cost,
         name="edge",
     )(par, block)
 
@@ -490,7 +487,7 @@
     )(got, jnp.asarray(place, jnp.bfloat16), jnp.asarray(perm, jnp.bfloat16))
 
 
-def exchange(value, send_a, send_b):
+def exchange(par, value, send_a, send_b):
     tms = lax.axis_size("tm")
     tiles = lax.axis_size(TILE)
     back = ring(tms)
@@ -499,14 +496,12 @@
     for k in range(1, tiles, 2):
         hops += [(k, (k + 1) % tiles), ((k + 1) % tiles, k)]
     diagonal = [(t * tiles + s, u * tiles + d) for t, u in back for s, d in hops]
-    partner = [
-        (t * tiles + s, u * tiles + (s ^ 1)) for t, u in back for s in range(tiles)
-    ]
     nxt = lax.ppermute(value, "tm", back)
     rb = lax.ppermute(send_b, TILE, hops)
     rbn = lax.ppermute(send_b, TM_TILE, diagonal)
-    ran = lax.ppermute(send_a, TM_TILE, partner)
     ra = lax.ppermute(send_a, "tile_2", swap)
+    (corner,) = edge_section(par, nxt, 1, None)
+    ran = lax.ppermute(corner, "tile_2", swap)
     return nxt, ra, rb, ran, rbn
 
 
@@ -551,12 +546,12 @@
     vectors = (second_gain, second_shift, first_gain, first_shift)
     mine, affine = moments(second_input, first_input, vectors, peers)
     mom = everyone(mine)
-    halo = exchange(grad, *edge_section(par, grad))
+    halo = exchange(par, grad, *edge_section(par, grad, 2, INPUTS_COVER))
     second, first = turn(second_input), turn(first_input)
     upstream = conv_section(par, grad, halo, second_kernel)
     q, sums, stats = norm_section(upstream, second, mom, affine, cells, peers)
     grad, send_a, send_b = dx_section(par, grad, q, second, stats, everyone(sums), cells)
-    nxt, ra, rb, ran, rbn = exchange(grad, send_a, send_b)
+    nxt, ra, rb, ran, rbn = exchange(par, grad, send_a, send_b)
     q, sums, stats = conv_norm_section(
         par, grad, (nxt, ra, rb, ran, rbn), first_kernel, first, mom, affine, cells,
         2 * frames, peers,

time: 80.4 us -> 81.7 us (1.016)
  starting transfers between devices: 27.4 us -> 33.7 us
  waiting for transfers between devices: 7.17 us -> 3.63 us
  local copies, waits for them, and re-layouts: 2.03 us -> 1.14 us
    ppermute x2, starting transfers between devices: 9.19 us -> 2.91 us  [exchange(): ran = lax.ppermute(corner, 'tile_2', swap)]
    ppermute x2, starting transfers between devices: 6.82 us -> 12.7 us  [exchange(): nxt = lax.ppermute(value, 'tm', back)]
    ppermute x2, starting transfers between devices: 1.88 us -> 5.7 us  [exchange(): ra = lax.ppermute(send_a, 'tile_2', swap)]
    ppermute x2, waiting for transfers between devices: 3.33 us -> 0.01 us  [exchange(): rb = lax.ppermute(send_b, TILE, hops)]
    ppermute x2, starting transfers between devices: 0.38 us -> 1.75 us  [exchange(): rb = lax.ppermute(send_b, TILE, hops)]
    ppermute x1, starting transfers between devices: 3.22 us -> 4.43 us  [shards(): own = own + jnp.where(later, lax.ppermute(prev, 'tm', ring(tms)), 0.0)]
    all_to_all x1, waiting for transfers between devices: 0.49 us -> 1.39 us  [everyone(): return lax.all_to_all(rows, TILE, 0, 0)]
    optimization_barrier x3, local copies, waits for them, and re-layouts: 1.93 us -> 1.03 us  [shards(): lax.optimization_barrier((par, later, output_grad, second_input, first_in...]
  transfers between devices with their start and end apart: 12 -> 12, of which waited for: 5 -> 5; matrix products, arithmetic and copies ran while one was open for 1% -> 0% of each run, Pallas kernels for 9% -> 8%
where the time goes in v2:
time: 81.7 us; the launch traced here: 81.4 us
  starting transfers between devices  33.7 us (41%)
  blocking collectives  30.6 us (37%)
  Pallas kernels  12.1 us (15%)
  waiting for transfers between devices  3.63 us (4%)
  local copies, waits for them, and re-layouts  1.14 us (1%)
    all_to_all x3, blocking collectives, everyone(): return lax.all_to_all(rows, TILE, 0, 0)  30.6 us
    ppermute x2, starting transfers between devices, exchange(): nxt = lax.ppermute(value, 'tm', back)  12.7 us
    ppermute x2, starting transfers between devices, exchange(): ra = lax.ppermute(send_a, 'tile_2', swap)  5.7 us
    all_to_all x1, starting transfers between devices, everyone(): return lax.all_to_all(rows, TILE, 0, 0)  5.61 us
    pallas_call x1, Pallas kernels, conv_section(): pl.pallas_call(conv_kernel, out_shape=jax.ShapeDtypeStruct((count, channe...  5.18 us
    ppermute x1, starting transfers between devices, shards(): own = own + jnp.where(later, lax.ppermute(prev, 'tm', ring(tms)), 0.0)  4.43 us
    ppermute x2, starting transfers between devices, exchange(): ran = lax.ppermute(corner, 'tile_2', swap)  2.91 us
    pallas_call x1, Pallas kernels, conv_norm_section(): pl.pallas_call(functools.partial(conv_norm_kernel, cells, base), out_shap...  2.89 us
  transfers between devices with their start and end apart: 12, of which 5 were waited for; matrix products, arithmetic and copies ran while one was open for 0% of the time, Pallas kernels for 8%

profile of v2, /device:TPU:1, one launch (start us, length us, event | category | flops | bytes accessed | tf_op | source)
XLA Modules:
  0.0 81.4 jit_solution(17079632345838698624)
XLA Ops:
  0.2 1.0 %copy.21 = bf16[2,32,4,384]{3,1,2,0:T(8,128)(2,1)S(1)} copy(bf16[2,32,4,384]{3,2,1,0:T(4,128)(2,1)} %param.14) | data formatting | bytes 393216 | tf_op jit(solution)/shard_map/optimization_barrier | solution.py:538
  1.1 6.0 %collective-permute-start = (bf16[2,4,32,384]{3,2,1,0:T(8,128)(2,1)S(1)}, bf16[2,4,32,384]{3,2,1,0:T(8,128)(2,1)S(1)}, u32[]{:S(2)}, u32[]{:S(2)}) collective-permute-start(bf16[2,4,32,384]{3,2,1,0:T(8,128)(2,1)S(1)} %bitcast.19), channel_id=1, source_target_pairs={{0,112},{16,0},{32,16},{48,32},{64,48},{80,64},{96,80},{112,96},{1... | collective-permute-start | bytes 589832 | tf_op jit(solution)/shard_map/ppermute | solution.py:499
  7.2 1.3 %collective-permute-start.2 = (bf16[2,32,384]{2,1,0:T(8,128)(2,1)S(1)}, bf16[2,32,384]{2,1,0:T(8,128)(2,1)S(1)}, u32[]{:S(2)}, u32[]{:S(2)}) collective-permute-start(bf16[2,32,384]{2,1,0:T(8,128)(2,1)S(1)} %get-tuple-element.28), channel_id=1, source_target_pairs={{1,2},{2,1},{3,4},{4,3},{5,6},{6,5},{7,8},{8,7},{9,10},{10,9},{11,... | collective-permute-start | bytes 147464 | tf_op jit(solution)/shard_map/ppermute | solution.py:500
  8.5 0.5 collective-permute-start.4
  8.9 3.0 %collective-permute-start.1 = (bf16[2,32,384]{2,1,0:T(8,128)(2,1)S(1)}, bf16[2,32,384]{2,1,0:T(8,128)(2,1)S(1)}, u32[]{:S(2)}, u32[]{:S(2)}) collective-permute-start(bf16[2,32,384]{2,1,0:T(8,128)(2,1)S(1)} %get-tuple-element.27), channel_id=1, source_target_pairs={{0,1},{1,0},{2,3},{3,2},{4,5},{5,4},{6,7},{7,6},{8,9},{9,8},{10,11... | collective-permute-start | bytes 147464 | tf_op jit(solution)/shard_map/ppermute | solution.py:502
  12.0 0.9 %collective-permute-start.3 = (bf16[2,32,384]{2,1,0:T(8,128)(2,1)S(1)}, bf16[2,32,384]{2,1,0:T(8,128)(2,1)S(1)}, u32[]{:S(2)}, u32[]{:S(2)}) collective-permute-start(bf16[2,32,384]{2,1,0:T(8,128)(2,1)S(1)} %edge.4), channel_id=1, source_target_pairs={{0,1},{1,0},{2,3},{3,2},{4,5},{5,4},{6,7},{7,6},{8,9},{9,8},{10,11... | collective-permute-start | bytes 147464 | tf_op jit(solution)/shard_map/ppermute | solution.py:504
  12.9 1.4 %moments.1 = (f32[16,8,384]{2,1,0:T(8,128)}, f32[4,384]{1,0:T(4,128)S(1)}) custom-call(bf16[2,32,4,384]{3,2,1,0:T(4,128)(2,1)S(1)} %copy-done, bf16[2,32,4,384]{3,2,1,0:T(4,128)(2,1)S(1)} %copy-done.1, f32[384]{0:T(512)} %refs_0_.1, f32[384]{0:T(512)} %refs_1_.1, f32[384]{0:T(512)} %refs_2_.1, f32[384]{0:T(512)} %refs_3_.1), custom_call_target="tpu_custom_call" | custom-call | tf_op jit(solution)/shard_map/moments/pallas_call | solution.py:90
  14.3 5.6 %all-to-all-start = ((f32[16,8,384]{2,1,0:T(8,128)}), f32[16,8,384]{2,1,0:T(8,128)S(1)}, u32[]{:S(2)}, u32[]{:S(2)}) async-start(f32[16,8,384]{2,1,0:T(8,128)} %get-tuple-element.31), calls=%async_computation | async-start | bytes 393216 | tf_op jit(solution)/shard_map/all_to_all | solution.py:513
  20.0 5.2 %conv.1.u_ref = f32[256,384]{1,0:T(8,128)S(1)} custom-call(bf16[3,384]{1,0:T(4,128)(2,1)S(1)} %broadcast_in_dim.10.par_ref, bf16[2,4,32,384]{3,2,1,0:T(8,128)(2,1)S(1)} %bitcast.21, bf16[2,4,32,384]{3,2,1,0:T(8,128)(2,1)S(1)} %collective-permute-done.block_ref.next_ref, bf16[2,32,384]{2,1,0:T(8,128)(2,1)S(1)} %collective-permute-done.1.ra_ref, ...), custom_call_target="tpu_custom_call" | custom-call | flops 2038431744 | bytes 7962624 | tf_op jit(solution)/shard_map/conv/pallas_call | solution.py:201
  25.2 1.4 %all-to-all-done.mom_ref = f32[16,8,384]{2,1,0:T(8,128)S(1)} async-done(((f32[16,8,384]{2,1,0:T(8,128)}), f32[16,8,384]{2,1,0:T(8,128)S(1)}, u32[]{:S(2)}, u32[]{:S(2)}) %all-to-all-start) | async-done | bytes 196640 | tf_op jit(solution)/shard_map/all_to_all | solution.py:513
  26.6 0.4 norm.1
  27.0 10.3 %all_to_all.20.sums_ref = f32[16,4,384]{2,1,0:T(4,128)S(1)} all-to-all(f32[16,4,384]{2,1,0:T(4,128)S(1)} %get-tuple-element.35), channel_id=1, replica_groups=mesh['tm'=8,'tile_0'=4,'tile_1'=2,'tile_2'=2] {'tile_0','tile_1','tile_2'}, dimensions={0} | all-to-all | bytes 196608 | tf_op jit(solution)/shard_map/all_to_all | solution.py:513
  37.7 6.7 %collective-permute-start.5 = (bf16[2,4,32,384]{3,2,1,0:T(8,128)(2,1)S(1)}, bf16[2,4,32,384]{3,2,1,0:T(8,128)(2,1)S(1)}, u32[]{:S(2)}, u32[]{:S(2)}) collective-permute-start(bf16[2,4,32,384]{3,2,1,0:T(8,128)(2,1)S(1)} %get-tuple-element.36.own_ref.grad_ref), channel_id=1, source_target_pairs={{0,112},{16,0},{32,16},{48,32},{64,48},{80,64},{96,80},{112,96},{1... | collective-permute-start | bytes 589832 | tf_op jit(solution)/shard_map/ppermute | solution.py:499
  44.3 0.4 collective-permute-start.7
  45.0 2.7 %collective-permute-start.6 = (bf16[2,32,384]{2,1,0:T(8,128)(2,1)S(1)}, bf16[2,32,384]{2,1,0:T(8,128)(2,1)S(1)}, u32[]{:S(2)}, u32[]{:S(2)}) collective-permute-start(bf16[2,32,384]{2,1,0:T(8,128)(2,1)S(1)} %get-tuple-element.37), channel_id=1, source_target_pairs={{0,1},{1,0},{2,3},{3,2},{4,5},{5,4},{6,7},{7,6},{8,9},{9,8},{10,11... | collective-permute-start | bytes 147464 | tf_op jit(solution)/shard_map/ppermute | solution.py:502
  48.1 2.0 %collective-permute-start.8 = (bf16[2,32,384]{2,1,0:T(8,128)(2,1)S(1)}, bf16[2,32,384]{2,1,0:T(8,128)(2,1)S(1)}, u32[]{:S(2)}, u32[]{:S(2)}) collective-permute-start(bf16[2,32,384]{2,1,0:T(8,128)(2,1)S(1)} %edge.5), channel_id=1, source_target_pairs={{0,1},{1,0},{2,3},{3,2},{4,5},{5,4},{6,7},{7,6},{8,9},{9,8},{10,11... | collective-permute-start | bytes 147464 | tf_op jit(solution)/shard_map/ppermute | solution.py:504
  50.3 0.7 collective-permute-done.8.ran_ref
  51.0 2.9 %convnorm.1 = (f32[2,4,32,384]{3,2,1,0:T(8,128)S(1)}, f32[16,4,384]{2,1,0:T(4,128)S(1)}, f32[4,384]{1,0:T(4,128)S(1)}) custom-call(bf16[3,384]{1,0:T(4,128)(2,1)S(1)} %broadcast_in_dim.10.par_ref, bf16[2,4,32,384]{3,2,1,0:T(8,128)(2,1)S(1)} %get-tuple-element.36.own_ref.grad_ref, bf16[2,4,32,384]{3,2,1,0:T(8,128)(2,1)S(1)} %collective-permute-done.5.block_ref.next_ref, ...), custom_call_target="tpu_custom_call" | custom-call | flops 2038431744 | bytes 7962624 | tf_op jit(solution)/shard_map/convnorm/pallas_call | solution.py:346
  53.9 10.6 %all_to_all.21.sums_ref = f32[16,4,384]{2,1,0:T(4,128)S(1)} all-to-all(f32[16,4,384]{2,1,0:T(4,128)S(1)} %get-tuple-element.41), channel_id=1, replica_groups=mesh['tm'=8,'tile_0'=4,'tile_1'=2,'tile_2'=2] {'tile_0','tile_1','tile_2'}, dimensions={0} | all-to-all | bytes 196608 | tf_op jit(solution)/shard_map/all_to_all | solution.py:513
  64.5 0.7 latent.1
  65.2 4.4 %collective-permute-start.10 = (f32[2,32,128]{2,1,0:T(8,128)S(1)}, f32[2,32,128]{2,1,0:T(8,128)S(1)}, u32[]{:S(2)}, u32[]{:S(2)}) collective-permute-start(f32[2,32,128]{2,1,0:T(8,128)S(1)} %get-tuple-element.44), channel_id=1, source_target_pairs={{0,112},{16,0},{32,16},{48,32},{64,48},{80,64},{96,80},{112,96},{1... | collective-permute-start | bytes 98312 | tf_op jit(solution)/shard_map/ppermute | solution.py:561
  69.6 1.0 %collective-permute-done.10 = f32[2,32,128]{2,1,0:T(8,128)S(1)} collective-permute-done((f32[2,32,128]{2,1,0:T(8,128)S(1)}, f32[2,32,128]{2,1,0:T(8,128)S(1)}, u32[]{:S(2)}, u32[]{:S(2)}) %collective-permute-start.10) | collective-permute-done | bytes 32800 | tf_op jit(solution)/shard_map/ppermute | solution.py:561
  70.7 9.7 %all_to_all.22.got_ref = f32[16,4,128]{2,1,0:T(4,128)S(1)} all-to-all(f32[16,4,128]{2,1,0:T(4,128)S(1)} %bitcast.23), channel_id=1, replica_groups=mesh['tm'=8,'tile_0'=4,'tile_1'=2,'tile_2'=2] {'tile_0','tile_1','tile_2'}, dimensions={0} | all-to-all | bytes 65536 | tf_op jit(solution)/shard_map/all_to_all | solution.py:513
  80.4 1.1 %assemble.1 = f32[64,64]{1,0:T(8,128)} custom-call(f32[16,4,128]{2,1,0:T(4,128)S(1)} %all_to_all.22.got_ref, bf16[96,768]{1,0:T(8,128)(2,1)S(1)} %copy-done.3, bf16[64,192]{1,0:T(8,128)(2,1)S(1)} %copy-done.4), custom_call_target="tpu_custom_call" | custom-call | tf_op jit(solution)/shard_map/assemble/pallas_call | solution.py:480
  (34 shorter events, 1.4 us)
Async XLA Ops:
  0.0 12.9 %copy-start.1 = (bf16[2,32,4,384]{3,2,1,0:T(4,128)(2,1)S(1)}, bf16[2,32,4,384]{3,2,1,0:T(4,128)(2,1)}, u32[]{:S(2)}) copy-start(bf16[2,32,4,384]{3,2,1,0:T(4,128)(2,1)} %first_ref) | copy-start | bytes 589828
  0.0 12.9 %copy-start = (bf16[2,32,4,384]{3,2,1,0:T(4,128)(2,1)S(1)}, bf16[2,32,4,384]{3,2,1,0:T(4,128)(2,1)}, u32[]{:S(2)}) copy-start(bf16[2,32,4,384]{3,2,1,0:T(4,128)(2,1)} %second_ref) | copy-start | bytes 589828
  1.1 10.8 %collective-permute-start = (bf16[2,4,32,384]{3,2,1,0:T(8,128)(2,1)S(1)}, bf16[2,4,32,384]{3,2,1,0:T(8,128)(2,1)S(1)}, u32[]{:S(2)}, u32[]{:S(2)}) collective-permute-start(bf16[2,4,32,384]{3,2,1,0:T(8,128)(2,1)S(1)} %bitcast.19), channel_id=1, source_target_pairs={{0,112},{16,0},{32,16},{48,32},{64,48},{80,64},{96,80},{112,96},{1... | collective-permute-start | bytes 589832 | tf_op jit(solution)/shard_map/ppermute | solution.py:499
  7.2 12.8 %collective-permute-start.2 = (bf16[2,32,384]{2,1,0:T(8,128)(2,1)S(1)}, bf16[2,32,384]{2,1,0:T(8,128)(2,1)S(1)}, u32[]{:S(2)}, u32[]{:S(2)}) collective-permute-start(bf16[2,32,384]{2,1,0:T(8,128)(2,1)S(1)} %get-tuple-element.28), channel_id=1, source_target_pairs={{1,2},{2,1},{3,4},{4,3},{5,6},{6,5},{7,8},{8,7},{9,10},{10,9},{11,... | collective-permute-start | bytes 147464 | tf_op jit(solution)/shard_map/ppermute | solution.py:500
  8.5 11.5 %collective-permute-start.4 = (bf16[2,32,384]{2,1,0:T(8,128)(2,1)S(1)}, bf16[2,32,384]{2,1,0:T(8,128)(2,1)S(1)}, u32[]{:S(2)}, u32[]{:S(2)}) collective-permute-start(bf16[2,32,384]{2,1,0:T(8,128)(2,1)S(1)} %get-tuple-element.28), channel_id=1, source_target_pairs={{1,114},{2,113},{3,116},{4,115},{5,118},{6,117},{7,120},{8,119},{9... | collective-permute-start | bytes 147464 | tf_op jit(solution)/shard_map/ppermute | solution.py:501
  8.9 11.0 %collective-permute-start.1 = (bf16[2,32,384]{2,1,0:T(8,128)(2,1)S(1)}, bf16[2,32,384]{2,1,0:T(8,128)(2,1)S(1)}, u32[]{:S(2)}, u32[]{:S(2)}) collective-permute-start(bf16[2,32,384]{2,1,0:T(8,128)(2,1)S(1)} %get-tuple-element.27), channel_id=1, source_target_pairs={{0,1},{1,0},{2,3},{3,2},{4,5},{5,4},{6,7},{7,6},{8,9},{9,8},{10,11... | collective-permute-start | bytes 147464 | tf_op jit(solution)/shard_map/ppermute | solution.py:502
  12.0 8.0 %collective-permute-start.3 = (bf16[2,32,384]{2,1,0:T(8,128)(2,1)S(1)}, bf16[2,32,384]{2,1,0:T(8,128)(2,1)S(1)}, u32[]{:S(2)}, u32[]{:S(2)}) collective-permute-start(bf16[2,32,384]{2,1,0:T(8,128)(2,1)S(1)} %edge.4), channel_id=1, source_target_pairs={{0,1},{1,0},{2,3},{3,2},{4,5},{5,4},{6,7},{7,6},{8,9},{9,8},{10,11... | collective-permute-start | bytes 147464 | tf_op jit(solution)/shard_map/ppermute | solution.py:504
  14.3 12.3 %all-to-all-start = ((f32[16,8,384]{2,1,0:T(8,128)}), f32[16,8,384]{2,1,0:T(8,128)S(1)}, u32[]{:S(2)}, u32[]{:S(2)}) async-start(f32[16,8,384]{2,1,0:T(8,128)} %get-tuple-element.31), calls=%async_computation | async-start | bytes 393216 | tf_op jit(solution)/shard_map/all_to_all | solution.py:513
  26.6 24.4 %slice-start = ((s8[7962624]{0:T(1024)(128)(4,1)}), s8[4194304]{0:T(1024)(128)(4,1)S(1)}, s32[]{:S(2)}) async-start(s8[7962624]{0:T(1024)(128)(4,1)} %bitcast.13), calls=%async_computation.4 | async-start | bytes 8388608
  37.3 13.7 %slice-start.1 = ((s8[7962624]{0:T(1024)(128)(4,1)}), s8[3768320]{0:T(1024)(128)(4,1)S(1)}, s32[]{:S(2)}) async-start(s8[7962624]{0:T(1024)(128)(4,1)} %bitcast.13), calls=%async_computation.5 | async-start | bytes 7536640
  37.6 26.9 %copy-start.2 = (bf16[27,16,384]{2,1,0:T(8,128)(2,1)S(1)}, bf16[27,16,384]{2,1,0:T(8,128)(2,1)}, u32[]{:S(2)}) copy-start(bf16[27,16,384]{2,1,0:T(8,128)(2,1)} %k_ref.1) | copy-start | bytes 995332
  37.7 42.7 %copy-start.3 = (bf16[96,768]{1,0:T(8,128)(2,1)S(1)}, bf16[96,768]{1,0:T(8,128)(2,1)}, u32[]{:S(2)}) copy-start(bf16[96,768]{1,0:T(8,128)(2,1)} %constant.33.clone.e_ref) | copy-start | bytes 442372
  37.7 42.7 %copy-start.4 = (bf16[64,192]{1,0:T(8,128)(2,1)S(1)}, bf16[64,192]{1,0:T(8,128)(2,1)}, u32[]{:S(2)}) copy-start(bf16[64,192]{1,0:T(8,128)(2,1)} %constant.34.clone.perm_ref) | copy-start | bytes 73732
  37.7 10.4 %collective-permute-start.5 = (bf16[2,4,32,384]{3,2,1,0:T(8,128)(2,1)S(1)}, bf16[2,4,32,384]{3,2,1,0:T(8,128)(2,1)S(1)}, u32[]{:S(2)}, u32[]{:S(2)}) collective-permute-start(bf16[2,4,32,384]{3,2,1,0:T(8,128)(2,1)S(1)} %get-tuple-element.36.own_ref.grad_ref), channel_id=1, source_target_pairs={{0,112},{16,0},{32,16},{48,32},{64,48},{80,64},{96,80},{112,96},{1... | collective-permute-start | bytes 589832 | tf_op jit(solution)/shard_map/ppermute | solution.py:499
  44.3 5.8 %collective-permute-start.7 = (bf16[2,32,384]{2,1,0:T(8,128)(2,1)S(1)}, bf16[2,32,384]{2,1,0:T(8,128)(2,1)S(1)}, u32[]{:S(2)}, u32[]{:S(2)}) collective-permute-start(bf16[2,32,384]{2,1,0:T(8,128)(2,1)S(1)} %get-tuple-element.38), channel_id=1, source_target_pairs={{1,2},{2,1},{3,4},{4,3},{5,6},{6,5},{7,8},{8,7},{9,10},{10,9},{11,... | collective-permute-start | bytes 147464 | tf_op jit(solution)/shard_map/ppermute | solution.py:500
  44.8 5.5 %collective-permute-start.9 = (bf16[2,32,384]{2,1,0:T(8,128)(2,1)S(1)}, bf16[2,32,384]{2,1,0:T(8,128)(2,1)S(1)}, u32[]{:S(2)}, u32[]{:S(2)}) collective-permute-start(bf16[2,32,384]{2,1,0:T(8,128)(2,1)S(1)} %get-tuple-element.38), channel_id=1, source_target_pairs={{1,114},{2,113},{3,116},{4,115},{5,118},{6,117},{7,120},{8,119},{9... | collective-permute-start | bytes 147464 | tf_op jit(solution)/shard_map/ppermute | solution.py:501
  45.0 5.1 %collective-permute-start.6 = (bf16[2,32,384]{2,1,0:T(8,128)(2,1)S(1)}, bf16[2,32,384]{2,1,0:T(8,128)(2,1)S(1)}, u32[]{:S(2)}, u32[]{:S(2)}) collective-permute-start(bf16[2,32,384]{2,1,0:T(8,128)(2,1)S(1)} %get-tuple-element.37), channel_id=1, source_target_pairs={{0,1},{1,0},{2,3},{3,2},{4,5},{5,4},{6,7},{7,6},{8,9},{9,8},{10,11... | collective-permute-start | bytes 147464 | tf_op jit(solution)/shard_map/ppermute | solution.py:502
  48.1 2.9 %collective-permute-start.8 = (bf16[2,32,384]{2,1,0:T(8,128)(2,1)S(1)}, bf16[2,32,384]{2,1,0:T(8,128)(2,1)S(1)}, u32[]{:S(2)}, u32[]{:S(2)}) collective-permute-start(bf16[2,32,384]{2,1,0:T(8,128)(2,1)S(1)} %edge.5), channel_id=1, source_target_pairs={{0,1},{1,0},{2,3},{3,2},{4,5},{5,4},{6,7},{7,6},{8,9},{9,8},{10,11... | collective-permute-start | bytes 147464 | tf_op jit(solution)/shard_map/ppermute | solution.py:504
  65.2 5.5 %collective-permute-start.10 = (f32[2,32,128]{2,1,0:T(8,128)S(1)}, f32[2,32,128]{2,1,0:T(8,128)S(1)}, u32[]{:S(2)}, u32[]{:S(2)}) collective-permute-start(f32[2,32,128]{2,1,0:T(8,128)S(1)} %get-tuple-element.44), channel_id=1, source_target_pairs={{0,112},{16,0},{32,16},{48,32},{64,48},{80,64},{96,80},{112,96},{1... | collective-permute-start | bytes 98312 | tf_op jit(solution)/shard_map/ppermute | solution.py:561

commit v3 on v2

--- a/solution.py
+++ b/solution.py
@@ -22,6 +22,9 @@
 
 
 WEIGHTS_COVER = pl.CostEstimate(flops=1 << 33, bytes_accessed=1 << 23, transcendentals=0)
+WEIGHTS_WINDOW = pl.CostEstimate(
+    flops=1 << 33, bytes_accessed=1 << 23, transcendentals=300000000
+)
 INPUTS_COVER = pl.CostEstimate(flops=1 << 31, bytes_accessed=1 << 20, transcendentals=0)
 HBM = [pl.BlockSpec(memory_space=pltpu.HBM)]
 
@@ -30,10 +33,6 @@
     return pl.CostEstimate(
         flops=2 * count * kernel.size, bytes_accessed=2 * kernel.size, transcendentals=0
     )
-
-
-def in_hbm(value):
-    return pltpu.with_memory_space_constraint(value, pltpu.HBM)
 
 
 def nt_dot(left, right, **kw):
@@ -67,12 +66,7 @@
 
 
 def moments_kernel(second_ref, first_ref, *refs):
-    vectors, (out_ref, affine_ref), (*lines, sems) = refs[:4], refs[4:6], refs[6:]
-    copies = [
-        pltpu.make_async_copy(*pair, sems.at[k]) for k, pair in enumerate(zip(vectors, lines))
-    ]
-    for copy in copies:
-        copy.start()
+    *vectors, out_ref, affine_ref = refs
     rows = []
     for ref in (second_ref, first_ref):
         frames = ref.shape[0]
@@ -80,8 +74,7 @@
         rows += [jnp.sum(v, axis=(0, 1)).reshape(1, -1) for v in values]
         rows += [jnp.sum(v * v, axis=(0, 1)).reshape(1, -1) for v in values]
     spread(out_ref, jnp.concatenate(rows, axis=0))
-    for k, (copy, line) in enumerate(zip(copies, lines)):
-        copy.wait()
+    for k, line in enumerate(vectors):
         affine_ref[k : k + 1] = line[...].reshape(1, -1)
 
 
@@ -93,15 +86,11 @@
             jax.ShapeDtypeStruct((peers, 4 * frames, channels), jnp.float32),
             jax.ShapeDtypeStruct((len(vectors), channels), jnp.float32),
         ),
-        in_specs=vmem(2) + HBM * len(vectors),
+        in_specs=vmem(2 + len(vectors)),
         out_specs=tuple(vmem(2)),
-        scratch_shapes=[
-            *[pltpu.VMEM(v.shape, jnp.float32) for v in vectors],
-            pltpu.SemaphoreType.DMA((len(vectors),)),
-        ],
         compiler_params=pltpu.CompilerParams(vmem_limit_bytes=16 * MIB),
         name="moments",
-    )(second, first, *map(in_hbm, vectors))
+    )(second, first, *vectors)
 
 
 def fill(ext, at, block, a, b, even):
@@ -157,62 +146,64 @@
         ext,
         frames,
         next_ref[...] * later,
-        ran_ref[...] * later,
+        jnp.zeros_like(rbn_ref) if ran_ref is None else ran_ref[...] * later,
         rbn_ref[...] * (later * side),
         even,
     )
 
 
-def conv_kernel(
-    par_ref,
-    own_ref,
-    next_ref,
-    ra_ref,
-    rb_ref,
-    ran_ref,
-    rbn_ref,
-    w_hbm,
-    u_ref,
-    ext,
-    acc,
-    w_ref,
-    sems,
-):
-    frames, cols, rows, _ = own_ref.shape
-    copies = {
-        a: pltpu.make_async_copy(
-            w_hbm.at[pl.ds(9 * a, 9)], w_ref.at[pl.ds(9 * a, 9)], sems.at[a]
-        )
-        for a in (2, 1, 0)
-    }
-    for copy in copies.values():
-        copy.start()
-    window(par_ref, own_ref, next_ref, ra_ref, rb_ref, ran_ref, rbn_ref, ext)
-    for a, copy in copies.items():
-        copy.wait()
-        part = time_taps(ext, w_ref, (a,), frames, cols)
-        acc[...] = part if a == 2 else acc[...] + part
+def gather_kernel(par_ref, own_ref, next_ref, ra_ref, rb_ref, rbn_ref, ext_ref, corner_ref):
+    even, _, _ = flags(par_ref)
+    cols = own_ref.shape[1]
+    window(par_ref, own_ref, next_ref, ra_ref, rb_ref, None, rbn_ref, ext_ref)
+    corner_ref[...], _ = swapped(even, next_ref[:, cols - 1], next_ref[:, 0])
+
+
+def gather_section(par, own, nxt, ra, rb, rbn):
+    frames, cols, rows, channels = own.shape
+    return pl.pallas_call(
+        gather_kernel,
+        out_shape=(
+            jax.ShapeDtypeStruct((2 * frames, cols + 2, rows, channels), own.dtype),
+            jax.ShapeDtypeStruct((frames, rows, channels), own.dtype),
+        ),
+        in_specs=vmem(6),
+        out_specs=tuple(vmem(2)),
+        compiler_params=pltpu.CompilerParams(vmem_limit_bytes=4 * MIB),
+        cost_estimate=WEIGHTS_WINDOW,
+        name="gather",
+    )(par, own, nxt, ra, rb, rbn)
+
+
+def conv_kernel(par_ref, part_ref, ran_ref, w_ref, u_ref, ext, acc):
+    frames, rows = ran_ref.shape[:2]
+    cols = part_ref.shape[1] - 2
+    even, _, later = flags(par_ref)
+    ext[...] = part_ref[...]
+    right, left = swapped(even, ran_ref[...] * later, jnp.zeros_like(ran_ref))
+    ext[frames:, 0] = part_ref[frames:, 0] + left
+    ext[frames:, cols + 1] = part_ref[frames:, cols + 1] + right
+    acc[...] = time_taps(ext, w_ref, (2, 1, 0), frames, cols)
     u_ref[...] = row_taps(acc, rows)
 
 
-def conv_section(par, grad, halo, kernel):
-    frames, cols, rows, channels = grad.shape
+def conv_section(par, part, ran, kernel):
+    frames, rows, channels = ran.shape
+    cols = part.shape[1] - 2
     count = frames * cols * rows
     return pl.pallas_call(
         conv_kernel,
         out_shape=jax.ShapeDtypeStruct((count, channels), jnp.float32),
-        in_specs=vmem(7) + HBM,
+        in_specs=vmem(4),
         out_specs=vmem(1)[0],
         scratch_shapes=[
-            pltpu.VMEM((2 * frames, cols + 2, rows, channels), jnp.bfloat16),
+            pltpu.VMEM(part.shape, jnp.bfloat16),
             pltpu.VMEM((count, 3 * channels), jnp.float32),
-            pltpu.VMEM(kernel.shape, jnp.bfloat16),
-            pltpu.SemaphoreType.DMA((3,)),
         ],
         compiler_params=pltpu.CompilerParams(vmem_limit_bytes=16 * MIB),
         cost_estimate=matmul_cost(count, kernel),
         name="conv",
-    )(par, grad, *halo, in_hbm(kernel))
+    )(par, part, ran, kernel)
 
 
 def norm_stats(cells, base, frames, mom_ref):
@@ -487,22 +478,26 @@
     )(got, jnp.asarray(place, jnp.bfloat16), jnp.asarray(perm, jnp.bfloat16))
 
 
-def exchange(par, value, send_a, send_b):
-    tms = lax.axis_size("tm")
-    tiles = lax.axis_size(TILE)
+def routes():
+    tms, tiles = lax.axis_size("tm"), lax.axis_size(TILE)
     back = ring(tms)
-    swap = [(0, 1), (1, 0)]
     hops = []
     for k in range(1, tiles, 2):
         hops += [(k, (k + 1) % tiles), ((k + 1) % tiles, k)]
     diagonal = [(t * tiles + s, u * tiles + d) for t, u in back for s, d in hops]
+    return back, hops, diagonal
+
+
+SWAP = [(0, 1), (1, 0)]
+
+
+def exchange(value, send_a, send_b):
+    back, hops, diagonal = routes()
     nxt = lax.ppermute(value, "tm", back)
     rb = lax.ppermute(send_b, TILE, hops)
     rbn = lax.ppermute(send_b, TM_TILE, diagonal)
-    ra = lax.ppermute(send_a, "tile_2", swap)
-    (corner,) = edge_section(par, nxt, 1, None)
-    ran = lax.ppermute(corner, "tile_2", swap)
-    return nxt, ra, rb, ran, rbn
+    ra = lax.ppermute(send_a, "tile_2", SWAP)
+    return nxt, ra, rb, rbn
 
 
 def ring(count):
@@ -546,12 +541,16 @@
     vectors = (second_gain, second_shift, first_gain, first_shift)
     mine, affine = moments(second_input, first_input, vectors, peers)
     mom = everyone(mine)
-    halo = exchange(par, grad, *edge_section(par, grad, 2, INPUTS_COVER))
+    nxt, ra, rb, rbn = exchange(grad, *edge_section(par, grad, 2, INPUTS_COVER))
+    part, corner = gather_section(par, grad, nxt, ra, rb, rbn)
+    ran = lax.ppermute(corner, "tile_2", SWAP)
     second, first = turn(second_input), turn(first_input)
-    upstream = conv_section(par, grad, halo, second_kernel)
+    upstream = conv_section(par, part, ran, second_kernel)
     q, sums, stats = norm_section(upstream, second, mom, affine, cells, peers)
     grad, send_a, send_b = dx_section(par, grad, q, second, stats, everyone(sums), cells)
-    nxt, ra, rb, ran, rbn = exchange(par, grad, send_a, send_b)
+    nxt, ra, rb, rbn = exchange(grad, send_a, send_b)
+    (corner,) = edge_section(par, nxt, 1, None)
+    ran = lax.ppermute(corner, "tile_2", SWAP)
     q, sums, stats = conv_norm_section(
         par, grad, (nxt, ra, rb, ran, rbn), first_kernel, first, mom, affine, cells,
         2 * frames, peers,

time: 81.7 us -> 83.5 us (1.022)
  local copies, waits for them, and re-layouts: 1.14 us -> 4.39 us
  Pallas kernels: 12.1 us -> 9.18 us
  waiting for transfers between devices: 3.63 us -> 4.59 us
    ppermute x4, starting transfers between devices: 8.61 us -> 12.6 us  [the longest x2 6.89 us: shards(): ran = lax.ppermute(corner, 'tile_2', SWAP)]
    unnamed x14 -> x24, local copies, waits for them, and re-layouts: 0.03 us -> 3.32 us
    ppermute x2, starting transfers between devices: 12.7 us -> 9.93 us  [exchange(): nxt = lax.ppermute(value, 'tm', back)]
    pallas_call x1, Pallas kernels: 5.18 us -> 2.61 us  [conv_section(): pl.pallas_call(conv_kernel, out_shape=jax.ShapeDtypeStruct((count, channe...]
    ppermute x2, waiting for transfers between devices: 0.15 us -> 1.87 us  [exchange(): rbn = lax.ppermute(send_b, TM_TILE, diagonal)]
    all_to_all x1, starting transfers between devices: 5.61 us -> 4.08 us  [everyone(): return lax.all_to_all(rows, TILE, 0, 0)]
  transfers between devices with their start and end apart: 12 -> 12, of which waited for: 5 -> 6; matrix products, arithmetic and copies ran while one was open for 0% -> 0% of each run, Pallas kernels for 8% -> 4%
where the time goes in v3:
time: 83.5 us; the launch traced here: 83.2 us
  starting transfers between devices  33.5 us (40%)
  blocking collectives  31.3 us (37%)
  Pallas kernels  9.18 us (11%)
  waiting for transfers between devices  4.59 us (5%)
  local copies, waits for them, and re-layouts  4.39 us (5%)
    all_to_all x3, blocking collectives, everyone(): return lax.all_to_all(rows, TILE, 0, 0)  31.3 us
    ppermute x2, starting transfers between devices, exchange(): nxt = lax.ppermute(value, 'tm', back)  9.93 us
    ppermute x2, starting transfers between devices, shards(): ran = lax.ppermute(corner, 'tile_2', SWAP)  6.89 us
    ppermute x2, starting transfers between devices, exchange(): ra = lax.ppermute(send_a, 'tile_2', SWAP)  5.7 us
    ppermute x1, starting transfers between devices, shards(): own = own + jnp.where(later, lax.ppermute(prev, 'tm', ring(tms)), 0.0)  4.43 us
    all_to_all x1, starting transfers between devices, everyone(): return lax.all_to_all(rows, TILE, 0, 0)  4.08 us
    unnamed x24, local copies, waits for them, and re-layouts  3.32 us
    pallas_call x1, Pallas kernels, conv_norm_section(): pl.pallas_call(functools.partial(conv_norm_kernel, cells, base), out_shap...  2.89 us
  transfers between devices with their start and end apart: 12, of which 6 were waited for; matrix products, arithmetic and copies ran while one was open for 0% of the time, Pallas kernels for 4%

profile of v3, /device:TPU:1, one launch (start us, length us, event | category | flops | bytes accessed | tf_op | source)
XLA Modules:
  0.0 83.2 jit_solution(8978620889891118063)
XLA Ops:
  0.2 1.0 %copy.21 = bf16[2,32,4,384]{3,1,2,0:T(8,128)(2,1)S(1)} copy(bf16[2,32,4,384]{3,2,1,0:T(4,128)(2,1)} %param.14) | data formatting | bytes 393216 | tf_op jit(solution)/shard_map/optimization_barrier | solution.py:533
  1.1 6.0 %collective-permute-start = (bf16[2,4,32,384]{3,2,1,0:T(8,128)(2,1)S(1)}, bf16[2,4,32,384]{3,2,1,0:T(8,128)(2,1)S(1)}, u32[]{:S(2)}, u32[]{:S(2)}) collective-permute-start(bf16[2,4,32,384]{3,2,1,0:T(8,128)(2,1)S(1)} %bitcast.19), channel_id=1, source_target_pairs={{0,112},{16,0},{32,16},{48,32},{64,48},{80,64},{96,80},{112,96},{1... | collective-permute-start | bytes 589832 | tf_op jit(solution)/shard_map/ppermute | solution.py:496
  7.1 1.3 %collective-permute-start.2 = (bf16[2,32,384]{2,1,0:T(8,128)(2,1)S(1)}, bf16[2,32,384]{2,1,0:T(8,128)(2,1)S(1)}, u32[]{:S(2)}, u32[]{:S(2)}) collective-permute-start(bf16[2,32,384]{2,1,0:T(8,128)(2,1)S(1)} %get-tuple-element.30), channel_id=1, source_target_pairs={{1,2},{2,1},{3,4},{4,3},{5,6},{6,5},{7,8},{8,7},{9,10},{10,9},{11,... | collective-permute-start | bytes 147464 | tf_op jit(solution)/shard_map/ppermute | solution.py:497
  8.4 0.5 collective-permute-start.3
  8.9 3.0 %collective-permute-start.1 = (bf16[2,32,384]{2,1,0:T(8,128)(2,1)S(1)}, bf16[2,32,384]{2,1,0:T(8,128)(2,1)S(1)}, u32[]{:S(2)}, u32[]{:S(2)}) collective-permute-start(bf16[2,32,384]{2,1,0:T(8,128)(2,1)S(1)} %get-tuple-element.29), channel_id=1, source_target_pairs={{0,1},{1,0},{2,3},{3,2},{4,5},{5,4},{6,7},{7,6},{8,9},{9,8},{10,11... | collective-permute-start | bytes 147464 | tf_op jit(solution)/shard_map/ppermute | solution.py:499
  11.9 1.6 %collective-permute-done.3.rbn_ref = bf16[2,32,384]{2,1,0:T(8,128)(2,1)S(1)} collective-permute-done((bf16[2,32,384]{2,1,0:T(8,128)(2,1)S(1)}, bf16[2,32,384]{2,1,0:T(8,128)(2,1)S(1)}, u32[]{:S(2)}, u32[]{:S(2)}) %collective-permute-start.3) | collective-permute-done | bytes 49184 | tf_op jit(solution)/shard_map/ppermute | solution.py:498
  13.7 4.9 %collective-permute-start.4 = (bf16[2,32,384]{2,1,0:T(8,128)(2,1)S(1)}, bf16[2,32,384]{2,1,0:T(8,128)(2,1)S(1)}, u32[]{:S(2)}, u32[]{:S(2)}) collective-permute-start(bf16[2,32,384]{2,1,0:T(8,128)(2,1)S(1)} %get-tuple-element.32), channel_id=1, source_target_pairs={{0,1},{1,0},{2,3},{3,2},{4,5},{5,4},{6,7},{7,6},{8,9},{9,8},{10,11... | collective-permute-start | bytes 147464 | tf_op jit(solution)/shard_map/ppermute | solution.py:546
  18.6 1.0 %moments.1 = (f32[16,8,384]{2,1,0:T(8,128)}, f32[4,384]{1,0:T(4,128)S(1)}) custom-call(bf16[2,32,4,384]{3,2,1,0:T(4,128)(2,1)S(1)} %copy-done.1, bf16[2,32,4,384]{3,2,1,0:T(4,128)(2,1)S(1)} %copy-done.2, f32[384]{0:T(512)S(1)} %copy-done.6, f32[384]{0:T(512)S(1)} %copy-done.7, f32[384]{0:T(512)S(1)} %copy-done.8, f32[384]{0:T(512)S(1)} %copy-done.9), custom_call_target="tpu_custom_call" | custom-call | tf_op jit(solution)/shard_map/moments/pallas_call | solution.py:83
  19.6 4.1 %all-to-all-start = ((f32[16,8,384]{2,1,0:T(8,128)}), f32[16,8,384]{2,1,0:T(8,128)S(1)}, u32[]{:S(2)}, u32[]{:S(2)}) async-start(f32[16,8,384]{2,1,0:T(8,128)} %get-tuple-element.35), calls=%async_computation | async-start | bytes 393216 | tf_op jit(solution)/shard_map/all_to_all | solution.py:508
  23.7 3.3 %copy-done = bf16[27,384,384]{2,1,0:T(8,128)(2,1)S(1)} copy-done((bf16[27,384,384]{2,1,0:T(8,128)(2,1)S(1)}, bf16[27,384,384]{2,1,0:T(8,128)(2,1)}, u32[]{:S(2)}) %copy-start) | copy-done | bytes 7962648
  27.0 2.6 %conv.1.u_ref = f32[256,384]{1,0:T(8,128)S(1)} custom-call(bf16[3,384]{1,0:T(4,128)(2,1)S(1)} %broadcast_in_dim.10.par_ref, bf16[4,6,32,384]{3,2,1,0:T(8,128)(2,1)S(1)} %get-tuple-element.31.part_ref, bf16[2,32,384]{2,1,0:T(8,128)(2,1)S(1)} %collective-permute-done.4.ran_ref, bf16[27,384,384]{2,1,0:T(8,128)(2,1)S(1)} %copy-done), custom_call_target="tpu_custom_call" | custom-call | flops 2038431744 | bytes 7962624 | tf_op jit(solution)/shard_map/conv/pallas_call | solution.py:194
  29.6 0.8 all-to-all-done.mom_ref
  30.8 11.0 %all_to_all.20.sums_ref = f32[16,4,384]{2,1,0:T(4,128)S(1)} all-to-all(f32[16,4,384]{2,1,0:T(4,128)S(1)} %get-tuple-element.39), channel_id=1, replica_groups=mesh['tm'=8,'tile_0'=4,'tile_1'=2,'tile_2'=2] {'tile_0','tile_1','tile_2'}, dimensions={0} | all-to-all | bytes 196608 | tf_op jit(solution)/shard_map/all_to_all | solution.py:508
  42.2 3.9 %collective-permute-start.5 = (bf16[2,4,32,384]{3,2,1,0:T(8,128)(2,1)S(1)}, bf16[2,4,32,384]{3,2,1,0:T(8,128)(2,1)S(1)}, u32[]{:S(2)}, u32[]{:S(2)}) collective-permute-start(bf16[2,4,32,384]{3,2,1,0:T(8,128)(2,1)S(1)} %get-tuple-element.40.own_ref.grad_ref), channel_id=1, source_target_pairs={{0,112},{16,0},{32,16},{48,32},{64,48},{80,64},{96,80},{112,96},{1... | collective-permute-start | bytes 589832 | tf_op jit(solution)/shard_map/ppermute | solution.py:496
  46.7 2.7 %collective-permute-start.6 = (bf16[2,32,384]{2,1,0:T(8,128)(2,1)S(1)}, bf16[2,32,384]{2,1,0:T(8,128)(2,1)S(1)}, u32[]{:S(2)}, u32[]{:S(2)}) collective-permute-start(bf16[2,32,384]{2,1,0:T(8,128)(2,1)S(1)} %get-tuple-element.41), channel_id=1, source_target_pairs={{0,1},{1,0},{2,3},{3,2},{4,5},{5,4},{6,7},{7,6},{8,9},{9,8},{10,11... | collective-permute-start | bytes 147464 | tf_op jit(solution)/shard_map/ppermute | solution.py:499
  49.8 2.0 %collective-permute-start.8 = (bf16[2,32,384]{2,1,0:T(8,128)(2,1)S(1)}, bf16[2,32,384]{2,1,0:T(8,128)(2,1)S(1)}, u32[]{:S(2)}, u32[]{:S(2)}) collective-permute-start(bf16[2,32,384]{2,1,0:T(8,128)(2,1)S(1)} %edge.3), channel_id=1, source_target_pairs={{0,1},{1,0},{2,3},{3,2},{4,5},{5,4},{6,7},{7,6},{8,9},{9,8},{10,11... | collective-permute-start | bytes 147464 | tf_op jit(solution)/shard_map/ppermute | solution.py:553
  52.2 0.5 collective-permute-done.8.ran_ref
  52.7 2.9 %convnorm.1 = (f32[2,4,32,384]{3,2,1,0:T(8,128)S(1)}, f32[16,4,384]{2,1,0:T(4,128)S(1)}, f32[4,384]{1,0:T(4,128)S(1)}) custom-call(bf16[3,384]{1,0:T(4,128)(2,1)S(1)} %broadcast_in_dim.10.par_ref, bf16[2,4,32,384]{3,2,1,0:T(8,128)(2,1)S(1)} %get-tuple-element.40.own_ref.grad_ref, bf16[2,4,32,384]{3,2,1,0:T(8,128)(2,1)S(1)} %collective-permute-done.5.block_ref.next_ref, ...), custom_call_target="tpu_custom_call" | custom-call | flops 2038431744 | bytes 7962624 | tf_op jit(solution)/shard_map/convnorm/pallas_call | solution.py:337
  55.6 10.6 %all_to_all.21.sums_ref = f32[16,4,384]{2,1,0:T(4,128)S(1)} all-to-all(f32[16,4,384]{2,1,0:T(4,128)S(1)} %get-tuple-element.45), channel_id=1, replica_groups=mesh['tm'=8,'tile_0'=4,'tile_1'=2,'tile_2'=2] {'tile_0','tile_1','tile_2'}, dimensions={0} | all-to-all | bytes 196608 | tf_op jit(solution)/shard_map/all_to_all | solution.py:508
  66.3 0.7 latent.1
  67.0 4.4 %collective-permute-start.10 = (f32[2,32,128]{2,1,0:T(8,128)S(1)}, f32[2,32,128]{2,1,0:T(8,128)S(1)}, u32[]{:S(2)}, u32[]{:S(2)}) collective-permute-start(f32[2,32,128]{2,1,0:T(8,128)S(1)} %get-tuple-element.48), channel_id=1, source_target_pairs={{0,112},{16,0},{32,16},{48,32},{64,48},{80,64},{96,80},{112,96},{1... | collective-permute-start | bytes 98312 | tf_op jit(solution)/shard_map/ppermute | solution.py:560
  71.4 1.0 %collective-permute-done.10 = f32[2,32,128]{2,1,0:T(8,128)S(1)} collective-permute-done((f32[2,32,128]{2,1,0:T(8,128)S(1)}, f32[2,32,128]{2,1,0:T(8,128)S(1)}, u32[]{:S(2)}, u32[]{:S(2)}) %collective-permute-start.10) | collective-permute-done | bytes 32800 | tf_op jit(solution)/shard_map/ppermute | solution.py:560
  72.4 9.7 %all_to_all.22.got_ref = f32[16,4,128]{2,1,0:T(4,128)S(1)} all-to-all(f32[16,4,128]{2,1,0:T(4,128)S(1)} %bitcast.23), channel_id=1, replica_groups=mesh['tm'=8,'tile_0'=4,'tile_1'=2,'tile_2'=2] {'tile_0','tile_1','tile_2'}, dimensions={0} | all-to-all | bytes 65536 | tf_op jit(solution)/shard_map/all_to_all | solution.py:508
  82.1 1.1 %assemble.1 = f32[64,64]{1,0:T(8,128)} custom-call(f32[16,4,128]{2,1,0:T(4,128)S(1)} %all_to_all.22.got_ref, bf16[96,768]{1,0:T(8,128)(2,1)S(1)} %copy-done.4, bf16[64,192]{1,0:T(8,128)(2,1)S(1)} %copy-done.5), custom_call_target="tpu_custom_call" | custom-call | tf_op jit(solution)/shard_map/assemble/pallas_call | solution.py:471
  (44 shorter events, 2.5 us)
Async XLA Ops:
  1.1 12.4 %collective-permute-start = (bf16[2,4,32,384]{3,2,1,0:T(8,128)(2,1)S(1)}, bf16[2,4,32,384]{3,2,1,0:T(8,128)(2,1)S(1)}, u32[]{:S(2)}, u32[]{:S(2)}) collective-permute-start(bf16[2,4,32,384]{3,2,1,0:T(8,128)(2,1)S(1)} %bitcast.19), channel_id=1, source_target_pairs={{0,112},{16,0},{32,16},{48,32},{64,48},{80,64},{96,80},{112,96},{1... | collective-permute-start | bytes 589832 | tf_op jit(solution)/shard_map/ppermute | solution.py:496
  7.1 4.8 %collective-permute-start.2 = (bf16[2,32,384]{2,1,0:T(8,128)(2,1)S(1)}, bf16[2,32,384]{2,1,0:T(8,128)(2,1)S(1)}, u32[]{:S(2)}, u32[]{:S(2)}) collective-permute-start(bf16[2,32,384]{2,1,0:T(8,128)(2,1)S(1)} %get-tuple-element.30), channel_id=1, source_target_pairs={{1,2},{2,1},{3,4},{4,3},{5,6},{6,5},{7,8},{8,7},{9,10},{10,9},{11,... | collective-permute-start | bytes 147464 | tf_op jit(solution)/shard_map/ppermute | solution.py:497
  8.4 5.1 %collective-permute-start.3 = (bf16[2,32,384]{2,1,0:T(8,128)(2,1)S(1)}, bf16[2,32,384]{2,1,0:T(8,128)(2,1)S(1)}, u32[]{:S(2)}, u32[]{:S(2)}) collective-permute-start(bf16[2,32,384]{2,1,0:T(8,128)(2,1)S(1)} %get-tuple-element.30), channel_id=1, source_target_pairs={{1,114},{2,113},{3,116},{4,115},{5,118},{6,117},{7,120},{8,119},{9... | collective-permute-start | bytes 147464 | tf_op jit(solution)/shard_map/ppermute | solution.py:498
  8.9 4.6 %collective-permute-start.1 = (bf16[2,32,384]{2,1,0:T(8,128)(2,1)S(1)}, bf16[2,32,384]{2,1,0:T(8,128)(2,1)S(1)}, u32[]{:S(2)}, u32[]{:S(2)}) collective-permute-start(bf16[2,32,384]{2,1,0:T(8,128)(2,1)S(1)} %get-tuple-element.29), channel_id=1, source_target_pairs={{0,1},{1,0},{2,3},{3,2},{4,5},{5,4},{6,7},{7,6},{8,9},{9,8},{10,11... | collective-permute-start | bytes 147464 | tf_op jit(solution)/shard_map/ppermute | solution.py:499
  13.5 5.0 %copy-start.1 = (bf16[2,32,4,384]{3,2,1,0:T(4,128)(2,1)S(1)}, bf16[2,32,4,384]{3,2,1,0:T(4,128)(2,1)}, u32[]{:S(2)}) copy-start(bf16[2,32,4,384]{3,2,1,0:T(4,128)(2,1)} %second_ref) | copy-start | bytes 589828
  13.5 5.0 %copy-start.2 = (bf16[2,32,4,384]{3,2,1,0:T(4,128)(2,1)S(1)}, bf16[2,32,4,384]{3,2,1,0:T(4,128)(2,1)}, u32[]{:S(2)}) copy-start(bf16[2,32,4,384]{3,2,1,0:T(4,128)(2,1)} %first_ref) | copy-start | bytes 589828
  13.6 5.0 %copy-start.6 = (f32[384]{0:T(512)S(1)}, f32[384]{0:T(512)}, u32[]{:S(2)}) copy-start(f32[384]{0:T(512)} %refs_0_.1) | copy-start | bytes 4612
  13.6 5.0 %copy-start.7 = (f32[384]{0:T(512)S(1)}, f32[384]{0:T(512)}, u32[]{:S(2)}) copy-start(f32[384]{0:T(512)} %refs_1_.1) | copy-start | bytes 4612
  13.6 5.0 %copy-start.8 = (f32[384]{0:T(512)S(1)}, f32[384]{0:T(512)}, u32[]{:S(2)}) copy-start(f32[384]{0:T(512)} %refs_2_.1) | copy-start | bytes 4612
  13.6 5.0 %copy-start.9 = (f32[384]{0:T(512)S(1)}, f32[384]{0:T(512)}, u32[]{:S(2)}) copy-start(f32[384]{0:T(512)} %refs_3_.1) | copy-start | bytes 4612
  13.7 10.0 %collective-permute-start.4 = (bf16[2,32,384]{2,1,0:T(8,128)(2,1)S(1)}, bf16[2,32,384]{2,1,0:T(8,128)(2,1)S(1)}, u32[]{:S(2)}, u32[]{:S(2)}) collective-permute-start(bf16[2,32,384]{2,1,0:T(8,128)(2,1)S(1)} %get-tuple-element.32), channel_id=1, source_target_pairs={{0,1},{1,0},{2,3},{3,2},{4,5},{5,4},{6,7},{7,6},{8,9},{9,8},{10,11... | collective-permute-start | bytes 147464 | tf_op jit(solution)/shard_map/ppermute | solution.py:546
  19.6 10.8 %all-to-all-start = ((f32[16,8,384]{2,1,0:T(8,128)}), f32[16,8,384]{2,1,0:T(8,128)S(1)}, u32[]{:S(2)}, u32[]{:S(2)}) async-start(f32[16,8,384]{2,1,0:T(8,128)} %get-tuple-element.35), calls=%async_computation | async-start | bytes 393216 | tf_op jit(solution)/shard_map/all_to_all | solution.py:508
  23.7 3.3 %copy-start = (bf16[27,384,384]{2,1,0:T(8,128)(2,1)S(1)}, bf16[27,384,384]{2,1,0:T(8,128)(2,1)}, u32[]{:S(2)}) copy-start(bf16[27,384,384]{2,1,0:T(8,128)(2,1)} %w_ref.2) | copy-start | bytes 23887876
  30.4 22.4 %slice-start = ((s8[7962624]{0:T(1024)(128)(4,1)}), s8[4194304]{0:T(1024)(128)(4,1)S(1)}, s32[]{:S(2)}) async-start(s8[7962624]{0:T(1024)(128)(4,1)} %bitcast.13), calls=%async_computation.4 | async-start | bytes 8388608
  41.8 11.0 %slice-start.1 = ((s8[7962624]{0:T(1024)(128)(4,1)}), s8[3768320]{0:T(1024)(128)(4,1)S(1)}, s32[]{:S(2)}) async-start(s8[7962624]{0:T(1024)(128)(4,1)} %bitcast.13), calls=%async_computation.5 | async-start | bytes 7536640
  42.1 24.1 %copy-start.3 = (bf16[27,16,384]{2,1,0:T(8,128)(2,1)S(1)}, bf16[27,16,384]{2,1,0:T(8,128)(2,1)}, u32[]{:S(2)}) copy-start(bf16[27,16,384]{2,1,0:T(8,128)(2,1)} %k_ref.1) | copy-start | bytes 995332
  42.1 40.0 %copy-start.4 = (bf16[96,768]{1,0:T(8,128)(2,1)S(1)}, bf16[96,768]{1,0:T(8,128)(2,1)}, u32[]{:S(2)}) copy-start(bf16[96,768]{1,0:T(8,128)(2,1)} %constant.33.clone.e_ref) | copy-start | bytes 442372
  42.1 40.0 %copy-start.5 = (bf16[64,192]{1,0:T(8,128)(2,1)S(1)}, bf16[64,192]{1,0:T(8,128)(2,1)}, u32[]{:S(2)}) copy-start(bf16[64,192]{1,0:T(8,128)(2,1)} %constant.34.clone.perm_ref) | copy-start | bytes 73732
  42.2 7.6 %collective-permute-start.5 = (bf16[2,4,32,384]{3,2,1,0:T(8,128)(2,1)S(1)}, bf16[2,4,32,384]{3,2,1,0:T(8,128)(2,1)S(1)}, u32[]{:S(2)}, u32[]{:S(2)}) collective-permute-start(bf16[2,4,32,384]{3,2,1,0:T(8,128)(2,1)S(1)} %get-tuple-element.40.own_ref.grad_ref), channel_id=1, source_target_pairs={{0,112},{16,0},{32,16},{48,32},{64,48},{80,64},{96,80},{112,96},{1... | collective-permute-start | bytes 589832 | tf_op jit(solution)/shard_map/ppermute | solution.py:496
  46.1 5.8 %collective-permute-start.7 = (bf16[2,32,384]{2,1,0:T(8,128)(2,1)S(1)}, bf16[2,32,384]{2,1,0:T(8,128)(2,1)S(1)}, u32[]{:S(2)}, u32[]{:S(2)}) collective-permute-start(bf16[2,32,384]{2,1,0:T(8,128)(2,1)S(1)} %get-tuple-element.42), channel_id=1, source_target_pairs={{1,2},{2,1},{3,4},{4,3},{5,6},{6,5},{7,8},{8,7},{9,10},{10,9},{11,... | collective-permute-start | bytes 147464 | tf_op jit(solution)/shard_map/ppermute | solution.py:497
  46.5 5.6 %collective-permute-start.9 = (bf16[2,32,384]{2,1,0:T(8,128)(2,1)S(1)}, bf16[2,32,384]{2,1,0:T(8,128)(2,1)S(1)}, u32[]{:S(2)}, u32[]{:S(2)}) collective-permute-start(bf16[2,32,384]{2,1,0:T(8,128)(2,1)S(1)} %get-tuple-element.42), channel_id=1, source_target_pairs={{1,114},{2,113},{3,116},{4,115},{5,118},{6,117},{7,120},{8,119},{9... | collective-permute-start | bytes 147464 | tf_op jit(solution)/shard_map/ppermute | solution.py:498
  46.7 5.1 %collective-permute-start.6 = (bf16[2,32,384]{2,1,0:T(8,128)(2,1)S(1)}, bf16[2,32,384]{2,1,0:T(8,128)(2,1)S(1)}, u32[]{:S(2)}, u32[]{:S(2)}) collective-permute-start(bf16[2,32,384]{2,1,0:T(8,128)(2,1)S(1)} %get-tuple-element.41), channel_id=1, source_target_pairs={{0,1},{1,0},{2,3},{3,2},{4,5},{5,4},{6,7},{7,6},{8,9},{9,8},{10,11... | collective-permute-start | bytes 147464 | tf_op jit(solution)/shard_map/ppermute | solution.py:499
  49.8 2.9 %collective-permute-start.8 = (bf16[2,32,384]{2,1,0:T(8,128)(2,1)S(1)}, bf16[2,32,384]{2,1,0:T(8,128)(2,1)S(1)}, u32[]{:S(2)}, u32[]{:S(2)}) collective-permute-start(bf16[2,32,384]{2,1,0:T(8,128)(2,1)S(1)} %edge.3), channel_id=1, source_target_pairs={{0,1},{1,0},{2,3},{3,2},{4,5},{5,4},{6,7},{7,6},{8,9},{9,8},{10,11... | collective-permute-start | bytes 147464 | tf_op jit(solution)/shard_map/ppermute | solution.py:553
  67.0 5.5 %collective-permute-start.10 = (f32[2,32,128]{2,1,0:T(8,128)S(1)}, f32[2,32,128]{2,1,0:T(8,128)S(1)}, u32[]{:S(2)}, u32[]{:S(2)}) collective-permute-start(f32[2,32,128]{2,1,0:T(8,128)S(1)} %get-tuple-element.48), channel_id=1, source_target_pairs={{0,112},{16,0},{32,16},{48,32},{64,48},{80,64},{96,80},{112,96},{1... | collective-permute-start | bytes 98312 | tf_op jit(solution)/shard_map/ppermute | solution.py:560

commit v4 on v3

--- a/solution.py
+++ b/solution.py
@@ -22,9 +22,6 @@
 
 
 WEIGHTS_COVER = pl.CostEstimate(flops=1 << 33, bytes_accessed=1 << 23, transcendentals=0)
-WEIGHTS_WINDOW = pl.CostEstimate(
-    flops=1 << 33, bytes_accessed=1 << 23, transcendentals=300000000
-)
 INPUTS_COVER = pl.CostEstimate(flops=1 << 31, bytes_accessed=1 << 20, transcendentals=0)
 HBM = [pl.BlockSpec(memory_space=pltpu.HBM)]
 
@@ -33,6 +30,10 @@
     return pl.CostEstimate(
         flops=2 * count * kernel.size, bytes_accessed=2 * kernel.size, transcendentals=0
     )
+
+
+def in_hbm(value):
+    return pltpu.with_memory_space_constraint(value, pltpu.HBM)
 
 
 def nt_dot(left, right, **kw):
@@ -101,7 +102,7 @@
     ext[at : at + frames, cols + 1] = right
 
 
-def time_taps(ext, w_ref, taps, frames, cols):
+def time_taps(ext, w_ref, taps, frames, cols, row_taps=(0, 1, 2)):
     _, channels = ext.shape[2:]
     pairs = [(a, c) for a in taps for c in range(3)]
     left = jnp.concatenate(
@@ -114,7 +115,7 @@
     right = jnp.concatenate(
         [
             jnp.concatenate([w_ref[9 * a + 3 * b + c] for a, c in pairs], axis=1)
-            for b in range(3)
+            for b in row_taps
         ],
         axis=0,
     )
@@ -170,20 +171,29 @@
         in_specs=vmem(6),
         out_specs=tuple(vmem(2)),
         compiler_params=pltpu.CompilerParams(vmem_limit_bytes=4 * MIB),
-        cost_estimate=WEIGHTS_WINDOW,
         name="gather",
     )(par, own, nxt, ra, rb, rbn)
 
 
-def conv_kernel(par_ref, part_ref, ran_ref, w_ref, u_ref, ext, acc):
-    frames, rows = ran_ref.shape[:2]
+def conv_kernel(par_ref, part_ref, ran_ref, w_hbm, u_ref, ext, acc, w_ref, sems):
+    frames, rows, channels = ran_ref.shape
     cols = part_ref.shape[1] - 2
+    pieces = [(2, (0, 1, 2)), (1, (0, 1, 2)), (0, (0,)), (0, (1,)), (0, (2,))]
+    copies = []
+    for k, (a, bs) in enumerate(pieces):
+        span = pl.ds(9 * a + 3 * bs[0], 3 * len(bs))
+        copies.append(pltpu.make_async_copy(w_hbm.at[span], w_ref.at[span], sems.at[k]))
+        copies[-1].start()
     even, _, later = flags(par_ref)
     ext[...] = part_ref[...]
     right, left = swapped(even, ran_ref[...] * later, jnp.zeros_like(ran_ref))
     ext[frames:, 0] = part_ref[frames:, 0] + left
     ext[frames:, cols + 1] = part_ref[frames:, cols + 1] + right
-    acc[...] = time_taps(ext, w_ref, (2, 1, 0), frames, cols)
+    for copy, (a, bs) in zip(copies, pieces):
+        copy.wait()
+        lanes = slice(bs[0] * channels, (bs[-1] + 1) * channels)
+        part = time_taps(ext, w_ref, (a,), frames, cols, bs)
+        acc[:, lanes] = part if a == 2 else acc[:, lanes] + part
     u_ref[...] = row_taps(acc, rows)
 
 
@@ -194,27 +204,27 @@
     return pl.pallas_call(
         conv_kernel,
         out_shape=jax.ShapeDtypeStruct((count, channels), jnp.float32),
-        in_specs=vmem(4),
+        in_specs=vmem(3) + HBM,
         out_specs=vmem(1)[0],
         scratch_shapes=[
             pltpu.VMEM(part.shape, jnp.bfloat16),
             pltpu.VMEM((count, 3 * channels), jnp.float32),
+            pltpu.VMEM(kernel.shape, jnp.bfloat16),
+            pltpu.SemaphoreType.DMA((5,)),
         ],
         compiler_params=pltpu.CompilerParams(vmem_limit_bytes=16 * MIB),
         cost_estimate=matmul_cost(count, kernel),
         name="conv",
-    )(par, part, ran, kernel)
-
-
-def norm_stats(cells, base, frames, mom_ref):
+    )(par, part, ran, in_hbm(kernel))
+
+
+def norm_stats(cells, frames, mom_ref):
     totals = group_sum(jnp.sum(mom_ref[...], axis=0)) * (1.0 / cells)
-    means, scales = [], []
-    for f in range(frames):
-        mean = totals[base + f : base + f + 1]
-        var = totals[base + frames + f : base + frames + f + 1] - mean * mean
-        means.append(mean)
-        scales.append(lax.rsqrt(var + EPSILON))
-    return means, scales
+    rows = []
+    for base in (0, 2 * frames):
+        mean = totals[base : base + frames]
+        rows += [mean, lax.rsqrt(totals[base + frames : base + 2 * frames] - mean * mean + EPSILON)]
+    return jnp.concatenate(rows, axis=0)
 
 
 def through(upstream, normed, gain, shift):
@@ -223,20 +233,19 @@
     return upstream * sig * (1.0 + pre * (1.0 - sig)) * gain
 
 
-def finish(cells, base, upstream, x_ref, mom_ref, affine_ref, at, q_ref, sums_ref, stats_ref):
+def finish(stats, upstream, x_ref, affine_ref, at, q_ref, sums_ref):
     frames, cols, rows, channels = x_ref.shape
-    means, scales = norm_stats(cells, base, frames, mom_ref)
     gain, shift = affine_ref[at : at + 1], affine_ref[at + 1 : at + 2]
     half = cols * rows
     sums, crosses = [], []
     for f in range(frames):
-        normed = (x_ref[f].astype(jnp.float32).reshape(half, channels) - means[f]) * scales[f]
+        mean, scale = stats[f : f + 1], stats[frames + f : frames + f + 1]
+        normed = (x_ref[f].astype(jnp.float32).reshape(half, channels) - mean) * scale
         q = through(upstream[f * half : (f + 1) * half], normed, gain, shift)
         q_ref[f] = q.reshape(cols, rows, channels)
         sums.append(jnp.sum(q, axis=0, keepdims=True))
         crosses.append(jnp.sum(q * normed, axis=0, keepdims=True))
     spread(sums_ref, jnp.concatenate(sums + crosses, axis=0))
-    stats_ref[...] = jnp.concatenate(means + scales, axis=0)
 
 
 def finish_shapes(stored, peers):
@@ -244,32 +253,36 @@
     return (
         jax.ShapeDtypeStruct(stored.shape, jnp.float32),
         jax.ShapeDtypeStruct((peers, 2 * frames, channels), jnp.float32),
-        jax.ShapeDtypeStruct((2 * frames, channels), jnp.float32),
     )
 
 
 def norm_kernel(cells, u_ref, x_ref, mom_ref, affine_ref, q_ref, sums_ref, stats_ref):
-    finish(cells, 0, u_ref, x_ref, mom_ref, affine_ref, 0, q_ref, sums_ref, stats_ref)
+    frames = x_ref.shape[0]
+    stats = norm_stats(cells, frames, mom_ref)
+    finish(stats[: 2 * frames], u_ref, x_ref, affine_ref, 0, q_ref, sums_ref)
+    stats_ref[...] = stats
 
 
 def norm_section(upstream, stored, mom, affine, cells, peers):
+    frames, _, _, channels = stored.shape
+    stats = jax.ShapeDtypeStruct((4 * frames, channels), jnp.float32)
     return pl.pallas_call(
         functools.partial(norm_kernel, cells),
-        out_shape=finish_shapes(stored, peers),
+        out_shape=(*finish_shapes(stored, peers), stats),
         in_specs=vmem(4),
         out_specs=tuple(vmem(3)),
-        compiler_params=pltpu.CompilerParams(vmem_limit_bytes=16 * MIB),
+        compiler_params=pltpu.CompilerParams(vmem_limit_bytes=4 * MIB),
         name="norm",
     )(upstream, stored, mom, affine)
 
 
-def block_grad(cells, grad_ref, q_ref, x_ref, stats_ref, sums_ref):
+def block_grad(cells, base, grad_ref, q_ref, x_ref, stats_ref, sums_ref):
     frames, cols, rows, channels = grad_ref.shape
     totals = group_sum(jnp.sum(sums_ref[...], axis=0)) * (1.0 / cells)
     result = []
     for f in range(frames):
-        mean = stats_ref[f : f + 1]
-        scale = stats_ref[frames + f : frames + f + 1]
+        mean = stats_ref[base + f : base + f + 1]
+        scale = stats_ref[base + frames + f : base + frames + f + 1]
         flat = (cols * rows, channels)
         normed = (x_ref[f].astype(jnp.float32).reshape(flat) - mean) * scale
         value = grad_ref[f].astype(jnp.float32).reshape(flat) + scale * (
@@ -284,7 +297,7 @@
 def dx_kernel(cells, par_ref, grad_ref, q_ref, x_ref, stats_ref, sums_ref, dx_ref, sa_ref, sb_ref):
     _, cols, rows, channels = grad_ref.shape
     even, _, _ = flags(par_ref)
-    for f, value in enumerate(block_grad(cells, grad_ref, q_ref, x_ref, stats_ref, sums_ref)):
+    for f, value in enumerate(block_grad(cells, 0, grad_ref, q_ref, x_ref, stats_ref, sums_ref)):
         value = value.reshape(cols, rows, channels)
         dx_ref[f] = value
         sa_ref[f], sb_ref[f] = swapped(even, value[cols - 1], value[0])
@@ -305,8 +318,6 @@
 
 
 def conv_norm_kernel(
-    cells,
-    base,
     par_ref,
     own_ref,
     next_ref,
@@ -316,11 +327,10 @@
     rbn_ref,
     w_ref,
     x_ref,
-    mom_ref,
+    stats_ref,
     affine_ref,
     q_ref,
     sums_ref,
-    stats_ref,
     ext,
     acc,
 ):
@@ -328,17 +338,18 @@
     window(par_ref, own_ref, next_ref, ra_ref, rb_ref, ran_ref, rbn_ref, ext)
     acc[...] = time_taps(ext, w_ref, (2, 1, 0), *own_ref.shape[:2])
     upstream = row_taps(acc, rows)
-    finish(cells, base, upstream, x_ref, mom_ref, affine_ref, 2, q_ref, sums_ref, stats_ref)
-
-
-def conv_norm_section(par, grad, halo, kernel, stored, mom, affine, cells, base, peers):
+    stats = stats_ref[2 * own_ref.shape[0] :]
+    finish(stats, upstream, x_ref, affine_ref, 2, q_ref, sums_ref)
+
+
+def conv_norm_section(par, grad, halo, kernel, stored, stats, affine, peers):
     frames, cols, rows, channels = grad.shape
     count = frames * cols * rows
     return pl.pallas_call(
-        functools.partial(conv_norm_kernel, cells, base),
+        conv_norm_kernel,
         out_shape=finish_shapes(stored, peers),
         in_specs=vmem(11),
-        out_specs=tuple(vmem(3)),
+        out_specs=tuple(vmem(2)),
         scratch_shapes=[
             pltpu.VMEM((2 * frames, cols + 2, rows, channels), jnp.bfloat16),
             pltpu.VMEM((count, 3 * channels), jnp.float32),
@@ -346,7 +357,7 @@
         compiler_params=pltpu.CompilerParams(vmem_limit_bytes=16 * MIB),
         cost_estimate=matmul_cost(count, kernel),
         name="convnorm",
-    )(par, grad, *halo, kernel, stored, mom, affine)
+    )(par, grad, *halo, kernel, stored, stats, affine)
 
 
 def edge_kernel(par_ref, block_ref, *out_refs):
@@ -374,7 +385,7 @@
     frames, cols, rows, channels = grad_ref.shape
     lat = k_ref.shape[1]
     lanes = own_ref.shape[-1]
-    values = block_grad(cells, grad_ref, q_ref, x_ref, stats_ref, sums_ref)
+    values = block_grad(cells, 2 * frames, grad_ref, q_ref, x_ref, stats_ref, sums_ref)
     grad = jnp.concatenate(values, axis=0)
     count = frames * cols * rows
     wide[...] = jnp.zeros_like(wide)
@@ -493,10 +504,10 @@
 
 def exchange(value, send_a, send_b):
     back, hops, diagonal = routes()
+    rb = lax.ppermute(send_b, TILE, hops)
+    ra = lax.ppermute(send_a, "tile_2", SWAP)
     nxt = lax.ppermute(value, "tm", back)
-    rb = lax.ppermute(send_b, TILE, hops)
     rbn = lax.ppermute(send_b, TM_TILE, diagonal)
-    ra = lax.ppermute(send_a, "tile_2", SWAP)
     return nxt, ra, rb, rbn
 
 
@@ -551,9 +562,8 @@
     nxt, ra, rb, rbn = exchange(grad, send_a, send_b)
     (corner,) = edge_section(par, nxt, 1, None)
     ran = lax.ppermute(corner, "tile_2", SWAP)
-    q, sums, stats = conv_norm_section(
-        par, grad, (nxt, ra, rb, ran, rbn), first_kernel, first, mom, affine, cells,
-        2 * frames, peers,
+    q, sums = conv_norm_section(
+        par, grad, (nxt, ra, rb, ran, rbn), first_kernel, first, stats, affine, peers
     )
     own, prev = latent_section(grad, q, first, stats, everyone(sums), latent_kernel, cells)
     tms = lax.axis_size("tm")

time: 83.5 us -> 82.7 us (level)
  local copies, waits for them, and re-layouts: 4.39 us -> 1.16 us
  Pallas kernels: 9.18 us -> 12 us
    unnamed x24 -> x22, local copies, waits for them, and re-layouts: 3.32 us -> 0.05 us
    pallas_call x1, Pallas kernels: 2.61 us -> 5.64 us  [conv_section(): pl.pallas_call(conv_kernel, out_shape=jax.ShapeDtypeStruct((count, channe...]
  transfers between devices with their start and end apart: 12 -> 12, of which waited for: 6 -> 6; matrix products, arithmetic and copies ran while one was open for 0% -> 0% of each run, Pallas kernels for 4% -> 8%
where the time goes in v4:
time: 82.7 us; the launch traced here: 82.4 us
  starting transfers between devices  33.2 us (40%)
  blocking collectives  31 us (37%)
  Pallas kernels  12 us (15%)
  waiting for transfers between devices  4.74 us (6%)
  local copies, waits for them, and re-layouts  1.16 us (1%)
    all_to_all x3, blocking collectives, everyone(): return lax.all_to_all(rows, TILE, 0, 0)  31 us
    ppermute x2, starting transfers between devices, exchange(): nxt = lax.ppermute(value, 'tm', back)  10.3 us
    ppermute x2, starting transfers between devices, shards(): ran = lax.ppermute(corner, 'tile_2', SWAP)  6.89 us
    ppermute x2, starting transfers between devices, exchange(): ra = lax.ppermute(send_a, 'tile_2', SWAP)  5.7 us
    pallas_call x1, Pallas kernels, conv_section(): pl.pallas_call(conv_kernel, out_shape=jax.ShapeDtypeStruct((count, channe...  5.64 us
    ppermute x1, starting transfers between devices, shards(): own = own + jnp.where(later, lax.ppermute(prev, 'tm', ring(tms)), 0.0)  4.43 us
    all_to_all x1, starting transfers between devices, everyone(): return lax.all_to_all(rows, TILE, 0, 0)  3.42 us
    pallas_call x1, Pallas kernels, conv_norm_section(): pl.pallas_call(conv_norm_kernel, out_shape=finish_shapes(stored, peers),...  2.71 us
  transfers between devices with their start and end apart: 12, of which 6 were waited for; matrix products, arithmetic and copies ran while one was open for 0% of the time, Pallas kernels for 8%

profile of v4, /device:TPU:1, one launch (start us, length us, event | category | flops | bytes accessed | tf_op | source)
XLA Modules:
  0.0 82.4 jit_solution(17245835984975176607)
XLA Ops:
  0.2 1.0 %copy.21 = bf16[2,32,4,384]{3,1,2,0:T(8,128)(2,1)S(1)} copy(bf16[2,32,4,384]{3,2,1,0:T(4,128)(2,1)} %param.14) | data formatting | bytes 393216 | tf_op jit(solution)/shard_map/optimization_barrier | solution.py:544
  1.2 6.0 %collective-permute-start = (bf16[2,4,32,384]{3,2,1,0:T(8,128)(2,1)S(1)}, bf16[2,4,32,384]{3,2,1,0:T(8,128)(2,1)S(1)}, u32[]{:S(2)}, u32[]{:S(2)}) collective-permute-start(bf16[2,4,32,384]{3,2,1,0:T(8,128)(2,1)S(1)} %bitcast.17), channel_id=1, source_target_pairs={{0,112},{16,0},{32,16},{48,32},{64,48},{80,64},{96,80},{112,96},{1... | collective-permute-start | bytes 589832 | tf_op jit(solution)/shard_map/ppermute | solution.py:509
  7.2 1.3 %collective-permute-start.2 = (bf16[2,32,384]{2,1,0:T(8,128)(2,1)S(1)}, bf16[2,32,384]{2,1,0:T(8,128)(2,1)S(1)}, u32[]{:S(2)}, u32[]{:S(2)}) collective-permute-start(bf16[2,32,384]{2,1,0:T(8,128)(2,1)S(1)} %get-tuple-element.29), channel_id=1, source_target_pairs={{1,2},{2,1},{3,4},{4,3},{5,6},{6,5},{7,8},{8,7},{9,10},{10,9},{11,... | collective-permute-start | bytes 147464 | tf_op jit(solution)/shard_map/ppermute | solution.py:507
  8.5 0.5 collective-permute-start.3
  9.0 3.0 %collective-permute-start.1 = (bf16[2,32,384]{2,1,0:T(8,128)(2,1)S(1)}, bf16[2,32,384]{2,1,0:T(8,128)(2,1)S(1)}, u32[]{:S(2)}, u32[]{:S(2)}) collective-permute-start(bf16[2,32,384]{2,1,0:T(8,128)(2,1)S(1)} %get-tuple-element.28), channel_id=1, source_target_pairs={{0,1},{1,0},{2,3},{3,2},{4,5},{5,4},{6,7},{7,6},{8,9},{9,8},{10,11... | collective-permute-start | bytes 147464 | tf_op jit(solution)/shard_map/ppermute | solution.py:508
  12.0 1.6 %collective-permute-done.3.rbn_ref = bf16[2,32,384]{2,1,0:T(8,128)(2,1)S(1)} collective-permute-done((bf16[2,32,384]{2,1,0:T(8,128)(2,1)S(1)}, bf16[2,32,384]{2,1,0:T(8,128)(2,1)S(1)}, u32[]{:S(2)}, u32[]{:S(2)}) %collective-permute-start.3) | collective-permute-done | bytes 49184 | tf_op jit(solution)/shard_map/ppermute | solution.py:510
  13.7 4.9 %collective-permute-start.4 = (bf16[2,32,384]{2,1,0:T(8,128)(2,1)S(1)}, bf16[2,32,384]{2,1,0:T(8,128)(2,1)S(1)}, u32[]{:S(2)}, u32[]{:S(2)}) collective-permute-start(bf16[2,32,384]{2,1,0:T(8,128)(2,1)S(1)} %get-tuple-element.31), channel_id=1, source_target_pairs={{0,1},{1,0},{2,3},{3,2},{4,5},{5,4},{6,7},{7,6},{8,9},{9,8},{10,11... | collective-permute-start | bytes 147464 | tf_op jit(solution)/shard_map/ppermute | solution.py:557
  18.6 1.0 %moments.1 = (f32[16,8,384]{2,1,0:T(8,128)}, f32[4,384]{1,0:T(4,128)S(1)}) custom-call(bf16[2,32,4,384]{3,2,1,0:T(4,128)(2,1)S(1)} %copy-done, bf16[2,32,4,384]{3,2,1,0:T(4,128)(2,1)S(1)} %copy-done.1, f32[384]{0:T(512)S(1)} %copy-done.5, f32[384]{0:T(512)S(1)} %copy-done.6, f32[384]{0:T(512)S(1)} %copy-done.7, f32[384]{0:T(512)S(1)} %copy-done.8), custom_call_target="tpu_custom_call" | custom-call | tf_op jit(solution)/shard_map/moments/pallas_call | solution.py:84
  19.6 3.4 %all-to-all-start = ((f32[16,8,384]{2,1,0:T(8,128)}), f32[16,8,384]{2,1,0:T(8,128)S(1)}, u32[]{:S(2)}, u32[]{:S(2)}) async-start(f32[16,8,384]{2,1,0:T(8,128)} %get-tuple-element.34), calls=%async_computation | async-start | bytes 393216 | tf_op jit(solution)/shard_map/all_to_all | solution.py:519
  23.1 5.6 %conv.1.u_ref = f32[256,384]{1,0:T(8,128)S(1)} custom-call(bf16[3,384]{1,0:T(4,128)(2,1)S(1)} %broadcast_in_dim.10.par_ref, bf16[4,6,32,384]{3,2,1,0:T(8,128)(2,1)S(1)} %get-tuple-element.30.part_ref, bf16[2,32,384]{2,1,0:T(8,128)(2,1)S(1)} %collective-permute-done.4.ran_ref, bf16[27,384,384]{2,1,0:T(8,128)(2,1)} %w_hbm.1), custom_call_target="tpu_custom_call" | custom-call | flops 2038431744 | bytes 7962624 | tf_op jit(solution)/shard_map/conv/pallas_call | solution.py:204
  28.8 0.9 %all-to-all-done.mom_ref = f32[16,8,384]{2,1,0:T(8,128)S(1)} async-done(((f32[16,8,384]{2,1,0:T(8,128)}), f32[16,8,384]{2,1,0:T(8,128)S(1)}, u32[]{:S(2)}, u32[]{:S(2)}) %all-to-all-start) | async-done | bytes 196640 | tf_op jit(solution)/shard_map/all_to_all | solution.py:519
  29.7 0.5 norm.1
  30.1 10.7 %all_to_all.20.sums_ref = f32[16,4,384]{2,1,0:T(4,128)S(1)} all-to-all(f32[16,4,384]{2,1,0:T(4,128)S(1)} %get-tuple-element.38), channel_id=1, replica_groups=mesh['tm'=8,'tile_0'=4,'tile_1'=2,'tile_2'=2] {'tile_0','tile_1','tile_2'}, dimensions={0} | all-to-all | bytes 196608 | tf_op jit(solution)/shard_map/all_to_all | solution.py:519
  41.2 4.3 %collective-permute-start.5 = (bf16[2,4,32,384]{3,2,1,0:T(8,128)(2,1)S(1)}, bf16[2,4,32,384]{3,2,1,0:T(8,128)(2,1)S(1)}, u32[]{:S(2)}, u32[]{:S(2)}) collective-permute-start(bf16[2,4,32,384]{3,2,1,0:T(8,128)(2,1)S(1)} %get-tuple-element.39.own_ref.grad_ref), channel_id=1, source_target_pairs={{0,112},{16,0},{32,16},{48,32},{64,48},{80,64},{96,80},{112,96},{1... | collective-permute-start | bytes 589832 | tf_op jit(solution)/shard_map/ppermute | solution.py:509
  46.2 2.7 %collective-permute-start.6 = (bf16[2,32,384]{2,1,0:T(8,128)(2,1)S(1)}, bf16[2,32,384]{2,1,0:T(8,128)(2,1)S(1)}, u32[]{:S(2)}, u32[]{:S(2)}) collective-permute-start(bf16[2,32,384]{2,1,0:T(8,128)(2,1)S(1)} %get-tuple-element.40), channel_id=1, source_target_pairs={{0,1},{1,0},{2,3},{3,2},{4,5},{5,4},{6,7},{7,6},{8,9},{9,8},{10,11... | collective-permute-start | bytes 147464 | tf_op jit(solution)/shard_map/ppermute | solution.py:508
  49.3 2.0 %collective-permute-start.8 = (bf16[2,32,384]{2,1,0:T(8,128)(2,1)S(1)}, bf16[2,32,384]{2,1,0:T(8,128)(2,1)S(1)}, u32[]{:S(2)}, u32[]{:S(2)}) collective-permute-start(bf16[2,32,384]{2,1,0:T(8,128)(2,1)S(1)} %edge.3), channel_id=1, source_target_pairs={{0,1},{1,0},{2,3},{3,2},{4,5},{5,4},{6,7},{7,6},{8,9},{9,8},{10,11... | collective-permute-start | bytes 147464 | tf_op jit(solution)/shard_map/ppermute | solution.py:564
  51.5 0.7 collective-permute-done.8.ran_ref
  52.2 2.7 %convnorm.1 = (f32[2,4,32,384]{3,2,1,0:T(8,128)S(1)}, f32[16,4,384]{2,1,0:T(4,128)S(1)}) custom-call(bf16[3,384]{1,0:T(4,128)(2,1)S(1)} %broadcast_in_dim.10.par_ref, bf16[2,4,32,384]{3,2,1,0:T(8,128)(2,1)S(1)} %get-tuple-element.39.own_ref.grad_ref, bf16[2,4,32,384]{3,2,1,0:T(8,128)(2,1)S(1)} %collective-permute-done.5.block_ref.next_ref, ...), custom_call_target="tpu_custom_call" | custom-call | flops 2038431744 | bytes 7962624 | tf_op jit(solution)/shard_map/convnorm/pallas_call | solution.py:348
  54.9 10.6 %all_to_all.21.sums_ref = f32[16,4,384]{2,1,0:T(4,128)S(1)} all-to-all(f32[16,4,384]{2,1,0:T(4,128)S(1)} %get-tuple-element.43), channel_id=1, replica_groups=mesh['tm'=8,'tile_0'=4,'tile_1'=2,'tile_2'=2] {'tile_0','tile_1','tile_2'}, dimensions={0} | all-to-all | bytes 196608 | tf_op jit(solution)/shard_map/all_to_all | solution.py:519
  65.5 0.7 latent.1
  66.2 4.4 %collective-permute-start.10 = (f32[2,32,128]{2,1,0:T(8,128)S(1)}, f32[2,32,128]{2,1,0:T(8,128)S(1)}, u32[]{:S(2)}, u32[]{:S(2)}) collective-permute-start(f32[2,32,128]{2,1,0:T(8,128)S(1)} %get-tuple-element.46), channel_id=1, source_target_pairs={{0,112},{16,0},{32,16},{48,32},{64,48},{80,64},{96,80},{112,96},{1... | collective-permute-start | bytes 98312 | tf_op jit(solution)/shard_map/ppermute | solution.py:570
  70.7 1.0 %collective-permute-done.10 = f32[2,32,128]{2,1,0:T(8,128)S(1)} collective-permute-done((f32[2,32,128]{2,1,0:T(8,128)S(1)}, f32[2,32,128]{2,1,0:T(8,128)S(1)}, u32[]{:S(2)}, u32[]{:S(2)}) %collective-permute-start.10) | collective-permute-done | bytes 32800 | tf_op jit(solution)/shard_map/ppermute | solution.py:570
  71.7 9.7 %all_to_all.22.got_ref = f32[16,4,128]{2,1,0:T(4,128)S(1)} all-to-all(f32[16,4,128]{2,1,0:T(4,128)S(1)} %bitcast.23), channel_id=1, replica_groups=mesh['tm'=8,'tile_0'=4,'tile_1'=2,'tile_2'=2] {'tile_0','tile_1','tile_2'}, dimensions={0} | all-to-all | bytes 65536 | tf_op jit(solution)/shard_map/all_to_all | solution.py:519
  81.4 1.1 %assemble.1 = f32[64,64]{1,0:T(8,128)} custom-call(f32[16,4,128]{2,1,0:T(4,128)S(1)} %all_to_all.22.got_ref, bf16[96,768]{1,0:T(8,128)(2,1)S(1)} %copy-done.3, bf16[64,192]{1,0:T(8,128)(2,1)S(1)} %copy-done.4), custom_call_target="tpu_custom_call" | custom-call | tf_op jit(solution)/shard_map/assemble/pallas_call | solution.py:482
  (42 shorter events, 1.9 us)
Async XLA Ops:
  0.0 18.6 %copy-start.1 = (bf16[2,32,4,384]{3,2,1,0:T(4,128)(2,1)S(1)}, bf16[2,32,4,384]{3,2,1,0:T(4,128)(2,1)}, u32[]{:S(2)}) copy-start(bf16[2,32,4,384]{3,2,1,0:T(4,128)(2,1)} %first_ref) | copy-start | bytes 589828
  0.0 18.6 %copy-start = (bf16[2,32,4,384]{3,2,1,0:T(4,128)(2,1)S(1)}, bf16[2,32,4,384]{3,2,1,0:T(4,128)(2,1)}, u32[]{:S(2)}) copy-start(bf16[2,32,4,384]{3,2,1,0:T(4,128)(2,1)} %second_ref) | copy-start | bytes 589828
  0.0 18.6 %copy-start.7 = (f32[384]{0:T(512)S(1)}, f32[384]{0:T(512)}, u32[]{:S(2)}) copy-start(f32[384]{0:T(512)} %refs_2_.1) | copy-start | bytes 4612
  0.0 18.6 %copy-start.8 = (f32[384]{0:T(512)S(1)}, f32[384]{0:T(512)}, u32[]{:S(2)}) copy-start(f32[384]{0:T(512)} %refs_3_.1) | copy-start | bytes 4612
  0.0 18.6 %copy-start.5 = (f32[384]{0:T(512)S(1)}, f32[384]{0:T(512)}, u32[]{:S(2)}) copy-start(f32[384]{0:T(512)} %refs_0_.1) | copy-start | bytes 4612
  0.0 18.6 %copy-start.6 = (f32[384]{0:T(512)S(1)}, f32[384]{0:T(512)}, u32[]{:S(2)}) copy-start(f32[384]{0:T(512)} %refs_1_.1) | copy-start | bytes 4612
  1.2 12.4 %collective-permute-start = (bf16[2,4,32,384]{3,2,1,0:T(8,128)(2,1)S(1)}, bf16[2,4,32,384]{3,2,1,0:T(8,128)(2,1)S(1)}, u32[]{:S(2)}, u32[]{:S(2)}) collective-permute-start(bf16[2,4,32,384]{3,2,1,0:T(8,128)(2,1)S(1)} %bitcast.17), channel_id=1, source_target_pairs={{0,112},{16,0},{32,16},{48,32},{64,48},{80,64},{96,80},{112,96},{1... | collective-permute-start | bytes 589832 | tf_op jit(solution)/shard_map/ppermute | solution.py:509
  7.2 4.8 %collective-permute-start.2 = (bf16[2,32,384]{2,1,0:T(8,128)(2,1)S(1)}, bf16[2,32,384]{2,1,0:T(8,128)(2,1)S(1)}, u32[]{:S(2)}, u32[]{:S(2)}) collective-permute-start(bf16[2,32,384]{2,1,0:T(8,128)(2,1)S(1)} %get-tuple-element.29), channel_id=1, source_target_pairs={{1,2},{2,1},{3,4},{4,3},{5,6},{6,5},{7,8},{8,7},{9,10},{10,9},{11,... | collective-permute-start | bytes 147464 | tf_op jit(solution)/shard_map/ppermute | solution.py:507
  8.5 5.1 %collective-permute-start.3 = (bf16[2,32,384]{2,1,0:T(8,128)(2,1)S(1)}, bf16[2,32,384]{2,1,0:T(8,128)(2,1)S(1)}, u32[]{:S(2)}, u32[]{:S(2)}) collective-permute-start(bf16[2,32,384]{2,1,0:T(8,128)(2,1)S(1)} %get-tuple-element.29), channel_id=1, source_target_pairs={{1,114},{2,113},{3,116},{4,115},{5,118},{6,117},{7,120},{8,119},{9... | collective-permute-start | bytes 147464 | tf_op jit(solution)/shard_map/ppermute | solution.py:510
  9.0 4.6 %collective-permute-start.1 = (bf16[2,32,384]{2,1,0:T(8,128)(2,1)S(1)}, bf16[2,32,384]{2,1,0:T(8,128)(2,1)S(1)}, u32[]{:S(2)}, u32[]{:S(2)}) collective-permute-start(bf16[2,32,384]{2,1,0:T(8,128)(2,1)S(1)} %get-tuple-element.28), channel_id=1, source_target_pairs={{0,1},{1,0},{2,3},{3,2},{4,5},{5,4},{6,7},{7,6},{8,9},{9,8},{10,11... | collective-permute-start | bytes 147464 | tf_op jit(solution)/shard_map/ppermute | solution.py:508
  13.7 9.4 %collective-permute-start.4 = (bf16[2,32,384]{2,1,0:T(8,128)(2,1)S(1)}, bf16[2,32,384]{2,1,0:T(8,128)(2,1)S(1)}, u32[]{:S(2)}, u32[]{:S(2)}) collective-permute-start(bf16[2,32,384]{2,1,0:T(8,128)(2,1)S(1)} %get-tuple-element.31), channel_id=1, source_target_pairs={{0,1},{1,0},{2,3},{3,2},{4,5},{5,4},{6,7},{7,6},{8,9},{9,8},{10,11... | collective-permute-start | bytes 147464 | tf_op jit(solution)/shard_map/ppermute | solution.py:557
  19.6 10.0 %all-to-all-start = ((f32[16,8,384]{2,1,0:T(8,128)}), f32[16,8,384]{2,1,0:T(8,128)S(1)}, u32[]{:S(2)}, u32[]{:S(2)}) async-start(f32[16,8,384]{2,1,0:T(8,128)} %get-tuple-element.34), calls=%async_computation | async-start | bytes 393216 | tf_op jit(solution)/shard_map/all_to_all | solution.py:519
  29.7 22.5 %slice-start = ((s8[7962624]{0:T(1024)(128)(4,1)}), s8[4194304]{0:T(1024)(128)(4,1)S(1)}, s32[]{:S(2)}) async-start(s8[7962624]{0:T(1024)(128)(4,1)} %bitcast.13), calls=%async_computation.4 | async-start | bytes 8388608
  40.9 11.3 %slice-start.1 = ((s8[7962624]{0:T(1024)(128)(4,1)}), s8[3768320]{0:T(1024)(128)(4,1)S(1)}, s32[]{:S(2)}) async-start(s8[7962624]{0:T(1024)(128)(4,1)} %bitcast.13), calls=%async_computation.5 | async-start | bytes 7536640
  41.2 24.3 %copy-start.2 = (bf16[27,16,384]{2,1,0:T(8,128)(2,1)S(1)}, bf16[27,16,384]{2,1,0:T(8,128)(2,1)}, u32[]{:S(2)}) copy-start(bf16[27,16,384]{2,1,0:T(8,128)(2,1)} %k_ref.1) | copy-start | bytes 995332
  41.2 40.1 %copy-start.3 = (bf16[96,768]{1,0:T(8,128)(2,1)S(1)}, bf16[96,768]{1,0:T(8,128)(2,1)}, u32[]{:S(2)}) copy-start(bf16[96,768]{1,0:T(8,128)(2,1)} %constant.33.clone.e_ref) | copy-start | bytes 442372
  41.2 40.1 %copy-start.4 = (bf16[64,192]{1,0:T(8,128)(2,1)S(1)}, bf16[64,192]{1,0:T(8,128)(2,1)}, u32[]{:S(2)}) copy-start(bf16[64,192]{1,0:T(8,128)(2,1)} %constant.34.clone.perm_ref) | copy-start | bytes 73732
  41.2 8.0 %collective-permute-start.5 = (bf16[2,4,32,384]{3,2,1,0:T(8,128)(2,1)S(1)}, bf16[2,4,32,384]{3,2,1,0:T(8,128)(2,1)S(1)}, u32[]{:S(2)}, u32[]{:S(2)}) collective-permute-start(bf16[2,4,32,384]{3,2,1,0:T(8,128)(2,1)S(1)} %get-tuple-element.39.own_ref.grad_ref), channel_id=1, source_target_pairs={{0,112},{16,0},{32,16},{48,32},{64,48},{80,64},{96,80},{112,96},{1... | collective-permute-start | bytes 589832 | tf_op jit(solution)/shard_map/ppermute | solution.py:509
  45.5 5.8 %collective-permute-start.7 = (bf16[2,32,384]{2,1,0:T(8,128)(2,1)S(1)}, bf16[2,32,384]{2,1,0:T(8,128)(2,1)S(1)}, u32[]{:S(2)}, u32[]{:S(2)}) collective-permute-start(bf16[2,32,384]{2,1,0:T(8,128)(2,1)S(1)} %get-tuple-element.41), channel_id=1, source_target_pairs={{1,2},{2,1},{3,4},{4,3},{5,6},{6,5},{7,8},{8,7},{9,10},{10,9},{11,... | collective-permute-start | bytes 147464 | tf_op jit(solution)/shard_map/ppermute | solution.py:507
  46.0 5.5 %collective-permute-start.9 = (bf16[2,32,384]{2,1,0:T(8,128)(2,1)S(1)}, bf16[2,32,384]{2,1,0:T(8,128)(2,1)S(1)}, u32[]{:S(2)}, u32[]{:S(2)}) collective-permute-start(bf16[2,32,384]{2,1,0:T(8,128)(2,1)S(1)} %get-tuple-element.41), channel_id=1, source_target_pairs={{1,114},{2,113},{3,116},{4,115},{5,118},{6,117},{7,120},{8,119},{9... | collective-permute-start | bytes 147464 | tf_op jit(solution)/shard_map/ppermute | solution.py:510
  46.2 5.1 %collective-permute-start.6 = (bf16[2,32,384]{2,1,0:T(8,128)(2,1)S(1)}, bf16[2,32,384]{2,1,0:T(8,128)(2,1)S(1)}, u32[]{:S(2)}, u32[]{:S(2)}) collective-permute-start(bf16[2,32,384]{2,1,0:T(8,128)(2,1)S(1)} %get-tuple-element.40), channel_id=1, source_target_pairs={{0,1},{1,0},{2,3},{3,2},{4,5},{5,4},{6,7},{7,6},{8,9},{9,8},{10,11... | collective-permute-start | bytes 147464 | tf_op jit(solution)/shard_map/ppermute | solution.py:508
  49.3 2.9 %collective-permute-start.8 = (bf16[2,32,384]{2,1,0:T(8,128)(2,1)S(1)}, bf16[2,32,384]{2,1,0:T(8,128)(2,1)S(1)}, u32[]{:S(2)}, u32[]{:S(2)}) collective-permute-start(bf16[2,32,384]{2,1,0:T(8,128)(2,1)S(1)} %edge.3), channel_id=1, source_target_pairs={{0,1},{1,0},{2,3},{3,2},{4,5},{5,4},{6,7},{7,6},{8,9},{9,8},{10,11... | collective-permute-start | bytes 147464 | tf_op jit(solution)/shard_map/ppermute | solution.py:564
  66.2 5.5 %collective-permute-start.10 = (f32[2,32,128]{2,1,0:T(8,128)S(1)}, f32[2,32,128]{2,1,0:T(8,128)S(1)}, u32[]{:S(2)}, u32[]{:S(2)}) collective-permute-start(f32[2,32,128]{2,1,0:T(8,128)S(1)} %get-tuple-element.46), channel_id=1, source_target_pairs={{0,112},{16,0},{32,16},{48,32},{64,48},{80,64},{96,80},{112,96},{1... | collective-permute-start | bytes 98312 | tf_op jit(solution)/shard_map/ppermute | solution.py:570

commit v5 on v4

--- a/solution.py
+++ b/solution.py
@@ -102,7 +102,7 @@
     ext[at : at + frames, cols + 1] = right
 
 
-def time_taps(ext, w_ref, taps, frames, cols, row_taps=(0, 1, 2)):
+def time_taps(ext, w_ref, taps, frames, cols):
     _, channels = ext.shape[2:]
     pairs = [(a, c) for a in taps for c in range(3)]
     left = jnp.concatenate(
@@ -115,7 +115,7 @@
     right = jnp.concatenate(
         [
             jnp.concatenate([w_ref[9 * a + 3 * b + c] for a, c in pairs], axis=1)
-            for b in row_taps
+            for b in range(3)
         ],
         axis=0,
     )
@@ -176,24 +176,22 @@
 
 
 def conv_kernel(par_ref, part_ref, ran_ref, w_hbm, u_ref, ext, acc, w_ref, sems):
-    frames, rows, channels = ran_ref.shape
+    frames, rows, _ = ran_ref.shape
     cols = part_ref.shape[1] - 2
-    pieces = [(2, (0, 1, 2)), (1, (0, 1, 2)), (0, (0,)), (0, (1,)), (0, (2,))]
-    copies = []
-    for k, (a, bs) in enumerate(pieces):
-        span = pl.ds(9 * a + 3 * bs[0], 3 * len(bs))
-        copies.append(pltpu.make_async_copy(w_hbm.at[span], w_ref.at[span], sems.at[k]))
-        copies[-1].start()
+    copies = {}
+    for a in (2, 1, 0):
+        span = pl.ds(9 * a, 9)
+        copies[a] = pltpu.make_async_copy(w_hbm.at[span], w_ref.at[span], sems.at[a])
+        copies[a].start()
     even, _, later = flags(par_ref)
     ext[...] = part_ref[...]
     right, left = swapped(even, ran_ref[...] * later, jnp.zeros_like(ran_ref))
     ext[frames:, 0] = part_ref[frames:, 0] + left
     ext[frames:, cols + 1] = part_ref[frames:, cols + 1] + right
-    for copy, (a, bs) in zip(copies, pieces):
+    for a, copy in copies.items():
         copy.wait()
-        lanes = slice(bs[0] * channels, (bs[-1] + 1) * channels)
-        part = time_taps(ext, w_ref, (a,), frames, cols, bs)
-        acc[:, lanes] = part if a == 2 else acc[:, lanes] + part
+        part = time_taps(ext, w_ref, (a,), frames, cols)
+        acc[...] = part if a == 2 else acc[...] + part
     u_ref[...] = row_taps(acc, rows)
 
 
@@ -210,7 +208,7 @@
             pltpu.VMEM(part.shape, jnp.bfloat16),
             pltpu.VMEM((count, 3 * channels), jnp.float32),
             pltpu.VMEM(kernel.shape, jnp.bfloat16),
-            pltpu.SemaphoreType.DMA((5,)),
+            pltpu.SemaphoreType.DMA((3,)),
         ],
         compiler_params=pltpu.CompilerParams(vmem_limit_bytes=16 * MIB),
         cost_estimate=matmul_cost(count, kernel),
@@ -502,13 +500,16 @@
 SWAP = [(0, 1), (1, 0)]
 
 
-def exchange(value, send_a, send_b):
-    back, hops, diagonal = routes()
+def frames_on(value):
+    return lax.ppermute(value, "tm", routes()[0])
+
+
+def columns_on(send_a, send_b):
+    _, hops, diagonal = routes()
     rb = lax.ppermute(send_b, TILE, hops)
+    rbn = lax.ppermute(send_b, TM_TILE, diagonal)
     ra = lax.ppermute(send_a, "tile_2", SWAP)
-    nxt = lax.ppermute(value, "tm", back)
-    rbn = lax.ppermute(send_b, TM_TILE, diagonal)
-    return nxt, ra, rb, rbn
+    return ra, rb, rbn
 
 
 def ring(count):
@@ -552,14 +553,16 @@
     vectors = (second_gain, second_shift, first_gain, first_shift)
     mine, affine = moments(second_input, first_input, vectors, peers)
     mom = everyone(mine)
-    nxt, ra, rb, rbn = exchange(grad, *edge_section(par, grad, 2, INPUTS_COVER))
+    nxt = turn(frames_on(output_grad))
+    ra, rb, rbn = columns_on(*edge_section(par, grad, 2, INPUTS_COVER))
     part, corner = gather_section(par, grad, nxt, ra, rb, rbn)
     ran = lax.ppermute(corner, "tile_2", SWAP)
     second, first = turn(second_input), turn(first_input)
     upstream = conv_section(par, part, ran, second_kernel)
     q, sums, stats = norm_section(upstream, second, mom, affine, cells, peers)
     grad, send_a, send_b = dx_section(par, grad, q, second, stats, everyone(sums), cells)
-    nxt, ra, rb, rbn = exchange(grad, send_a, send_b)
+    nxt = frames_on(grad)
+    ra, rb, rbn = columns_on(send_a, send_b)
     (corner,) = edge_section(par, nxt, 1, None)
     ran = lax.ppermute(corner, "tile_2", SWAP)
     q, sums = conv_norm_section(

time: 82.7 us -> 82.3 us (level)
  no operation moved by 1% of the time
where the time goes in v5:
time: 82.3 us; the launch traced here: 82 us
  starting transfers between devices  33.2 us (40%)
  blocking collectives  30.6 us (37%)
  Pallas kernels  11.6 us (14%)
  waiting for transfers between devices  5.2 us (6%)
  local copies, waits for them, and re-layouts  1.16 us (1%)
    all_to_all x3, blocking collectives, everyone(): return lax.all_to_all(rows, TILE, 0, 0)  30.6 us
    ppermute x2, starting transfers between devices, frames_on(): return lax.ppermute(value, 'tm', routes()[0])  10.3 us
    ppermute x2, starting transfers between devices, shards(): ran = lax.ppermute(corner, 'tile_2', SWAP)  6.89 us
    ppermute x2, starting transfers between devices, columns_on(): ra = lax.ppermute(send_a, 'tile_2', SWAP)  5.7 us
    pallas_call x1, Pallas kernels, conv_section(): pl.pallas_call(conv_kernel, out_shape=jax.ShapeDtypeStruct((count, channe...  5.18 us
    ppermute x1, starting transfers between devices, shards(): own = own + jnp.where(later, lax.ppermute(prev, 'tm', ring(tms)), 0.0)  4.43 us
    all_to_all x1, starting transfers between devices, everyone(): return lax.all_to_all(rows, TILE, 0, 0)  3.42 us
    pallas_call x1, Pallas kernels, conv_norm_section(): pl.pallas_call(conv_norm_kernel, out_shape=finish_shapes(stored, peers),...  2.71 us
  transfers between devices with their start and end apart: 12, of which 6 were waited for; matrix products, arithmetic and copies ran while one was open for 0% of the time, Pallas kernels for 8%

profile of v5, /device:TPU:1, one launch (start us, length us, event | category | flops | bytes accessed | tf_op | source)
XLA Modules:
  0.0 82.0 jit_solution(14870206410642577617)
XLA Ops:
  0.2 1.0 %copy.23 = bf16[2,32,4,384]{3,1,2,0:T(8,128)(2,1)S(1)} copy(bf16[2,32,4,384]{3,2,1,0:T(4,128)(2,1)} %param.14) | data formatting | bytes 393216 | tf_op jit(solution)/shard_map/optimization_barrier | solution.py:545
  1.2 6.0 %collective-permute-start = (bf16[2,32,4,384]{3,1,2,0:T(8,128)(2,1)S(1)}, bf16[2,32,4,384]{3,1,2,0:T(8,128)(2,1)S(1)}, u32[]{:S(2)}, u32[]{:S(2)}) collective-permute-start(bf16[2,32,4,384]{3,1,2,0:T(8,128)(2,1)S(1)} %copy.23), channel_id=1, source_target_pairs={{0,112},{16,0},{32,16},{48,32},{64,48},{80,64},{96,80},{112,96},{1... | collective-permute-start | bytes 589832 | tf_op jit(solution)/shard_map/ppermute | solution.py:504
  7.2 1.3 %collective-permute-start.2 = (bf16[2,32,384]{2,1,0:T(8,128)(2,1)S(1)}, bf16[2,32,384]{2,1,0:T(8,128)(2,1)S(1)}, u32[]{:S(2)}, u32[]{:S(2)}) collective-permute-start(bf16[2,32,384]{2,1,0:T(8,128)(2,1)S(1)} %get-tuple-element.29), channel_id=1, source_target_pairs={{1,2},{2,1},{3,4},{4,3},{5,6},{6,5},{7,8},{8,7},{9,10},{10,9},{11,... | collective-permute-start | bytes 147464 | tf_op jit(solution)/shard_map/ppermute | solution.py:509
  8.5 0.5 collective-permute-start.3
  9.0 3.0 %collective-permute-start.1 = (bf16[2,32,384]{2,1,0:T(8,128)(2,1)S(1)}, bf16[2,32,384]{2,1,0:T(8,128)(2,1)S(1)}, u32[]{:S(2)}, u32[]{:S(2)}) collective-permute-start(bf16[2,32,384]{2,1,0:T(8,128)(2,1)S(1)} %get-tuple-element.28), channel_id=1, source_target_pairs={{0,1},{1,0},{2,3},{3,2},{4,5},{5,4},{6,7},{7,6},{8,9},{9,8},{10,11... | collective-permute-start | bytes 147464 | tf_op jit(solution)/shard_map/ppermute | solution.py:511
  12.0 1.6 %collective-permute-done.3.rbn_ref = bf16[2,32,384]{2,1,0:T(8,128)(2,1)S(1)} collective-permute-done((bf16[2,32,384]{2,1,0:T(8,128)(2,1)S(1)}, bf16[2,32,384]{2,1,0:T(8,128)(2,1)S(1)}, u32[]{:S(2)}, u32[]{:S(2)}) %collective-permute-start.3) | collective-permute-done | bytes 49184 | tf_op jit(solution)/shard_map/ppermute | solution.py:510
  13.7 4.9 %collective-permute-start.4 = (bf16[2,32,384]{2,1,0:T(8,128)(2,1)S(1)}, bf16[2,32,384]{2,1,0:T(8,128)(2,1)S(1)}, u32[]{:S(2)}, u32[]{:S(2)}) collective-permute-start(bf16[2,32,384]{2,1,0:T(8,128)(2,1)S(1)} %get-tuple-element.31), channel_id=1, source_target_pairs={{0,1},{1,0},{2,3},{3,2},{4,5},{5,4},{6,7},{7,6},{8,9},{9,8},{10,11... | collective-permute-start | bytes 147464 | tf_op jit(solution)/shard_map/ppermute | solution.py:559
  18.6 1.0 %moments.1 = (f32[16,8,384]{2,1,0:T(8,128)}, f32[4,384]{1,0:T(4,128)S(1)}) custom-call(bf16[2,32,4,384]{3,2,1,0:T(4,128)(2,1)S(1)} %copy-done, bf16[2,32,4,384]{3,2,1,0:T(4,128)(2,1)S(1)} %copy-done.1, f32[384]{0:T(512)S(1)} %copy-done.5, f32[384]{0:T(512)S(1)} %copy-done.6, f32[384]{0:T(512)S(1)} %copy-done.7, f32[384]{0:T(512)S(1)} %copy-done.8), custom_call_target="tpu_custom_call" | custom-call | tf_op jit(solution)/shard_map/moments/pallas_call | solution.py:84
  19.6 3.4 %all-to-all-start = ((f32[16,8,384]{2,1,0:T(8,128)}), f32[16,8,384]{2,1,0:T(8,128)S(1)}, u32[]{:S(2)}, u32[]{:S(2)}) async-start(f32[16,8,384]{2,1,0:T(8,128)} %get-tuple-element.34), calls=%async_computation | async-start | bytes 393216 | tf_op jit(solution)/shard_map/all_to_all | solution.py:520
  23.1 5.2 %conv.1.u_ref = f32[256,384]{1,0:T(8,128)S(1)} custom-call(bf16[3,384]{1,0:T(4,128)(2,1)S(1)} %broadcast_in_dim.10.par_ref, bf16[4,6,32,384]{3,2,1,0:T(8,128)(2,1)S(1)} %get-tuple-element.30.part_ref, bf16[2,32,384]{2,1,0:T(8,128)(2,1)S(1)} %collective-permute-done.4.ran_ref, bf16[27,384,384]{2,1,0:T(8,128)(2,1)} %w_hbm.1), custom_call_target="tpu_custom_call" | custom-call | flops 2038431744 | bytes 7962624 | tf_op jit(solution)/shard_map/conv/pallas_call | solution.py:202
  28.3 1.4 %all-to-all-done.mom_ref = f32[16,8,384]{2,1,0:T(8,128)S(1)} async-done(((f32[16,8,384]{2,1,0:T(8,128)}), f32[16,8,384]{2,1,0:T(8,128)S(1)}, u32[]{:S(2)}, u32[]{:S(2)}) %all-to-all-start) | async-done | bytes 196640 | tf_op jit(solution)/shard_map/all_to_all | solution.py:520
  29.7 0.5 norm.1
  30.1 10.2 %all_to_all.20.sums_ref = f32[16,4,384]{2,1,0:T(4,128)S(1)} all-to-all(f32[16,4,384]{2,1,0:T(4,128)S(1)} %get-tuple-element.38), channel_id=1, replica_groups=mesh['tm'=8,'tile_0'=4,'tile_1'=2,'tile_2'=2] {'tile_0','tile_1','tile_2'}, dimensions={0} | all-to-all | bytes 196608 | tf_op jit(solution)/shard_map/all_to_all | solution.py:520
  40.8 4.3 %collective-permute-start.5 = (bf16[2,4,32,384]{3,2,1,0:T(8,128)(2,1)S(1)}, bf16[2,4,32,384]{3,2,1,0:T(8,128)(2,1)S(1)}, u32[]{:S(2)}, u32[]{:S(2)}) collective-permute-start(bf16[2,4,32,384]{3,2,1,0:T(8,128)(2,1)S(1)} %get-tuple-element.39.own_ref.grad_ref), channel_id=1, source_target_pairs={{0,112},{16,0},{32,16},{48,32},{64,48},{80,64},{96,80},{112,96},{1... | collective-permute-start | bytes 589832 | tf_op jit(solution)/shard_map/ppermute | solution.py:504
  45.7 2.7 %collective-permute-start.6 = (bf16[2,32,384]{2,1,0:T(8,128)(2,1)S(1)}, bf16[2,32,384]{2,1,0:T(8,128)(2,1)S(1)}, u32[]{:S(2)}, u32[]{:S(2)}) collective-permute-start(bf16[2,32,384]{2,1,0:T(8,128)(2,1)S(1)} %get-tuple-element.40), channel_id=1, source_target_pairs={{0,1},{1,0},{2,3},{3,2},{4,5},{5,4},{6,7},{7,6},{8,9},{9,8},{10,11... | collective-permute-start | bytes 147464 | tf_op jit(solution)/shard_map/ppermute | solution.py:511
  48.8 2.0 %collective-permute-start.8 = (bf16[2,32,384]{2,1,0:T(8,128)(2,1)S(1)}, bf16[2,32,384]{2,1,0:T(8,128)(2,1)S(1)}, u32[]{:S(2)}, u32[]{:S(2)}) collective-permute-start(bf16[2,32,384]{2,1,0:T(8,128)(2,1)S(1)} %edge.3), channel_id=1, source_target_pairs={{0,1},{1,0},{2,3},{3,2},{4,5},{5,4},{6,7},{7,6},{8,9},{9,8},{10,11... | collective-permute-start | bytes 147464 | tf_op jit(solution)/shard_map/ppermute | solution.py:567
  51.0 0.7 collective-permute-done.8.ran_ref
  51.7 2.7 %convnorm.1 = (f32[2,4,32,384]{3,2,1,0:T(8,128)S(1)}, f32[16,4,384]{2,1,0:T(4,128)S(1)}) custom-call(bf16[3,384]{1,0:T(4,128)(2,1)S(1)} %broadcast_in_dim.10.par_ref, bf16[2,4,32,384]{3,2,1,0:T(8,128)(2,1)S(1)} %get-tuple-element.39.own_ref.grad_ref, bf16[2,4,32,384]{3,2,1,0:T(8,128)(2,1)S(1)} %collective-permute-done.5.block_ref.next_ref, ...), custom_call_target="tpu_custom_call" | custom-call | flops 2038431744 | bytes 7962624 | tf_op jit(solution)/shard_map/convnorm/pallas_call | solution.py:346
  54.4 10.6 %all_to_all.21.sums_ref = f32[16,4,384]{2,1,0:T(4,128)S(1)} all-to-all(f32[16,4,384]{2,1,0:T(4,128)S(1)} %get-tuple-element.43), channel_id=1, replica_groups=mesh['tm'=8,'tile_0'=4,'tile_1'=2,'tile_2'=2] {'tile_0','tile_1','tile_2'}, dimensions={0} | all-to-all | bytes 196608 | tf_op jit(solution)/shard_map/all_to_all | solution.py:520
  65.1 0.7 latent.1
  65.8 4.4 %collective-permute-start.10 = (f32[2,32,128]{2,1,0:T(8,128)S(1)}, f32[2,32,128]{2,1,0:T(8,128)S(1)}, u32[]{:S(2)}, u32[]{:S(2)}) collective-permute-start(f32[2,32,128]{2,1,0:T(8,128)S(1)} %get-tuple-element.46), channel_id=1, source_target_pairs={{0,112},{16,0},{32,16},{48,32},{64,48},{80,64},{96,80},{112,96},{1... | collective-permute-start | bytes 98312 | tf_op jit(solution)/shard_map/ppermute | solution.py:573
  70.2 1.0 %collective-permute-done.10 = f32[2,32,128]{2,1,0:T(8,128)S(1)} collective-permute-done((f32[2,32,128]{2,1,0:T(8,128)S(1)}, f32[2,32,128]{2,1,0:T(8,128)S(1)}, u32[]{:S(2)}, u32[]{:S(2)}) %collective-permute-start.10) | collective-permute-done | bytes 32800 | tf_op jit(solution)/shard_map/ppermute | solution.py:573
  71.2 9.7 %all_to_all.22.got_ref = f32[16,4,128]{2,1,0:T(4,128)S(1)} all-to-all(f32[16,4,128]{2,1,0:T(4,128)S(1)} %bitcast.23), channel_id=1, replica_groups=mesh['tm'=8,'tile_0'=4,'tile_1'=2,'tile_2'=2] {'tile_0','tile_1','tile_2'}, dimensions={0} | all-to-all | bytes 65536 | tf_op jit(solution)/shard_map/all_to_all | solution.py:520
  80.9 1.1 %assemble.1 = f32[64,64]{1,0:T(8,128)} custom-call(f32[16,4,128]{2,1,0:T(4,128)S(1)} %all_to_all.22.got_ref, bf16[96,768]{1,0:T(8,128)(2,1)S(1)} %copy-done.3, bf16[64,192]{1,0:T(8,128)(2,1)S(1)} %copy-done.4), custom_call_target="tpu_custom_call" | custom-call | tf_op jit(solution)/shard_map/assemble/pallas_call | solution.py:480
  (42 shorter events, 1.9 us)
Async XLA Ops:
  0.0 18.6 %copy-start.1 = (bf16[2,32,4,384]{3,2,1,0:T(4,128)(2,1)S(1)}, bf16[2,32,4,384]{3,2,1,0:T(4,128)(2,1)}, u32[]{:S(2)}) copy-start(bf16[2,32,4,384]{3,2,1,0:T(4,128)(2,1)} %first_ref) | copy-start | bytes 589828
  0.0 18.6 %copy-start = (bf16[2,32,4,384]{3,2,1,0:T(4,128)(2,1)S(1)}, bf16[2,32,4,384]{3,2,1,0:T(4,128)(2,1)}, u32[]{:S(2)}) copy-start(bf16[2,32,4,384]{3,2,1,0:T(4,128)(2,1)} %second_ref) | copy-start | bytes 589828
  0.0 18.6 %copy-start.7 = (f32[384]{0:T(512)S(1)}, f32[384]{0:T(512)}, u32[]{:S(2)}) copy-start(f32[384]{0:T(512)} %refs_2_.1) | copy-start | bytes 4612
  0.0 18.6 %copy-start.8 = (f32[384]{0:T(512)S(1)}, f32[384]{0:T(512)}, u32[]{:S(2)}) copy-start(f32[384]{0:T(512)} %refs_3_.1) | copy-start | bytes 4612
  0.0 18.6 %copy-start.5 = (f32[384]{0:T(512)S(1)}, f32[384]{0:T(512)}, u32[]{:S(2)}) copy-start(f32[384]{0:T(512)} %refs_0_.1) | copy-start | bytes 4612
  0.0 18.6 %copy-start.6 = (f32[384]{0:T(512)S(1)}, f32[384]{0:T(512)}, u32[]{:S(2)}) copy-start(f32[384]{0:T(512)} %refs_1_.1) | copy-start | bytes 4612
  1.2 12.4 %collective-permute-start = (bf16[2,32,4,384]{3,1,2,0:T(8,128)(2,1)S(1)}, bf16[2,32,4,384]{3,1,2,0:T(8,128)(2,1)S(1)}, u32[]{:S(2)}, u32[]{:S(2)}) collective-permute-start(bf16[2,32,4,384]{3,1,2,0:T(8,128)(2,1)S(1)} %copy.23), channel_id=1, source_target_pairs={{0,112},{16,0},{32,16},{48,32},{64,48},{80,64},{96,80},{112,96},{1... | collective-permute-start | bytes 589832 | tf_op jit(solution)/shard_map/ppermute | solution.py:504
  7.2 4.8 %collective-permute-start.2 = (bf16[2,32,384]{2,1,0:T(8,128)(2,1)S(1)}, bf16[2,32,384]{2,1,0:T(8,128)(2,1)S(1)}, u32[]{:S(2)}, u32[]{:S(2)}) collective-permute-start(bf16[2,32,384]{2,1,0:T(8,128)(2,1)S(1)} %get-tuple-element.29), channel_id=1, source_target_pairs={{1,2},{2,1},{3,4},{4,3},{5,6},{6,5},{7,8},{8,7},{9,10},{10,9},{11,... | collective-permute-start | bytes 147464 | tf_op jit(solution)/shard_map/ppermute | solution.py:509
  8.5 5.1 %collective-permute-start.3 = (bf16[2,32,384]{2,1,0:T(8,128)(2,1)S(1)}, bf16[2,32,384]{2,1,0:T(8,128)(2,1)S(1)}, u32[]{:S(2)}, u32[]{:S(2)}) collective-permute-start(bf16[2,32,384]{2,1,0:T(8,128)(2,1)S(1)} %get-tuple-element.29), channel_id=1, source_target_pairs={{1,114},{2,113},{3,116},{4,115},{5,118},{6,117},{7,120},{8,119},{9... | collective-permute-start | bytes 147464 | tf_op jit(solution)/shard_map/ppermute | solution.py:510
  9.0 4.6 %collective-permute-start.1 = (bf16[2,32,384]{2,1,0:T(8,128)(2,1)S(1)}, bf16[2,32,384]{2,1,0:T(8,128)(2,1)S(1)}, u32[]{:S(2)}, u32[]{:S(2)}) collective-permute-start(bf16[2,32,384]{2,1,0:T(8,128)(2,1)S(1)} %get-tuple-element.28), channel_id=1, source_target_pairs={{0,1},{1,0},{2,3},{3,2},{4,5},{5,4},{6,7},{7,6},{8,9},{9,8},{10,11... | collective-permute-start | bytes 147464 | tf_op jit(solution)/shard_map/ppermute | solution.py:511
  13.7 9.4 %collective-permute-start.4 = (bf16[2,32,384]{2,1,0:T(8,128)(2,1)S(1)}, bf16[2,32,384]{2,1,0:T(8,128)(2,1)S(1)}, u32[]{:S(2)}, u32[]{:S(2)}) collective-permute-start(bf16[2,32,384]{2,1,0:T(8,128)(2,1)S(1)} %get-tuple-element.31), channel_id=1, source_target_pairs={{0,1},{1,0},{2,3},{3,2},{4,5},{5,4},{6,7},{7,6},{8,9},{9,8},{10,11... | collective-permute-start | bytes 147464 | tf_op jit(solution)/shard_map/ppermute | solution.py:559
  19.6 10.0 %all-to-all-start = ((f32[16,8,384]{2,1,0:T(8,128)}), f32[16,8,384]{2,1,0:T(8,128)S(1)}, u32[]{:S(2)}, u32[]{:S(2)}) async-start(f32[16,8,384]{2,1,0:T(8,128)} %get-tuple-element.34), calls=%async_computation | async-start | bytes 393216 | tf_op jit(solution)/shard_map/all_to_all | solution.py:520
  29.7 22.0 %slice-start = ((s8[7962624]{0:T(1024)(128)(4,1)}), s8[4194304]{0:T(1024)(128)(4,1)S(1)}, s32[]{:S(2)}) async-start(s8[7962624]{0:T(1024)(128)(4,1)} %bitcast.13), calls=%async_computation.4 | async-start | bytes 8388608
  40.4 11.3 %slice-start.1 = ((s8[7962624]{0:T(1024)(128)(4,1)}), s8[3768320]{0:T(1024)(128)(4,1)S(1)}, s32[]{:S(2)}) async-start(s8[7962624]{0:T(1024)(128)(4,1)} %bitcast.13), calls=%async_computation.5 | async-start | bytes 7536640
  40.7 24.3 %copy-start.2 = (bf16[27,16,384]{2,1,0:T(8,128)(2,1)S(1)}, bf16[27,16,384]{2,1,0:T(8,128)(2,1)}, u32[]{:S(2)}) copy-start(bf16[27,16,384]{2,1,0:T(8,128)(2,1)} %k_ref.1) | copy-start | bytes 995332
  40.7 40.2 %copy-start.3 = (bf16[96,768]{1,0:T(8,128)(2,1)S(1)}, bf16[96,768]{1,0:T(8,128)(2,1)}, u32[]{:S(2)}) copy-start(bf16[96,768]{1,0:T(8,128)(2,1)} %constant.33.clone.e_ref) | copy-start | bytes 442372
  40.8 40.1 %copy-start.4 = (bf16[64,192]{1,0:T(8,128)(2,1)S(1)}, bf16[64,192]{1,0:T(8,128)(2,1)}, u32[]{:S(2)}) copy-start(bf16[64,192]{1,0:T(8,128)(2,1)} %constant.34.clone.perm_ref) | copy-start | bytes 73732
  40.8 8.0 %collective-permute-start.5 = (bf16[2,4,32,384]{3,2,1,0:T(8,128)(2,1)S(1)}, bf16[2,4,32,384]{3,2,1,0:T(8,128)(2,1)S(1)}, u32[]{:S(2)}, u32[]{:S(2)}) collective-permute-start(bf16[2,4,32,384]{3,2,1,0:T(8,128)(2,1)S(1)} %get-tuple-element.39.own_ref.grad_ref), channel_id=1, source_target_pairs={{0,112},{16,0},{32,16},{48,32},{64,48},{80,64},{96,80},{112,96},{1... | collective-permute-start | bytes 589832 | tf_op jit(solution)/shard_map/ppermute | solution.py:504
  45.1 5.8 %collective-permute-start.7 = (bf16[2,32,384]{2,1,0:T(8,128)(2,1)S(1)}, bf16[2,32,384]{2,1,0:T(8,128)(2,1)S(1)}, u32[]{:S(2)}, u32[]{:S(2)}) collective-permute-start(bf16[2,32,384]{2,1,0:T(8,128)(2,1)S(1)} %get-tuple-element.41), channel_id=1, source_target_pairs={{1,2},{2,1},{3,4},{4,3},{5,6},{6,5},{7,8},{8,7},{9,10},{10,9},{11,... | collective-permute-start | bytes 147464 | tf_op jit(solution)/shard_map/ppermute | solution.py:509
  45.5 5.5 %collective-permute-start.9 = (bf16[2,32,384]{2,1,0:T(8,128)(2,1)S(1)}, bf16[2,32,384]{2,1,0:T(8,128)(2,1)S(1)}, u32[]{:S(2)}, u32[]{:S(2)}) collective-permute-start(bf16[2,32,384]{2,1,0:T(8,128)(2,1)S(1)} %get-tuple-element.41), channel_id=1, source_target_pairs={{1,114},{2,113},{3,116},{4,115},{5,118},{6,117},{7,120},{8,119},{9... | collective-permute-start | bytes 147464 | tf_op jit(solution)/shard_map/ppermute | solution.py:510
  45.7 5.1 %collective-permute-start.6 = (bf16[2,32,384]{2,1,0:T(8,128)(2,1)S(1)}, bf16[2,32,384]{2,1,0:T(8,128)(2,1)S(1)}, u32[]{:S(2)}, u32[]{:S(2)}) collective-permute-start(bf16[2,32,384]{2,1,0:T(8,128)(2,1)S(1)} %get-tuple-element.40), channel_id=1, source_target_pairs={{0,1},{1,0},{2,3},{3,2},{4,5},{5,4},{6,7},{7,6},{8,9},{9,8},{10,11... | collective-permute-start | bytes 147464 | tf_op jit(solution)/shard_map/ppermute | solution.py:511
  48.8 2.9 %collective-permute-start.8 = (bf16[2,32,384]{2,1,0:T(8,128)(2,1)S(1)}, bf16[2,32,384]{2,1,0:T(8,128)(2,1)S(1)}, u32[]{:S(2)}, u32[]{:S(2)}) collective-permute-start(bf16[2,32,384]{2,1,0:T(8,128)(2,1)S(1)} %edge.3), channel_id=1, source_target_pairs={{0,1},{1,0},{2,3},{3,2},{4,5},{5,4},{6,7},{7,6},{8,9},{9,8},{10,11... | collective-permute-start | bytes 147464 | tf_op jit(solution)/shard_map/ppermute | solution.py:567
  65.8 5.5 %collective-permute-start.10 = (f32[2,32,128]{2,1,0:T(8,128)S(1)}, f32[2,32,128]{2,1,0:T(8,128)S(1)}, u32[]{:S(2)}, u32[]{:S(2)}) collective-permute-start(f32[2,32,128]{2,1,0:T(8,128)S(1)} %get-tuple-element.46), channel_id=1, source_target_pairs={{0,112},{16,0},{32,16},{48,32},{64,48},{80,64},{96,80},{112,96},{1... | collective-permute-start | bytes 98312 | tf_op jit(solution)/shard_map/ppermute | solution.py:573

commit v6 on v5

--- a/solution.py
+++ b/solution.py
@@ -22,6 +22,9 @@
 
 
 WEIGHTS_COVER = pl.CostEstimate(flops=1 << 33, bytes_accessed=1 << 23, transcendentals=0)
+WEIGHTS_WINDOW = pl.CostEstimate(
+    flops=1 << 33, bytes_accessed=1 << 23, transcendentals=262000000
+)
 INPUTS_COVER = pl.CostEstimate(flops=1 << 31, bytes_accessed=1 << 20, transcendentals=0)
 HBM = [pl.BlockSpec(memory_space=pltpu.HBM)]
 
@@ -30,10 +33,6 @@
     return pl.CostEstimate(
         flops=2 * count * kernel.size, bytes_accessed=2 * kernel.size, transcendentals=0
     )
-
-
-def in_hbm(value):
-    return pltpu.with_memory_space_constraint(value, pltpu.HBM)
 
 
 def nt_dot(left, right, **kw):
@@ -171,27 +170,20 @@
         in_specs=vmem(6),
         out_specs=tuple(vmem(2)),
         compiler_params=pltpu.CompilerParams(vmem_limit_bytes=4 * MIB),
+        cost_estimate=WEIGHTS_WINDOW,
         name="gather",
     )(par, own, nxt, ra, rb, rbn)
 
 
-def conv_kernel(par_ref, part_ref, ran_ref, w_hbm, u_ref, ext, acc, w_ref, sems):
-    frames, rows, _ = ran_ref.shape
+def conv_kernel(par_ref, part_ref, ran_ref, w_ref, u_ref, ext, acc):
+    frames, rows = ran_ref.shape[:2]
     cols = part_ref.shape[1] - 2
-    copies = {}
-    for a in (2, 1, 0):
-        span = pl.ds(9 * a, 9)
-        copies[a] = pltpu.make_async_copy(w_hbm.at[span], w_ref.at[span], sems.at[a])
-        copies[a].start()
     even, _, later = flags(par_ref)
     ext[...] = part_ref[...]
     right, left = swapped(even, ran_ref[...] * later, jnp.zeros_like(ran_ref))
     ext[frames:, 0] = part_ref[frames:, 0] + left
     ext[frames:, cols + 1] = part_ref[frames:, cols + 1] + right
-    for a, copy in copies.items():
-        copy.wait()
-        part = time_taps(ext, w_ref, (a,), frames, cols)
-        acc[...] = part if a == 2 else acc[...] + part
+    acc[...] = time_taps(ext, w_ref, (2, 1, 0), frames, cols)
     u_ref[...] = row_taps(acc, rows)
 
 
@@ -202,18 +194,16 @@
     return pl.pallas_call(
         conv_kernel,
         out_shape=jax.ShapeDtypeStruct((count, channels), jnp.float32),
-        in_specs=vmem(3) + HBM,
+        in_specs=vmem(4),
         out_specs=vmem(1)[0],
         scratch_shapes=[
             pltpu.VMEM(part.shape, jnp.bfloat16),
             pltpu.VMEM((count, 3 * channels), jnp.float32),
-            pltpu.VMEM(kernel.shape, jnp.bfloat16),
-            pltpu.SemaphoreType.DMA((3,)),
         ],
         compiler_params=pltpu.CompilerParams(vmem_limit_bytes=16 * MIB),
         cost_estimate=matmul_cost(count, kernel),
         name="conv",
-    )(par, part, ran, in_hbm(kernel))
+    )(par, part, ran, kernel)
 
 
 def norm_stats(cells, frames, mom_ref):
@@ -561,7 +551,7 @@
     upstream = conv_section(par, part, ran, second_kernel)
     q, sums, stats = norm_section(upstream, second, mom, affine, cells, peers)
     grad, send_a, send_b = dx_section(par, grad, q, second, stats, everyone(sums), cells)
-    nxt = frames_on(grad)
+    nxt = jnp.concatenate([frames_on(grad[f : f + 1]) for f in range(frames)], axis=0)
     ra, rb, rbn = columns_on(send_a, send_b)
     (corner,) = edge_section(par, nxt, 1, None)
     ran = lax.ppermute(corner, "tile_2", SWAP)

time: 82.3 us -> 86.2 us (1.047)
  starting transfers between devices: 33.2 us -> 37.7 us
  local copies, waits for them, and re-layouts: 1.16 us -> 4.44 us
  Pallas kernels: 11.6 us -> 9.01 us
  blocking collectives: 30.6 us -> 29.3 us
    unnamed x22 -> x25, local copies, waits for them, and re-layouts: 0.05 us -> 3.33 us
    pallas_call x1, Pallas kernels: 5.18 us -> 2.62 us  [conv_section(): pl.pallas_call(conv_kernel, out_shape=jax.ShapeDtypeStruct((count, channe...]
    ppermute x2 -> x3, starting transfers between devices: 10.3 us -> 12.7 us  [frames_on(): return lax.ppermute(value, 'tm', routes()[0])]
    ppermute x2, starting transfers between devices: 6.89 us -> 8.47 us  [shards(): ran = lax.ppermute(corner, 'tile_2', SWAP)]
    all_to_all x3, blocking collectives: 30.6 us -> 29.3 us  [everyone(): return lax.all_to_all(rows, TILE, 0, 0)]
  transfers between devices with their start and end apart: 12 -> 13, of which waited for: 6 -> 5; matrix products, arithmetic and copies ran while one was open for 0% -> 0% of each run, Pallas kernels for 8% -> 4%
where the time goes in v6:
time: 86.2 us; the launch traced here: 85.5 us
  starting transfers between devices  37.7 us (44%)
  blocking collectives  29.3 us (34%)
  Pallas kernels  9.01 us (10%)
  waiting for transfers between devices  4.74 us (5%)
  local copies, waits for them, and re-layouts  4.44 us (5%)
    all_to_all x3, blocking collectives, everyone(): return lax.all_to_all(rows, TILE, 0, 0)  29.3 us
    ppermute x3, starting transfers between devices, frames_on(): return lax.ppermute(value, 'tm', routes()[0])  12.7 us
    ppermute x2, starting transfers between devices, shards(): ran = lax.ppermute(corner, 'tile_2', SWAP)  8.47 us
    ppermute x2, starting transfers between devices, columns_on(): ra = lax.ppermute(send_a, 'tile_2', SWAP)  6.26 us
    all_to_all x1, starting transfers between devices, everyone(): return lax.all_to_all(rows, TILE, 0, 0)  4.08 us
    ppermute x1, starting transfers between devices, shards(): own = own + jnp.where(later, lax.ppermute(prev, 'tm', ring(tms)), 0.0)  3.96 us
    unnamed x25, local copies, waits for them, and re-layouts  3.33 us
    pallas_call x1, Pallas kernels, conv_norm_section(): pl.pallas_call(conv_norm_kernel, out_shape=finish_shapes(stored, peers),...  2.71 us
  transfers between devices with their start and end apart: 13, of which 5 were waited for; matrix products, arithmetic and copies ran while one was open for 0% of the time, Pallas kernels for 4%

profile of v6, /device:TPU:1, one launch (start us, length us, event | category | flops | bytes accessed | tf_op | source)
XLA Modules:
  0.0 85.5 jit_solution(5582076893293860167)
XLA Ops:
  0.2 1.0 %copy.23 = bf16[2,32,4,384]{3,1,2,0:T(8,128)(2,1)S(1)} copy(bf16[2,32,4,384]{3,2,1,0:T(4,128)(2,1)} %param.14) | data formatting | bytes 393216 | tf_op jit(solution)/shard_map/optimization_barrier | solution.py:535
  1.1 6.0 %collective-permute-start = (bf16[2,32,4,384]{3,1,2,0:T(8,128)(2,1)S(1)}, bf16[2,32,4,384]{3,1,2,0:T(8,128)(2,1)S(1)}, u32[]{:S(2)}, u32[]{:S(2)}) collective-permute-start(bf16[2,32,4,384]{3,1,2,0:T(8,128)(2,1)S(1)} %copy.23), channel_id=1, source_target_pairs={{0,112},{16,0},{32,16},{48,32},{64,48},{80,64},{96,80},{112,96},{1... | collective-permute-start | bytes 589832 | tf_op jit(solution)/shard_map/ppermute | solution.py:494
  7.1 1.3 %collective-permute-start.2 = (bf16[2,32,384]{2,1,0:T(8,128)(2,1)S(1)}, bf16[2,32,384]{2,1,0:T(8,128)(2,1)S(1)}, u32[]{:S(2)}, u32[]{:S(2)}) collective-permute-start(bf16[2,32,384]{2,1,0:T(8,128)(2,1)S(1)} %get-tuple-element.29), channel_id=1, source_target_pairs={{1,2},{2,1},{3,4},{4,3},{5,6},{6,5},{7,8},{8,7},{9,10},{10,9},{11,... | collective-permute-start | bytes 147464 | tf_op jit(solution)/shard_map/ppermute | solution.py:499
  8.9 3.0 %collective-permute-start.1 = (bf16[2,32,384]{2,1,0:T(8,128)(2,1)S(1)}, bf16[2,32,384]{2,1,0:T(8,128)(2,1)S(1)}, u32[]{:S(2)}, u32[]{:S(2)}) collective-permute-start(bf16[2,32,384]{2,1,0:T(8,128)(2,1)S(1)} %get-tuple-element.28), channel_id=1, source_target_pairs={{0,1},{1,0},{2,3},{3,2},{4,5},{5,4},{6,7},{7,6},{8,9},{9,8},{10,11... | collective-permute-start | bytes 147464 | tf_op jit(solution)/shard_map/ppermute | solution.py:501
  11.9 1.6 %collective-permute-done.3.rbn_ref = bf16[2,32,384]{2,1,0:T(8,128)(2,1)S(1)} collective-permute-done((bf16[2,32,384]{2,1,0:T(8,128)(2,1)S(1)}, bf16[2,32,384]{2,1,0:T(8,128)(2,1)S(1)}, u32[]{:S(2)}, u32[]{:S(2)}) %collective-permute-start.3) | collective-permute-done | bytes 49184 | tf_op jit(solution)/shard_map/ppermute | solution.py:500
  13.7 4.9 %collective-permute-start.4 = (bf16[2,32,384]{2,1,0:T(8,128)(2,1)S(1)}, bf16[2,32,384]{2,1,0:T(8,128)(2,1)S(1)}, u32[]{:S(2)}, u32[]{:S(2)}) collective-permute-start(bf16[2,32,384]{2,1,0:T(8,128)(2,1)S(1)} %get-tuple-element.31), channel_id=1, source_target_pairs={{0,1},{1,0},{2,3},{3,2},{4,5},{5,4},{6,7},{7,6},{8,9},{9,8},{10,11... | collective-permute-start | bytes 147464 | tf_op jit(solution)/shard_map/ppermute | solution.py:549
  18.6 1.0 %moments.1 = (f32[16,8,384]{2,1,0:T(8,128)}, f32[4,384]{1,0:T(4,128)S(1)}) custom-call(bf16[2,32,4,384]{3,2,1,0:T(4,128)(2,1)S(1)} %copy-done.1, bf16[2,32,4,384]{3,2,1,0:T(4,128)(2,1)S(1)} %copy-done.2, f32[384]{0:T(512)S(1)} %copy-done.6, f32[384]{0:T(512)S(1)} %copy-done.7, f32[384]{0:T(512)S(1)} %copy-done.8, f32[384]{0:T(512)S(1)} %copy-done.9), custom_call_target="tpu_custom_call" | custom-call | tf_op jit(solution)/shard_map/moments/pallas_call | solution.py:83
  19.6 4.1 %all-to-all-start = ((f32[16,8,384]{2,1,0:T(8,128)}), f32[16,8,384]{2,1,0:T(8,128)S(1)}, u32[]{:S(2)}, u32[]{:S(2)}) async-start(f32[16,8,384]{2,1,0:T(8,128)} %get-tuple-element.34), calls=%async_computation | async-start | bytes 393216 | tf_op jit(solution)/shard_map/all_to_all | solution.py:510
  23.7 3.3 %copy-done = bf16[27,384,384]{2,1,0:T(8,128)(2,1)S(1)} copy-done((bf16[27,384,384]{2,1,0:T(8,128)(2,1)S(1)}, bf16[27,384,384]{2,1,0:T(8,128)(2,1)}, u32[]{:S(2)}) %copy-start) | copy-done | bytes 7962648
  27.0 2.6 %conv.1.u_ref = f32[256,384]{1,0:T(8,128)S(1)} custom-call(bf16[3,384]{1,0:T(4,128)(2,1)S(1)} %broadcast_in_dim.10.par_ref, bf16[4,6,32,384]{3,2,1,0:T(8,128)(2,1)S(1)} %get-tuple-element.30.part_ref, bf16[2,32,384]{2,1,0:T(8,128)(2,1)S(1)} %collective-permute-done.4.ran_ref, bf16[27,384,384]{2,1,0:T(8,128)(2,1)S(1)} %copy-done), custom_call_target="tpu_custom_call" | custom-call | flops 2038431744 | bytes 7962624 | tf_op jit(solution)/shard_map/conv/pallas_call | solution.py:194
  29.6 0.8 all-to-all-done.mom_ref
  30.8 10.9 %all_to_all.20.sums_ref = f32[16,4,384]{2,1,0:T(4,128)S(1)} all-to-all(f32[16,4,384]{2,1,0:T(4,128)S(1)} %get-tuple-element.38), channel_id=1, replica_groups=mesh['tm'=8,'tile_0'=4,'tile_1'=2,'tile_2'=2] {'tile_0','tile_1','tile_2'}, dimensions={0} | all-to-all | bytes 196608 | tf_op jit(solution)/shard_map/all_to_all | solution.py:510
  42.2 4.0 %collective-permute-start.5 = (bf16[1,4,32,384]{3,2,1,0:T(8,128)(2,1)S(1)}, bf16[1,4,32,384]{3,2,1,0:T(8,128)(2,1)S(1)}, u32[]{:S(2)}, u32[]{:S(2)}) collective-permute-start(bf16[1,4,32,384]{3,2,1,0:T(8,128)(2,1)S(1)} %get-tuple-element.48), channel_id=1, source_target_pairs={{0,112},{16,0},{32,16},{48,32},{64,48},{80,64},{96,80},{112,96},{1... | collective-permute-start | bytes 294920 | tf_op jit(solution)/shard_map/ppermute | solution.py:494
  46.6 2.8 %collective-permute-start.6 = (bf16[1,4,32,384]{3,2,1,0:T(8,128)(2,1)S(1)}, bf16[1,4,32,384]{3,2,1,0:T(8,128)(2,1)S(1)}, u32[]{:S(2)}, u32[]{:S(2)}) collective-permute-start(bf16[1,4,32,384]{3,2,1,0:T(8,128)(2,1)S(1)} %get-tuple-element.47), channel_id=1, source_target_pairs={{0,112},{16,0},{32,16},{48,32},{64,48},{80,64},{96,80},{112,96},{1... | collective-permute-start | bytes 294920 | tf_op jit(solution)/shard_map/ppermute | solution.py:494
  49.3 3.2 %collective-permute-start.7 = (bf16[2,32,384]{2,1,0:T(8,128)(2,1)S(1)}, bf16[2,32,384]{2,1,0:T(8,128)(2,1)S(1)}, u32[]{:S(2)}, u32[]{:S(2)}) collective-permute-start(bf16[2,32,384]{2,1,0:T(8,128)(2,1)S(1)} %get-tuple-element.40), channel_id=1, source_target_pairs={{0,1},{1,0},{2,3},{3,2},{4,5},{5,4},{6,7},{7,6},{8,9},{9,8},{10,11... | collective-permute-start | bytes 147464 | tf_op jit(solution)/shard_map/ppermute | solution.py:501
  53.1 3.6 %collective-permute-start.9 = (bf16[2,32,384]{2,1,0:T(8,128)(2,1)S(1)}, bf16[2,32,384]{2,1,0:T(8,128)(2,1)S(1)}, u32[]{:S(2)}, u32[]{:S(2)}) collective-permute-start(bf16[2,32,384]{2,1,0:T(8,128)(2,1)S(1)} %edge.3), channel_id=1, source_target_pairs={{0,1},{1,0},{2,3},{3,2},{4,5},{5,4},{6,7},{7,6},{8,9},{9,8},{10,11... | collective-permute-start | bytes 147464 | tf_op jit(solution)/shard_map/ppermute | solution.py:557
  56.8 0.8 collective-permute-done.9.ran_ref
  57.6 2.7 %convnorm.1 = (f32[2,4,32,384]{3,2,1,0:T(8,128)S(1)}, f32[16,4,384]{2,1,0:T(4,128)S(1)}) custom-call(bf16[3,384]{1,0:T(4,128)(2,1)S(1)} %broadcast_in_dim.10.par_ref, bf16[2,4,32,384]{3,2,1,0:T(8,128)(2,1)S(1)} %get-tuple-element.39.own_ref.grad_ref, bf16[2,4,32,384]{3,2,1,0:T(8,128)(2,1)S(1)} %constant_dynamic-update-slice_fusion.block_ref.next_ref, ...), custom_call_target="tpu_custom_call" | custom-call | flops 2038431744 | bytes 7962624 | tf_op jit(solution)/shard_map/convnorm/pallas_call | solution.py:336
  60.4 8.7 %all_to_all.21.sums_ref = f32[16,4,384]{2,1,0:T(4,128)S(1)} all-to-all(f32[16,4,384]{2,1,0:T(4,128)S(1)} %get-tuple-element.43), channel_id=1, replica_groups=mesh['tm'=8,'tile_0'=4,'tile_1'=2,'tile_2'=2] {'tile_0','tile_1','tile_2'}, dimensions={0} | all-to-all | bytes 196608 | tf_op jit(solution)/shard_map/all_to_all | solution.py:510
  69.0 0.7 latent.1
  69.7 4.0 %collective-permute-start.11 = (f32[2,32,128]{2,1,0:T(8,128)S(1)}, f32[2,32,128]{2,1,0:T(8,128)S(1)}, u32[]{:S(2)}, u32[]{:S(2)}) collective-permute-start(f32[2,32,128]{2,1,0:T(8,128)S(1)} %get-tuple-element.46), channel_id=1, source_target_pairs={{0,112},{16,0},{32,16},{48,32},{64,48},{80,64},{96,80},{112,96},{1... | collective-permute-start | bytes 98312 | tf_op jit(solution)/shard_map/ppermute | solution.py:563
  73.7 1.0 %collective-permute-done.11 = f32[2,32,128]{2,1,0:T(8,128)S(1)} collective-permute-done((f32[2,32,128]{2,1,0:T(8,128)S(1)}, f32[2,32,128]{2,1,0:T(8,128)S(1)}, u32[]{:S(2)}, u32[]{:S(2)}) %collective-permute-start.11) | collective-permute-done | bytes 32800 | tf_op jit(solution)/shard_map/ppermute | solution.py:563
  74.7 9.7 %all_to_all.22.got_ref = f32[16,4,128]{2,1,0:T(4,128)S(1)} all-to-all(f32[16,4,128]{2,1,0:T(4,128)S(1)} %bitcast.23), channel_id=1, replica_groups=mesh['tm'=8,'tile_0'=4,'tile_1'=2,'tile_2'=2] {'tile_0','tile_1','tile_2'}, dimensions={0} | all-to-all | bytes 65536 | tf_op jit(solution)/shard_map/all_to_all | solution.py:510
  84.4 1.1 %assemble.1 = f32[64,64]{1,0:T(8,128)} custom-call(f32[16,4,128]{2,1,0:T(4,128)S(1)} %all_to_all.22.got_ref, bf16[96,768]{1,0:T(8,128)(2,1)S(1)} %copy-done.4, bf16[64,192]{1,0:T(8,128)(2,1)S(1)} %copy-done.5), custom_call_target="tpu_custom_call" | custom-call | tf_op jit(solution)/shard_map/assemble/pallas_call | solution.py:470
  (49 shorter events, 2.7 us)
Async XLA Ops:
  1.1 12.4 %collective-permute-start = (bf16[2,32,4,384]{3,1,2,0:T(8,128)(2,1)S(1)}, bf16[2,32,4,384]{3,1,2,0:T(8,128)(2,1)S(1)}, u32[]{:S(2)}, u32[]{:S(2)}) collective-permute-start(bf16[2,32,4,384]{3,1,2,0:T(8,128)(2,1)S(1)} %copy.23), channel_id=1, source_target_pairs={{0,112},{16,0},{32,16},{48,32},{64,48},{80,64},{96,80},{112,96},{1... | collective-permute-start | bytes 589832 | tf_op jit(solution)/shard_map/ppermute | solution.py:494
  7.1 4.8 %collective-permute-start.2 = (bf16[2,32,384]{2,1,0:T(8,128)(2,1)S(1)}, bf16[2,32,384]{2,1,0:T(8,128)(2,1)S(1)}, u32[]{:S(2)}, u32[]{:S(2)}) collective-permute-start(bf16[2,32,384]{2,1,0:T(8,128)(2,1)S(1)} %get-tuple-element.29), channel_id=1, source_target_pairs={{1,2},{2,1},{3,4},{4,3},{5,6},{6,5},{7,8},{8,7},{9,10},{10,9},{11,... | collective-permute-start | bytes 147464 | tf_op jit(solution)/shard_map/ppermute | solution.py:499
  8.4 5.1 %collective-permute-start.3 = (bf16[2,32,384]{2,1,0:T(8,128)(2,1)S(1)}, bf16[2,32,384]{2,1,0:T(8,128)(2,1)S(1)}, u32[]{:S(2)}, u32[]{:S(2)}) collective-permute-start(bf16[2,32,384]{2,1,0:T(8,128)(2,1)S(1)} %get-tuple-element.29), channel_id=1, source_target_pairs={{1,114},{2,113},{3,116},{4,115},{5,118},{6,117},{7,120},{8,119},{9... | collective-permute-start | bytes 147464 | tf_op jit(solution)/shard_map/ppermute | solution.py:500
  8.9 4.6 %collective-permute-start.1 = (bf16[2,32,384]{2,1,0:T(8,128)(2,1)S(1)}, bf16[2,32,384]{2,1,0:T(8,128)(2,1)S(1)}, u32[]{:S(2)}, u32[]{:S(2)}) collective-permute-start(bf16[2,32,384]{2,1,0:T(8,128)(2,1)S(1)} %get-tuple-element.28), channel_id=1, source_target_pairs={{0,1},{1,0},{2,3},{3,2},{4,5},{5,4},{6,7},{7,6},{8,9},{9,8},{10,11... | collective-permute-start | bytes 147464 | tf_op jit(solution)/shard_map/ppermute | solution.py:501
  13.5 5.0 %copy-start.1 = (bf16[2,32,4,384]{3,2,1,0:T(4,128)(2,1)S(1)}, bf16[2,32,4,384]{3,2,1,0:T(4,128)(2,1)}, u32[]{:S(2)}) copy-start(bf16[2,32,4,384]{3,2,1,0:T(4,128)(2,1)} %second_ref) | copy-start | bytes 589828
  13.5 5.0 %copy-start.2 = (bf16[2,32,4,384]{3,2,1,0:T(4,128)(2,1)S(1)}, bf16[2,32,4,384]{3,2,1,0:T(4,128)(2,1)}, u32[]{:S(2)}) copy-start(bf16[2,32,4,384]{3,2,1,0:T(4,128)(2,1)} %first_ref) | copy-start | bytes 589828
  13.6 5.0 %copy-start.6 = (f32[384]{0:T(512)S(1)}, f32[384]{0:T(512)}, u32[]{:S(2)}) copy-start(f32[384]{0:T(512)} %refs_0_.1) | copy-start | bytes 4612
  13.6 5.0 %copy-start.7 = (f32[384]{0:T(512)S(1)}, f32[384]{0:T(512)}, u32[]{:S(2)}) copy-start(f32[384]{0:T(512)} %refs_1_.1) | copy-start | bytes 4612
  13.6 5.0 %copy-start.8 = (f32[384]{0:T(512)S(1)}, f32[384]{0:T(512)}, u32[]{:S(2)}) copy-start(f32[384]{0:T(512)} %refs_2_.1) | copy-start | bytes 4612
  13.6 5.0 %copy-start.9 = (f32[384]{0:T(512)S(1)}, f32[384]{0:T(512)}, u32[]{:S(2)}) copy-start(f32[384]{0:T(512)} %refs_3_.1) | copy-start | bytes 4612
  13.7 10.0 %collective-permute-start.4 = (bf16[2,32,384]{2,1,0:T(8,128)(2,1)S(1)}, bf16[2,32,384]{2,1,0:T(8,128)(2,1)S(1)}, u32[]{:S(2)}, u32[]{:S(2)}) collective-permute-start(bf16[2,32,384]{2,1,0:T(8,128)(2,1)S(1)} %get-tuple-element.31), channel_id=1, source_target_pairs={{0,1},{1,0},{2,3},{3,2},{4,5},{5,4},{6,7},{7,6},{8,9},{9,8},{10,11... | collective-permute-start | bytes 147464 | tf_op jit(solution)/shard_map/ppermute | solution.py:549
  19.6 10.8 %all-to-all-start = ((f32[16,8,384]{2,1,0:T(8,128)}), f32[16,8,384]{2,1,0:T(8,128)S(1)}, u32[]{:S(2)}, u32[]{:S(2)}) async-start(f32[16,8,384]{2,1,0:T(8,128)} %get-tuple-element.34), calls=%async_computation | async-start | bytes 393216 | tf_op jit(solution)/shard_map/all_to_all | solution.py:510
  30.4 27.3 %slice-start = ((s8[7962624]{0:T(1024)(128)(4,1)}), s8[4194304]{0:T(1024)(128)(4,1)S(1)}, s32[]{:S(2)}) async-start(s8[7962624]{0:T(1024)(128)(4,1)} %bitcast.13), calls=%async_computation.4 | async-start | bytes 8388608
  41.8 15.9 %slice-start.1 = ((s8[7962624]{0:T(1024)(128)(4,1)}), s8[3768320]{0:T(1024)(128)(4,1)S(1)}, s32[]{:S(2)}) async-start(s8[7962624]{0:T(1024)(128)(4,1)} %bitcast.13), calls=%async_computation.5 | async-start | bytes 7536640
  42.1 26.9 %copy-start.3 = (bf16[27,16,384]{2,1,0:T(8,128)(2,1)S(1)}, bf16[27,16,384]{2,1,0:T(8,128)(2,1)}, u32[]{:S(2)}) copy-start(bf16[27,16,384]{2,1,0:T(8,128)(2,1)} %k_ref.1) | copy-start | bytes 995332
  42.1 42.3 %copy-start.4 = (bf16[96,768]{1,0:T(8,128)(2,1)S(1)}, bf16[96,768]{1,0:T(8,128)(2,1)}, u32[]{:S(2)}) copy-start(bf16[96,768]{1,0:T(8,128)(2,1)} %constant.33.clone.e_ref) | copy-start | bytes 442372
  42.1 42.3 %copy-start.5 = (bf16[64,192]{1,0:T(8,128)(2,1)S(1)}, bf16[64,192]{1,0:T(8,128)(2,1)}, u32[]{:S(2)}) copy-start(bf16[64,192]{1,0:T(8,128)(2,1)} %constant.34.clone.perm_ref) | copy-start | bytes 73732
  42.2 10.4 %collective-permute-start.5 = (bf16[1,4,32,384]{3,2,1,0:T(8,128)(2,1)S(1)}, bf16[1,4,32,384]{3,2,1,0:T(8,128)(2,1)S(1)}, u32[]{:S(2)}, u32[]{:S(2)}) collective-permute-start(bf16[1,4,32,384]{3,2,1,0:T(8,128)(2,1)S(1)} %get-tuple-element.48), channel_id=1, source_target_pairs={{0,112},{16,0},{32,16},{48,32},{64,48},{80,64},{96,80},{112,96},{1... | collective-permute-start | bytes 294920 | tf_op jit(solution)/shard_map/ppermute | solution.py:494
  46.1 10.6 %collective-permute-start.10 = (bf16[2,32,384]{2,1,0:T(8,128)(2,1)S(1)}, bf16[2,32,384]{2,1,0:T(8,128)(2,1)S(1)}, u32[]{:S(2)}, u32[]{:S(2)}) collective-permute-start(bf16[2,32,384]{2,1,0:T(8,128)(2,1)S(1)} %get-tuple-element.41), channel_id=1, source_target_pairs={{1,114},{2,113},{3,116},{4,115},{5,118},{6,117},{7,120},{8,119},{9... | collective-permute-start | bytes 147464 | tf_op jit(solution)/shard_map/ppermute | solution.py:500
  46.1 10.7 %collective-permute-start.8 = (bf16[2,32,384]{2,1,0:T(8,128)(2,1)S(1)}, bf16[2,32,384]{2,1,0:T(8,128)(2,1)S(1)}, u32[]{:S(2)}, u32[]{:S(2)}) collective-permute-start(bf16[2,32,384]{2,1,0:T(8,128)(2,1)S(1)} %get-tuple-element.41), channel_id=1, source_target_pairs={{1,2},{2,1},{3,4},{4,3},{5,6},{6,5},{7,8},{8,7},{9,10},{10,9},{11,... | collective-permute-start | bytes 147464 | tf_op jit(solution)/shard_map/ppermute | solution.py:499
  46.6 6.5 %collective-permute-start.6 = (bf16[1,4,32,384]{3,2,1,0:T(8,128)(2,1)S(1)}, bf16[1,4,32,384]{3,2,1,0:T(8,128)(2,1)S(1)}, u32[]{:S(2)}, u32[]{:S(2)}) collective-permute-start(bf16[1,4,32,384]{3,2,1,0:T(8,128)(2,1)S(1)} %get-tuple-element.47), channel_id=1, source_target_pairs={{0,112},{16,0},{32,16},{48,32},{64,48},{80,64},{96,80},{112,96},{1... | collective-permute-start | bytes 294920 | tf_op jit(solution)/shard_map/ppermute | solution.py:494
  49.3 7.5 %collective-permute-start.7 = (bf16[2,32,384]{2,1,0:T(8,128)(2,1)S(1)}, bf16[2,32,384]{2,1,0:T(8,128)(2,1)S(1)}, u32[]{:S(2)}, u32[]{:S(2)}) collective-permute-start(bf16[2,32,384]{2,1,0:T(8,128)(2,1)S(1)} %get-tuple-element.40), channel_id=1, source_target_pairs={{0,1},{1,0},{2,3},{3,2},{4,5},{5,4},{6,7},{7,6},{8,9},{9,8},{10,11... | collective-permute-start | bytes 147464 | tf_op jit(solution)/shard_map/ppermute | solution.py:501
  53.1 4.5 %collective-permute-start.9 = (bf16[2,32,384]{2,1,0:T(8,128)(2,1)S(1)}, bf16[2,32,384]{2,1,0:T(8,128)(2,1)S(1)}, u32[]{:S(2)}, u32[]{:S(2)}) collective-permute-start(bf16[2,32,384]{2,1,0:T(8,128)(2,1)S(1)} %edge.3), channel_id=1, source_target_pairs={{0,1},{1,0},{2,3},{3,2},{4,5},{5,4},{6,7},{7,6},{8,9},{9,8},{10,11... | collective-permute-start | bytes 147464 | tf_op jit(solution)/shard_map/ppermute | solution.py:557
  69.7 5.0 %collective-permute-start.11 = (f32[2,32,128]{2,1,0:T(8,128)S(1)}, f32[2,32,128]{2,1,0:T(8,128)S(1)}, u32[]{:S(2)}, u32[]{:S(2)}) collective-permute-start(f32[2,32,128]{2,1,0:T(8,128)S(1)} %get-tuple-element.46), channel_id=1, source_target_pairs={{0,112},{16,0},{32,16},{48,32},{64,48},{80,64},{96,80},{112,96},{1... | collective-permute-start | bytes 98312 | tf_op jit(solution)/shard_map/ppermute | solution.py:563
  (1 other events, 3.3 us)

commit v7 on v6

--- a/solution.py
+++ b/solution.py
@@ -535,15 +535,14 @@
     par, later, output_grad, second_input, first_input = lax.optimization_barrier(
         (par, later, output_grad, second_input, first_input)
     )
-    turn = lambda x: with_layout_constraint(
-        jnp.transpose(x, (0, 2, 1, 3)), Layout(major_to_minor=(0, 1, 2, 3))
-    )
+    plain = lambda x: with_layout_constraint(x, Layout(major_to_minor=(0, 1, 2, 3)))
+    turn = lambda x: plain(jnp.transpose(x, (0, 2, 1, 3)))
 
     grad = turn(output_grad)
     vectors = (second_gain, second_shift, first_gain, first_shift)
     mine, affine = moments(second_input, first_input, vectors, peers)
     mom = everyone(mine)
-    nxt = turn(frames_on(output_grad))
+    nxt = turn(plain(frames_on(plain(output_grad))))
     ra, rb, rbn = columns_on(*edge_section(par, grad, 2, INPUTS_COVER))
     part, corner = gather_section(par, grad, nxt, ra, rb, rbn)
     ran = lax.ppermute(corner, "tile_2", SWAP)
@@ -551,7 +550,7 @@
     upstream = conv_section(par, part, ran, second_kernel)
     q, sums, stats = norm_section(upstream, second, mom, affine, cells, peers)
     grad, send_a, send_b = dx_section(par, grad, q, second, stats, everyone(sums), cells)
-    nxt = jnp.concatenate([frames_on(grad[f : f + 1]) for f in range(frames)], axis=0)
+    nxt = frames_on(grad)
     ra, rb, rbn = columns_on(send_a, send_b)
     (corner,) = edge_section(par, nxt, 1, None)
     ran = lax.ppermute(corner, "tile_2", SWAP)

time: 86.2 us -> 82.9 us (0.962)
  starting transfers between devices: 37.7 us -> 33.3 us
  blocking collectives: 29.3 us -> 30.9 us
    ppermute x3 -> x2, starting transfers between devices: 12.7 us -> 9.44 us  [frames_on(): return lax.ppermute(value, 'tm', routes()[0])]
    all_to_all x3, blocking collectives: 29.3 us -> 30.9 us  [everyone(): return lax.all_to_all(rows, TILE, 0, 0)]
    ppermute x2, starting transfers between devices: 8.47 us -> 6.99 us  [shards(): ran = lax.ppermute(corner, 'tile_2', SWAP)]
    unnamed x25 -> x24, local copies, waits for them, and re-layouts: 3.33 us -> 3.31 us
  transfers between devices with their start and end apart: 13 -> 12, of which waited for: 5 -> 6; matrix products, arithmetic and copies ran while one was open for 0% -> 1% of each run, Pallas kernels for 4% -> 4%
where the time goes in v7:
time: 82.9 us; the launch traced here: 82.5 us
  starting transfers between devices  33.3 us (40%)
  blocking collectives  30.9 us (37%)
  Pallas kernels  9.01 us (11%)
  waiting for transfers between devices  4.61 us (6%)
  local copies, waits for them, and re-layouts  4.44 us (5%)
    all_to_all x3, blocking collectives, everyone(): return lax.all_to_all(rows, TILE, 0, 0)  30.9 us
    ppermute x2, starting transfers between devices, frames_on(): return lax.ppermute(value, 'tm', routes()[0])  9.44 us
    ppermute x2, starting transfers between devices, shards(): ran = lax.ppermute(corner, 'tile_2', SWAP)  6.99 us
    ppermute x2, starting transfers between devices, columns_on(): ra = lax.ppermute(send_a, 'tile_2', SWAP)  5.91 us
    ppermute x1, starting transfers between devices, shards(): own = own + jnp.where(later, lax.ppermute(prev, 'tm', ring(tms)), 0.0)  4.43 us
    all_to_all x1, starting transfers between devices, everyone(): return lax.all_to_all(rows, TILE, 0, 0)  4.09 us
    unnamed x24, local copies, waits for them, and re-layouts  3.31 us
    pallas_call x1, Pallas kernels, conv_norm_section(): pl.pallas_call(conv_norm_kernel, out_shape=finish_shapes(stored, peers),...  2.71 us
  transfers between devices with their start and end apart: 12, of which 6 were waited for; matrix products, arithmetic and copies ran while one was open for 1% of the time, Pallas kernels for 4%

profile of v7, /device:TPU:1, one launch (start us, length us, event | category | flops | bytes accessed | tf_op | source)
XLA Modules:
  0.0 82.5 jit_solution(18177042353019517615)
XLA Ops:
  0.2 5.9 %collective-permute-start = (bf16[2,32,4,384]{3,2,1,0:T(4,128)(2,1)}, bf16[2,32,4,384]{3,2,1,0:T(4,128)(2,1)S(1)}, u32[]{:S(2)}, u32[]{:S(2)}) collective-permute-start(bf16[2,32,4,384]{3,2,1,0:T(4,128)(2,1)} %param.14), channel_id=1, source_target_pairs={{0,112},{16,0},{32,16},{48,32},{64,48},{80,64},{96,80},{112,96},{1... | collective-permute-start | bytes 589832 | tf_op jit(solution)/shard_map/ppermute | solution.py:494
  6.1 1.0 %copy.24 = bf16[2,32,4,384]{3,1,2,0:T(8,128)(2,1)S(1)} copy(bf16[2,32,4,384]{3,2,1,0:T(4,128)(2,1)} %param.14) | data formatting | bytes 393216 | tf_op jit(solution)/shard_map/optimization_barrier | solution.py:535
  7.1 1.3 %collective-permute-start.2 = (bf16[2,32,384]{2,1,0:T(8,128)(2,1)S(1)}, bf16[2,32,384]{2,1,0:T(8,128)(2,1)S(1)}, u32[]{:S(2)}, u32[]{:S(2)}) collective-permute-start(bf16[2,32,384]{2,1,0:T(8,128)(2,1)S(1)} %get-tuple-element.29), channel_id=1, source_target_pairs={{1,2},{2,1},{3,4},{4,3},{5,6},{6,5},{7,8},{8,7},{9,10},{10,9},{11,... | collective-permute-start | bytes 147464 | tf_op jit(solution)/shard_map/ppermute | solution.py:499
  8.4 0.5 collective-permute-start.3
  8.9 3.0 %collective-permute-start.1 = (bf16[2,32,384]{2,1,0:T(8,128)(2,1)S(1)}, bf16[2,32,384]{2,1,0:T(8,128)(2,1)S(1)}, u32[]{:S(2)}, u32[]{:S(2)}) collective-permute-start(bf16[2,32,384]{2,1,0:T(8,128)(2,1)S(1)} %get-tuple-element.28), channel_id=1, source_target_pairs={{0,1},{1,0},{2,3},{3,2},{4,5},{5,4},{6,7},{7,6},{8,9},{9,8},{10,11... | collective-permute-start | bytes 147464 | tf_op jit(solution)/shard_map/ppermute | solution.py:501
  12.0 1.6 %collective-permute-done.3.rbn_ref = bf16[2,32,384]{2,1,0:T(8,128)(2,1)S(1)} collective-permute-done((bf16[2,32,384]{2,1,0:T(8,128)(2,1)S(1)}, bf16[2,32,384]{2,1,0:T(8,128)(2,1)S(1)}, u32[]{:S(2)}, u32[]{:S(2)}) %collective-permute-start.3) | collective-permute-done | bytes 49184 | tf_op jit(solution)/shard_map/ppermute | solution.py:500
  13.6 4.9 %collective-permute-start.4 = (bf16[2,32,384]{2,1,0:T(8,128)(2,1)S(1)}, bf16[2,32,384]{2,1,0:T(8,128)(2,1)S(1)}, u32[]{:S(2)}, u32[]{:S(2)}) collective-permute-start(bf16[2,32,384]{2,1,0:T(8,128)(2,1)S(1)} %get-tuple-element.31), channel_id=1, source_target_pairs={{0,1},{1,0},{2,3},{3,2},{4,5},{5,4},{6,7},{7,6},{8,9},{9,8},{10,11... | collective-permute-start | bytes 147464 | tf_op jit(solution)/shard_map/ppermute | solution.py:548
  18.5 1.0 %moments.1 = (f32[16,8,384]{2,1,0:T(8,128)}, f32[4,384]{1,0:T(4,128)S(1)}) custom-call(bf16[2,32,4,384]{3,2,1,0:T(4,128)(2,1)S(1)} %copy-done.1, bf16[2,32,4,384]{3,2,1,0:T(4,128)(2,1)S(1)} %copy-done.2, f32[384]{0:T(512)S(1)} %copy-done.6, f32[384]{0:T(512)S(1)} %copy-done.7, f32[384]{0:T(512)S(1)} %copy-done.8, f32[384]{0:T(512)S(1)} %copy-done.9), custom_call_target="tpu_custom_call" | custom-call | tf_op jit(solution)/shard_map/moments/pallas_call | solution.py:83
  19.6 4.1 %all-to-all-start = ((f32[16,8,384]{2,1,0:T(8,128)}), f32[16,8,384]{2,1,0:T(8,128)S(1)}, u32[]{:S(2)}, u32[]{:S(2)}) async-start(f32[16,8,384]{2,1,0:T(8,128)} %get-tuple-element.34), calls=%async_computation | async-start | bytes 393216 | tf_op jit(solution)/shard_map/all_to_all | solution.py:510
  23.7 3.3 %copy-done = bf16[27,384,384]{2,1,0:T(8,128)(2,1)S(1)} copy-done((bf16[27,384,384]{2,1,0:T(8,128)(2,1)S(1)}, bf16[27,384,384]{2,1,0:T(8,128)(2,1)}, u32[]{:S(2)}) %copy-start) | copy-done | bytes 7962648
  26.9 2.6 %conv.1.u_ref = f32[256,384]{1,0:T(8,128)S(1)} custom-call(bf16[3,384]{1,0:T(4,128)(2,1)S(1)} %broadcast_in_dim.10.par_ref, bf16[4,6,32,384]{3,2,1,0:T(8,128)(2,1)S(1)} %get-tuple-element.30.part_ref, bf16[2,32,384]{2,1,0:T(8,128)(2,1)S(1)} %collective-permute-done.4.ran_ref, bf16[27,384,384]{2,1,0:T(8,128)(2,1)S(1)} %copy-done), custom_call_target="tpu_custom_call" | custom-call | flops 2038431744 | bytes 7962624 | tf_op jit(solution)/shard_map/conv/pallas_call | solution.py:194
  29.6 0.8 all-to-all-done.mom_ref
  30.8 10.9 %all_to_all.20.sums_ref = f32[16,4,384]{2,1,0:T(4,128)S(1)} all-to-all(f32[16,4,384]{2,1,0:T(4,128)S(1)} %get-tuple-element.38), channel_id=1, replica_groups=mesh['tm'=8,'tile_0'=4,'tile_1'=2,'tile_2'=2] {'tile_0','tile_1','tile_2'}, dimensions={0} | all-to-all | bytes 196608 | tf_op jit(solution)/shard_map/all_to_all | solution.py:510
  42.1 3.5 %collective-permute-start.5 = (bf16[2,4,32,384]{3,2,1,0:T(8,128)(2,1)S(1)}, bf16[2,4,32,384]{3,2,1,0:T(8,128)(2,1)S(1)}, u32[]{:S(2)}, u32[]{:S(2)}) collective-permute-start(bf16[2,4,32,384]{3,2,1,0:T(8,128)(2,1)S(1)} %get-tuple-element.39.own_ref.grad_ref), channel_id=1, source_target_pairs={{0,112},{16,0},{32,16},{48,32},{64,48},{80,64},{96,80},{112,96},{1... | collective-permute-start | bytes 589832 | tf_op jit(solution)/shard_map/ppermute | solution.py:494
  46.3 2.9 %collective-permute-start.6 = (bf16[2,32,384]{2,1,0:T(8,128)(2,1)S(1)}, bf16[2,32,384]{2,1,0:T(8,128)(2,1)S(1)}, u32[]{:S(2)}, u32[]{:S(2)}) collective-permute-start(bf16[2,32,384]{2,1,0:T(8,128)(2,1)S(1)} %get-tuple-element.40), channel_id=1, source_target_pairs={{0,1},{1,0},{2,3},{3,2},{4,5},{5,4},{6,7},{7,6},{8,9},{9,8},{10,11... | collective-permute-start | bytes 147464 | tf_op jit(solution)/shard_map/ppermute | solution.py:501
  49.6 2.1 %collective-permute-start.8 = (bf16[2,32,384]{2,1,0:T(8,128)(2,1)S(1)}, bf16[2,32,384]{2,1,0:T(8,128)(2,1)S(1)}, u32[]{:S(2)}, u32[]{:S(2)}) collective-permute-start(bf16[2,32,384]{2,1,0:T(8,128)(2,1)S(1)} %edge.3), channel_id=1, source_target_pairs={{0,1},{1,0},{2,3},{3,2},{4,5},{5,4},{6,7},{7,6},{8,9},{9,8},{10,11... | collective-permute-start | bytes 147464 | tf_op jit(solution)/shard_map/ppermute | solution.py:556
  52.1 0.5 collective-permute-done.8.ran_ref
  52.6 2.7 %convnorm.1 = (f32[2,4,32,384]{3,2,1,0:T(8,128)S(1)}, f32[16,4,384]{2,1,0:T(4,128)S(1)}) custom-call(bf16[3,384]{1,0:T(4,128)(2,1)S(1)} %broadcast_in_dim.10.par_ref, bf16[2,4,32,384]{3,2,1,0:T(8,128)(2,1)S(1)} %get-tuple-element.39.own_ref.grad_ref, bf16[2,4,32,384]{3,2,1,0:T(8,128)(2,1)S(1)} %collective-permute-done.5.block_ref.next_ref, ...), custom_call_target="tpu_custom_call" | custom-call | flops 2038431744 | bytes 7962624 | tf_op jit(solution)/shard_map/convnorm/pallas_call | solution.py:336
  55.3 10.3 %all_to_all.21.sums_ref = f32[16,4,384]{2,1,0:T(4,128)S(1)} all-to-all(f32[16,4,384]{2,1,0:T(4,128)S(1)} %get-tuple-element.43), channel_id=1, replica_groups=mesh['tm'=8,'tile_0'=4,'tile_1'=2,'tile_2'=2] {'tile_0','tile_1','tile_2'}, dimensions={0} | all-to-all | bytes 196608 | tf_op jit(solution)/shard_map/all_to_all | solution.py:510
  65.6 0.7 latent.1
  66.3 4.4 %collective-permute-start.10 = (f32[2,32,128]{2,1,0:T(8,128)S(1)}, f32[2,32,128]{2,1,0:T(8,128)S(1)}, u32[]{:S(2)}, u32[]{:S(2)}) collective-permute-start(f32[2,32,128]{2,1,0:T(8,128)S(1)} %get-tuple-element.46), channel_id=1, source_target_pairs={{0,112},{16,0},{32,16},{48,32},{64,48},{80,64},{96,80},{112,96},{1... | collective-permute-start | bytes 98312 | tf_op jit(solution)/shard_map/ppermute | solution.py:562
  70.8 1.0 %collective-permute-done.10 = f32[2,32,128]{2,1,0:T(8,128)S(1)} collective-permute-done((f32[2,32,128]{2,1,0:T(8,128)S(1)}, f32[2,32,128]{2,1,0:T(8,128)S(1)}, u32[]{:S(2)}, u32[]{:S(2)}) %collective-permute-start.10) | collective-permute-done | bytes 32800 | tf_op jit(solution)/shard_map/ppermute | solution.py:562
  71.8 9.7 %all_to_all.22.got_ref = f32[16,4,128]{2,1,0:T(4,128)S(1)} all-to-all(f32[16,4,128]{2,1,0:T(4,128)S(1)} %bitcast.26), channel_id=1, replica_groups=mesh['tm'=8,'tile_0'=4,'tile_1'=2,'tile_2'=2] {'tile_0','tile_1','tile_2'}, dimensions={0} | all-to-all | bytes 65536 | tf_op jit(solution)/shard_map/all_to_all | solution.py:510
  81.5 1.1 %assemble.1 = f32[64,64]{1,0:T(8,128)} custom-call(f32[16,4,128]{2,1,0:T(4,128)S(1)} %all_to_all.22.got_ref, bf16[96,768]{1,0:T(8,128)(2,1)S(1)} %copy-done.4, bf16[64,192]{1,0:T(8,128)(2,1)S(1)} %copy-done.5), custom_call_target="tpu_custom_call" | custom-call | tf_op jit(solution)/shard_map/assemble/pallas_call | solution.py:470
  (45 shorter events, 2.6 us)
Async XLA Ops:
  0.2 11.8 %collective-permute-start = (bf16[2,32,4,384]{3,2,1,0:T(4,128)(2,1)}, bf16[2,32,4,384]{3,2,1,0:T(4,128)(2,1)S(1)}, u32[]{:S(2)}, u32[]{:S(2)}) collective-permute-start(bf16[2,32,4,384]{3,2,1,0:T(4,128)(2,1)} %param.14), channel_id=1, source_target_pairs={{0,112},{16,0},{32,16},{48,32},{64,48},{80,64},{96,80},{112,96},{1... | collective-permute-start | bytes 589832 | tf_op jit(solution)/shard_map/ppermute | solution.py:494
  7.1 4.8 %collective-permute-start.2 = (bf16[2,32,384]{2,1,0:T(8,128)(2,1)S(1)}, bf16[2,32,384]{2,1,0:T(8,128)(2,1)S(1)}, u32[]{:S(2)}, u32[]{:S(2)}) collective-permute-start(bf16[2,32,384]{2,1,0:T(8,128)(2,1)S(1)} %get-tuple-element.29), channel_id=1, source_target_pairs={{1,2},{2,1},{3,4},{4,3},{5,6},{6,5},{7,8},{8,7},{9,10},{10,9},{11,... | collective-permute-start | bytes 147464 | tf_op jit(solution)/shard_map/ppermute | solution.py:499
  8.4 5.1 %collective-permute-start.3 = (bf16[2,32,384]{2,1,0:T(8,128)(2,1)S(1)}, bf16[2,32,384]{2,1,0:T(8,128)(2,1)S(1)}, u32[]{:S(2)}, u32[]{:S(2)}) collective-permute-start(bf16[2,32,384]{2,1,0:T(8,128)(2,1)S(1)} %get-tuple-element.29), channel_id=1, source_target_pairs={{1,114},{2,113},{3,116},{4,115},{5,118},{6,117},{7,120},{8,119},{9... | collective-permute-start | bytes 147464 | tf_op jit(solution)/shard_map/ppermute | solution.py:500
  8.9 4.6 %collective-permute-start.1 = (bf16[2,32,384]{2,1,0:T(8,128)(2,1)S(1)}, bf16[2,32,384]{2,1,0:T(8,128)(2,1)S(1)}, u32[]{:S(2)}, u32[]{:S(2)}) collective-permute-start(bf16[2,32,384]{2,1,0:T(8,128)(2,1)S(1)} %get-tuple-element.28), channel_id=1, source_target_pairs={{0,1},{1,0},{2,3},{3,2},{4,5},{5,4},{6,7},{7,6},{8,9},{9,8},{10,11... | collective-permute-start | bytes 147464 | tf_op jit(solution)/shard_map/ppermute | solution.py:501
  13.5 5.0 %copy-start.1 = (bf16[2,32,4,384]{3,2,1,0:T(4,128)(2,1)S(1)}, bf16[2,32,4,384]{3,2,1,0:T(4,128)(2,1)}, u32[]{:S(2)}) copy-start(bf16[2,32,4,384]{3,2,1,0:T(4,128)(2,1)} %second_ref) | copy-start | bytes 589828
  13.5 5.0 %copy-start.2 = (bf16[2,32,4,384]{3,2,1,0:T(4,128)(2,1)S(1)}, bf16[2,32,4,384]{3,2,1,0:T(4,128)(2,1)}, u32[]{:S(2)}) copy-start(bf16[2,32,4,384]{3,2,1,0:T(4,128)(2,1)} %first_ref) | copy-start | bytes 589828
  13.5 5.0 %copy-start.6 = (f32[384]{0:T(512)S(1)}, f32[384]{0:T(512)}, u32[]{:S(2)}) copy-start(f32[384]{0:T(512)} %refs_0_.1) | copy-start | bytes 4612
  13.5 5.0 %copy-start.7 = (f32[384]{0:T(512)S(1)}, f32[384]{0:T(512)}, u32[]{:S(2)}) copy-start(f32[384]{0:T(512)} %refs_1_.1) | copy-start | bytes 4612
  13.5 5.0 %copy-start.8 = (f32[384]{0:T(512)S(1)}, f32[384]{0:T(512)}, u32[]{:S(2)}) copy-start(f32[384]{0:T(512)} %refs_2_.1) | copy-start | bytes 4612
  13.5 5.0 %copy-start.9 = (f32[384]{0:T(512)S(1)}, f32[384]{0:T(512)}, u32[]{:S(2)}) copy-start(f32[384]{0:T(512)} %refs_3_.1) | copy-start | bytes 4612
  13.6 10.0 %collective-permute-start.4 = (bf16[2,32,384]{2,1,0:T(8,128)(2,1)S(1)}, bf16[2,32,384]{2,1,0:T(8,128)(2,1)S(1)}, u32[]{:S(2)}, u32[]{:S(2)}) collective-permute-start(bf16[2,32,384]{2,1,0:T(8,128)(2,1)S(1)} %get-tuple-element.31), channel_id=1, source_target_pairs={{0,1},{1,0},{2,3},{3,2},{4,5},{5,4},{6,7},{7,6},{8,9},{9,8},{10,11... | collective-permute-start | bytes 147464 | tf_op jit(solution)/shard_map/ppermute | solution.py:548
  19.6 10.8 %all-to-all-start = ((f32[16,8,384]{2,1,0:T(8,128)}), f32[16,8,384]{2,1,0:T(8,128)S(1)}, u32[]{:S(2)}, u32[]{:S(2)}) async-start(f32[16,8,384]{2,1,0:T(8,128)} %get-tuple-element.34), calls=%async_computation | async-start | bytes 393216 | tf_op jit(solution)/shard_map/all_to_all | solution.py:510
  23.7 3.3 %copy-start = (bf16[27,384,384]{2,1,0:T(8,128)(2,1)S(1)}, bf16[27,384,384]{2,1,0:T(8,128)(2,1)}, u32[]{:S(2)}) copy-start(bf16[27,384,384]{2,1,0:T(8,128)(2,1)} %w_ref.2) | copy-start | bytes 23887876
  30.3 22.3 %slice-start = ((s8[7962624]{0:T(1024)(128)(4,1)}), s8[4194304]{0:T(1024)(128)(4,1)S(1)}, s32[]{:S(2)}) async-start(s8[7962624]{0:T(1024)(128)(4,1)} %bitcast.16), calls=%async_computation.4 | async-start | bytes 8388608
  41.7 10.9 %slice-start.1 = ((s8[7962624]{0:T(1024)(128)(4,1)}), s8[3768320]{0:T(1024)(128)(4,1)S(1)}, s32[]{:S(2)}) async-start(s8[7962624]{0:T(1024)(128)(4,1)} %bitcast.16), calls=%async_computation.5 | async-start | bytes 7536640
  42.1 23.5 %copy-start.3 = (bf16[27,16,384]{2,1,0:T(8,128)(2,1)S(1)}, bf16[27,16,384]{2,1,0:T(8,128)(2,1)}, u32[]{:S(2)}) copy-start(bf16[27,16,384]{2,1,0:T(8,128)(2,1)} %k_ref.1) | copy-start | bytes 995332
  42.1 39.4 %copy-start.4 = (bf16[96,768]{1,0:T(8,128)(2,1)S(1)}, bf16[96,768]{1,0:T(8,128)(2,1)}, u32[]{:S(2)}) copy-start(bf16[96,768]{1,0:T(8,128)(2,1)} %constant.33.clone.e_ref) | copy-start | bytes 442372
  42.1 39.4 %copy-start.5 = (bf16[64,192]{1,0:T(8,128)(2,1)S(1)}, bf16[64,192]{1,0:T(8,128)(2,1)}, u32[]{:S(2)}) copy-start(bf16[64,192]{1,0:T(8,128)(2,1)} %constant.34.clone.perm_ref) | copy-start | bytes 73732
  42.1 7.5 %collective-permute-start.5 = (bf16[2,4,32,384]{3,2,1,0:T(8,128)(2,1)S(1)}, bf16[2,4,32,384]{3,2,1,0:T(8,128)(2,1)S(1)}, u32[]{:S(2)}, u32[]{:S(2)}) collective-permute-start(bf16[2,4,32,384]{3,2,1,0:T(8,128)(2,1)S(1)} %get-tuple-element.39.own_ref.grad_ref), channel_id=1, source_target_pairs={{0,112},{16,0},{32,16},{48,32},{64,48},{80,64},{96,80},{112,96},{1... | collective-permute-start | bytes 589832 | tf_op jit(solution)/shard_map/ppermute | solution.py:494
  45.6 6.1 %collective-permute-start.7 = (bf16[2,32,384]{2,1,0:T(8,128)(2,1)S(1)}, bf16[2,32,384]{2,1,0:T(8,128)(2,1)S(1)}, u32[]{:S(2)}, u32[]{:S(2)}) collective-permute-start(bf16[2,32,384]{2,1,0:T(8,128)(2,1)S(1)} %get-tuple-element.41), channel_id=1, source_target_pairs={{1,2},{2,1},{3,4},{4,3},{5,6},{6,5},{7,8},{8,7},{9,10},{10,9},{11,... | collective-permute-start | bytes 147464 | tf_op jit(solution)/shard_map/ppermute | solution.py:499
  46.1 6.1 %collective-permute-start.9 = (bf16[2,32,384]{2,1,0:T(8,128)(2,1)S(1)}, bf16[2,32,384]{2,1,0:T(8,128)(2,1)S(1)}, u32[]{:S(2)}, u32[]{:S(2)}) collective-permute-start(bf16[2,32,384]{2,1,0:T(8,128)(2,1)S(1)} %get-tuple-element.41), channel_id=1, source_target_pairs={{1,114},{2,113},{3,116},{4,115},{5,118},{6,117},{7,120},{8,119},{9... | collective-permute-start | bytes 147464 | tf_op jit(solution)/shard_map/ppermute | solution.py:500
  46.3 5.5 %collective-permute-start.6 = (bf16[2,32,384]{2,1,0:T(8,128)(2,1)S(1)}, bf16[2,32,384]{2,1,0:T(8,128)(2,1)S(1)}, u32[]{:S(2)}, u32[]{:S(2)}) collective-permute-start(bf16[2,32,384]{2,1,0:T(8,128)(2,1)S(1)} %get-tuple-element.40), channel_id=1, source_target_pairs={{0,1},{1,0},{2,3},{3,2},{4,5},{5,4},{6,7},{7,6},{8,9},{9,8},{10,11... | collective-permute-start | bytes 147464 | tf_op jit(solution)/shard_map/ppermute | solution.py:501
  49.6 3.0 %collective-permute-start.8 = (bf16[2,32,384]{2,1,0:T(8,128)(2,1)S(1)}, bf16[2,32,384]{2,1,0:T(8,128)(2,1)S(1)}, u32[]{:S(2)}, u32[]{:S(2)}) collective-permute-start(bf16[2,32,384]{2,1,0:T(8,128)(2,1)S(1)} %edge.3), channel_id=1, source_target_pairs={{0,1},{1,0},{2,3},{3,2},{4,5},{5,4},{6,7},{7,6},{8,9},{9,8},{10,11... | collective-permute-start | bytes 147464 | tf_op jit(solution)/shard_map/ppermute | solution.py:556
  66.3 5.5 %collective-permute-start.10 = (f32[2,32,128]{2,1,0:T(8,128)S(1)}, f32[2,32,128]{2,1,0:T(8,128)S(1)}, u32[]{:S(2)}, u32[]{:S(2)}) collective-permute-start(f32[2,32,128]{2,1,0:T(8,128)S(1)} %get-tuple-element.46), channel_id=1, source_target_pairs={{0,112},{16,0},{32,16},{48,32},{64,48},{80,64},{96,80},{112,96},{1... | collective-permute-start | bytes 98312 | tf_op jit(solution)/shard_map/ppermute | solution.py:562
